TPU v7x, 32 devices: a whole 2x2x4 slice. The times are simulated.
32 devices in a mesh: pair: 2 (over x), tp: 4 (over z), side: 4 (over y, core).
Axes of the slice: x: 2, y: 2, z: 4, core: 2. Of those that a mesh axis runs over, the one named last changes fastest.
Arguments:
- x_prompt: bfloat16 [8, 2048, 3584], P(('pair', 'side')), parts along dimension 0
- s_len: int32 [8], P(('pair', 'side')), parts along dimension 0
- y_tok: bfloat16 [256, 3584], P(('pair', 'side')), parts along dimension 0
- c_len: int32 [256], P(('pair', 'side')), parts along dimension 0
- k_cache: bfloat16 [1, 256, 256, 4, 128], P(None, ('pair', 'side'), 'tp'), parts along dimension 1
- v_cache: bfloat16 [1, 256, 256, 4, 128], P(None, ('pair', 'side'), 'tp'), parts along dimension 1
- attn_gain: bfloat16 [1, 3584], replicated
- w_qkv: bfloat16 [1, 3584, 4, 9, 128], P(None, None, 'tp')
- w_out: bfloat16 [1, 4, 7, 128, 3584], P(None, 'tp')
- mlp_gain: bfloat16 [1, 3584], replicated
- w_gate_up: bfloat16 [1, 3584, 2, 18944], P(None, None, None, 'tp')
- w_down: bfloat16 [1, 18944, 3584], P(None, 'tp')
Outputs:
- output 1: bfloat16 [8, 2048, 3584], P(('pair', 'side')), parts along dimension 0
- output 2: bfloat16 [256, 3584], P(('pair', 'side')), parts along dimension 0
- output 3: bfloat16 [1, 8, 2048, 4, 128], P(None, ('pair', 'side'), 'tp'), parts along dimension 1
- output 4: bfloat16 [1, 8, 2048, 4, 128], P(None, ('pair', 'side'), 'tp'), parts along dimension 1
- output 5: bfloat16 [1, 256, 256, 4, 128], P(None, ('pair', 'side'), 'tp'), parts along dimension 1
- output 6: bfloat16 [1, 256, 256, 4, 128], P(None, ('pair', 'side'), 'tp'), parts along dimension 1
There are 2 independent parts. A program takes and returns all parts, laid end to end along the dimension named above; an argument that names none is the same for every part.
All inputs are finite; a program needn't handle non-finite values.
Results may differ from a plain program's by a relative error of at most 0.0063243.
Values are sent between devices in bfloat16 or wider.
A program may use at most 1 GiB of HBM per device.

v0:
```python
import jax
import jax.numpy as jnp
from jax import lax
from jax.sharding import PartitionSpec as P

ROPE_BASE = 10000.0
NORM_EPS = 1e-5
Q_BLOCK = 128


def rms_norm(hidden, norm_gain):
    hidden_f32 = hidden.astype(jnp.float32)
    inv_rms = lax.rsqrt(jnp.mean(hidden_f32 * hidden_f32, axis=-1, keepdims=True) + NORM_EPS)
    return (hidden_f32 * inv_rms * norm_gain.astype(jnp.float32)).astype(jnp.bfloat16)


def rope_rotate(vals_f32, positions):
    head_dim = vals_f32.shape[-1]
    half_dim = head_dim // 2
    inv_freq = ROPE_BASE ** (-2.0 * jnp.arange(half_dim, dtype=jnp.float32) / head_dim)
    angles = positions.astype(jnp.float32)[:, None] * inv_freq[None, :]
    cos_table = jnp.cos(angles)[:, None, None, :]
    sin_table = jnp.sin(angles)[:, None, None, :]
    first_half = vals_f32[..., :half_dim]
    second_half = vals_f32[..., half_dim:]
    return jnp.concatenate([first_half * cos_table - second_half * sin_table, second_half * cos_table + first_half * sin_table], axis=-1)


def mlp_partial(hidden, norm_gain, w_gate_up, w_down):
    normed = rms_norm(hidden, norm_gain)
    gate_up = jnp.einsum('...d,dcf->...cf', normed, w_gate_up, preferred_element_type=jnp.float32)
    activated = (jax.nn.silu(gate_up[..., 0, :]) * gate_up[..., 1, :]).astype(jnp.bfloat16)
    return jnp.einsum('...f,fd->...d', activated, w_down, preferred_element_type=jnp.float32)


def prefill_attention(queries, key_rows, value_rows, key_valid):
    seq_len = queries.shape[0]
    head_dim = queries.shape[-1]
    block_count = seq_len // Q_BLOCK
    positions = jnp.arange(seq_len)
    query_blocks = queries.reshape((block_count, Q_BLOCK) + queries.shape[1:])
    block_starts = jnp.arange(block_count) * Q_BLOCK

    def attend_block(block_args):
        query_block, block_start = block_args
        scores = jnp.einsum('qkgh,tkh->kgqt', query_block, key_rows, preferred_element_type=jnp.float32) * head_dim ** -0.5
        query_pos = block_start + jnp.arange(Q_BLOCK)
        allowed = (positions[None, :] <= query_pos[:, None]) & key_valid[None, :]
        scores = jnp.where(allowed, scores, -1e30)
        weights = jnp.exp(scores - jnp.max(scores, axis=-1, keepdims=True))
        weight_sum = jnp.transpose(jnp.sum(weights, axis=-1), (2, 0, 1))
        mixed_sum = jnp.einsum('kgqt,tkh->qkgh', weights.astype(jnp.bfloat16), value_rows, preferred_element_type=jnp.float32)
        return (mixed_sum / weight_sum[..., None]).astype(jnp.bfloat16)

    context = lax.map(attend_block, (query_blocks, block_starts))
    return context.reshape((seq_len,) + context.shape[2:])


def decode_local(tokens, cache_lens, k_cache, v_cache, attn_gain, w_qkv, w_out, mlp_gain, w_gate_up, w_down):
    layers = w_qkv.shape[0]
    group_q = w_qkv.shape[3] - 2
    head_dim = w_qkv.shape[4]
    cache_local = k_cache.shape[2]
    cache_pos = lax.axis_index('tp') * cache_local + jnp.arange(cache_local)
    write_mask = (cache_pos[None, :] == cache_lens[:, None])[:, :, None, None]
    allowed = (cache_pos[None, :] <= cache_lens[:, None])[:, None, None, :]
    key_outs = []
    value_outs = []
    for layer_idx in range(layers):
        normed = rms_norm(tokens, attn_gain[layer_idx])
        projected = jnp.einsum('bd,dkjh->bkjh', normed, w_qkv[layer_idx], preferred_element_type=jnp.float32)
        rotated = rope_rotate(projected[:, :, :group_q + 1], cache_lens)
        local_qkv = jnp.concatenate([rotated, projected[:, :, group_q + 1:]], axis=2).astype(jnp.bfloat16)
        full_qkv = lax.all_gather(local_qkv, 'tp', axis=1, tiled=True)
        key_now = jnp.where(write_mask, full_qkv[:, None, :, group_q], k_cache[layer_idx])
        value_now = jnp.where(write_mask, full_qkv[:, None, :, group_q + 1], v_cache[layer_idx])
        scores = jnp.einsum('bkgh,btkh->bkgt', full_qkv[:, :, :group_q], key_now, preferred_element_type=jnp.float32) * head_dim ** -0.5
        scores = jnp.where(allowed, scores, -1e30)
        score_max = lax.pmax(jnp.max(scores, axis=-1, keepdims=True), 'tp')
        weights = jnp.exp(scores - score_max)
        sum_own = lax.psum_scatter(jnp.sum(weights, axis=-1), 'tp', scatter_dimension=1, tiled=True)
        mixed_sum = jnp.einsum('bkgt,btkh->bkgh', weights.astype(jnp.bfloat16), value_now, preferred_element_type=jnp.float32)
        mixed_own = lax.psum_scatter(mixed_sum, 'tp', scatter_dimension=1, tiled=True)
        context = (mixed_own / sum_own[..., None]).astype(jnp.bfloat16)
        attn_part = jnp.einsum('bkgh,kghd->bd', context, w_out[layer_idx], preferred_element_type=jnp.float32)
        tokens = (tokens.astype(jnp.float32) + lax.psum(attn_part, 'tp')).astype(jnp.bfloat16)
        down_part = mlp_partial(tokens, mlp_gain[layer_idx], w_gate_up[layer_idx], w_down[layer_idx])
        tokens = (tokens.astype(jnp.float32) + lax.psum(down_part, 'tp')).astype(jnp.bfloat16)
        key_outs.append(key_now)
        value_outs.append(value_now)
    return tokens, jnp.stack(key_outs), jnp.stack(value_outs)


def solution(mesh):
    side_size = mesh.shape['side']
    send_pairs = [(source, (source + 1) % side_size) for source in range(side_size)]
    group_axes = ('pair', 'side')

    def device_fn(x_prompt, s_len, y_tok, c_len, k_cache, v_cache, attn_gain, w_qkv, w_out, mlp_gain, w_gate_up, w_down):
        layers = w_qkv.shape[0]
        group_q = w_qkv.shape[3] - 2
        seq_len = x_prompt.shape[1]
        positions = jnp.arange(seq_len)
        key_valid = positions < s_len[0]
        keep_mask = key_valid[:, None, None].astype(jnp.bfloat16)
        hidden = x_prompt[0]
        key_parts = []
        value_parts = []
        for layer_idx in range(layers):
            normed = rms_norm(hidden, attn_gain[layer_idx])
            projected = jnp.einsum('sd,dkjh->skjh', normed, w_qkv[layer_idx], preferred_element_type=jnp.float32)
            rotated = rope_rotate(projected[:, :, :group_q + 1], positions).astype(jnp.bfloat16)
            value_rows = projected[:, :, group_q + 1].astype(jnp.bfloat16)
            key_rows = rotated[:, :, group_q]
            context = prefill_attention(rotated[:, :, :group_q], key_rows, value_rows, key_valid)
            attn_part = jnp.einsum('skgh,kghd->sd', context, w_out[layer_idx], preferred_element_type=jnp.float32)
            hidden = (hidden.astype(jnp.float32) + lax.psum(attn_part, 'tp')).astype(jnp.bfloat16)
            down_part = mlp_partial(hidden, mlp_gain[layer_idx], w_gate_up[layer_idx], w_down[layer_idx])
            hidden = (hidden.astype(jnp.float32) + lax.psum(down_part, 'tp')).astype(jnp.bfloat16)
            kv_pair = jnp.stack([key_rows, value_rows]) * keep_mask
            kv_by_pos = lax.all_to_all(kv_pair, 'tp', 1, 2, tiled=True)
            kv_recv = lax.ppermute(kv_by_pos, 'side', send_pairs)
            key_parts.append(kv_recv[0])
            value_parts.append(kv_recv[1])
        tokens, key_cache, value_cache = decode_local(y_tok, c_len, k_cache, v_cache, attn_gain, w_qkv, w_out, mlp_gain, w_gate_up, w_down)
        return (hidden[None], tokens, jnp.stack(key_parts)[:, None], jnp.stack(value_parts)[:, None], key_cache, value_cache)

    cache_spec = P(None, group_axes, 'tp', None, None)
    in_specs = (P(group_axes, None, None), P(group_axes), P(group_axes, None), P(group_axes), cache_spec, cache_spec, P(), P(None, None, 'tp', None, None), P(None, 'tp', None, None, None), P(), P(None, None, None, 'tp'), P(None, 'tp', None))
    out_specs = (P(group_axes, None, None), P(group_axes, None), cache_spec, cache_spec, cache_spec, cache_spec)
    return jax.shard_map(device_fn, mesh=mesh, in_specs=in_specs, out_specs=out_specs, check_vma=False)
```

profile of v0, /device:TPU:0, one launch (start us, length us, event | category | flops | bytes accessed | tf_op | source)
XLA Modules:
  0.0 2647.0 jit_solution(8223525431960822853)
XLA Ops:
  9.9 5.0 convolution_bitcast_fusion.1
  15.3 15.7 all_gather.3
  31.3 6.9 bitcast_select_fusion.2
  39.5 20.4 pmax.7
  63.3 12.1 copy.87
  75.4 8.1 fusion.46
  85.4 23.6 fusion.60
  113.9 5.1 copy.110
  119.0 6.3 copy.88
  125.6 144.5 %while.11 = (s32[]{:T(128)}, bf16[16,128,1,7,128]{4,1,0,3,2:T(8,128)(2,1)}, s32[16]{0:T(128)S(1)}, bf16[16,128,1,7,128]{4,1,3,2,0:T(8,128)(2,1)}, bf16[2048,1,12...) while((s32[]{:T(128)}, ...), condition=%wide.region_4.5_spmd.clone, body=%wide.region_1.4_spmd.clone.sunk | while | flops 960463232 | bytes 24600168 | solution.py:55
  127.8 2.4 fusion.134
  132.2 2.7 fusion.136
  136.9 2.4 fusion.134
  141.2 2.7 fusion.136
  145.9 2.4 fusion.134
  150.2 2.7 fusion.136
  154.9 2.4 fusion.134
  159.2 2.7 fusion.136
  163.9 2.4 fusion.134
  168.2 2.7 fusion.136
  172.9 2.4 fusion.134
  177.3 2.7 fusion.136
  182.0 2.4 fusion.134
  186.3 2.7 fusion.136
  195.3 2.7 fusion.136
  204.3 2.7 fusion.136
  213.3 2.7 fusion.136
  222.3 2.7 fusion.136
  231.4 2.7 fusion.136
  240.4 2.7 fusion.136
  249.4 2.7 fusion.136
  258.4 2.7 fusion.136
  267.4 2.7 fusion.136
  270.1 22.9 convolution_bitcast_fusion
  294.2 15.5 all-reduce
  310.4 4.9 fusion.69
  316.1 978.2 %all-reduce.8.cloned.1.call-done = (f32[2048,3584]{1,0:T(8,128)}, f32[32,3584]{1,0:T(8,128)}) async-done(((f32[2048,3584]{1,0:T(8,128)}, f32[32,3584]{1,0:T(8,128)}), (f32[2048,3584]{1,0:T(8,128)}, f32[32,3584]{1,0:T(8,128)})) %all-reduce.8.cloned.1.call-update) | async-done | bytes 29818896 | tf_op jit(solution)/shard_map/psum | solution.py:117
  1294.3 20.8 fusion.50
  1316.5 157.5 %fusion.37 = f32[2048,2,4736]{2,0,1:T(8,128)} fusion(bf16[3584,2,4736]{2,1,0:T(2,128)(2,1)} %bitcast.14, bf16[2048,3584]{1,0:T(8,128)(2,1)} %get-tuple-element.135, f32[3584]{0:T(1024)S(1)} %convert_reduce_fusion, f32[2048]{0:T(1024)S(1)} %add_rsqrt_fusion), kind=kOutput, calls=%fused_computation.29 | convolution fusion | flops 139078926336 | bytes 160192512 | tf_op jit(solution)/shard_map/...d,dcf->...cf/dot_general | solution.py:31
  1474.0 93.1 %fusion.44 = f32[2048,3584]{1,0:T(8,128)} fusion(bf16[1,4736,3584]{2,1,0:T(8,128)(2,1)} %param.25, f32[2048,2,4736]{2,0,1:T(8,128)} %fusion.37), kind=kOutput, calls=%fused_computation.42 | convolution fusion | flops 69582979072 | bytes 140902400 | tf_op jit(solution)/shard_map/...f,fd->...d/dot_general | solution.py:33
  1567.2 33.8 %fusion.35 = f32[32,2,4736]{2,0,1:T(8,128)S(1)} fusion(bf16[3584,2,4736]{2,1,0:T(2,128)(2,1)} %bitcast.14, bf16[32,3584]{1,0:T(8,128)(2,1)S(1)} %copy-done.6, f32[3584]{0:T(1024)S(1)} %copy-done.15, f32[32]{0:T(128)S(1)} %copy-done.19), kind=kOutput, calls=%fused_computation.27 | convolution fusion | flops 2173108224 | bytes 69351552 | tf_op jit(solution)/shard_map/...d,dcf->...cf/dot_general | solution.py:31
  1601.0 14.8 fusion.42
  1618.1 2.4 copy.101
  1620.6 57.4 %all_to_all.18 = bf16[2,2048,1,128]{3,0,2,1:T(2,128)(2,1)S(1)} all-to-all(bf16[2,2048,1,128]{3,0,2,1:T(2,128)(2,1)S(1)} %copy.101), channel_id=1, replica_groups=mesh['pair'=2,'tp'=4,'side'=4] {'tp'}, dimensions={1} | all-to-all | bytes 2097152 | tf_op jit(solution)/shard_map/all_to_all | solution.py:121
  1678.3 7.3 broadcast_select_fusion
  1685.5 6.9 collective-permute-done
  1694.9 922.5 %all-reduce.6.cloned.1.call-done = (f32[2048,3584]{1,0:T(8,128)}, f32[32,3584]{1,0:T(8,128)}) async-done(((f32[2048,3584]{1,0:T(8,128)}, f32[32,3584]{1,0:T(8,128)}), (f32[2048,3584]{1,0:T(8,128)}, f32[32,3584]{1,0:T(8,128)})) %all-reduce.6.cloned.1.call-update) | async-done | bytes 29818896 | tf_op jit(solution)/shard_map/psum | solution.py:119
  2619.2 20.8 fusion.56
  (181 shorter events, 108.7 us)
Async XLA Ops:
  7.2 24.0 copy-start.17
  7.2 24.1 copy-start
  7.2 303.2 %reduce-scatter.2.cloned.1.call-start = ((), (), s32[]{:S(2)}) async-start(), calls=%async_computation.2 | async-start | bytes 573440 | tf_op jit(solution)/shard_map/reduce_scatter | solution.py:83
  31.1 31.1 %copy-start.8 = (bf16[32,4,128]{2,1,0:T(4,128)(2,1)}, bf16[32,4,128]{2,1,0:T(4,128)(2,1)S(1)}, u32[]{:S(2)}) copy-start(bf16[32,4,128]{2,1,0:T(4,128)(2,1)S(1)} %copy.94) | copy-start | bytes 98308
  31.1 31.1 %copy-start.10 = (bf16[32,4,128]{2,1,0:T(4,128)(2,1)}, bf16[32,4,128]{2,1,0:T(4,128)(2,1)S(1)}, u32[]{:S(2)}) copy-start(bf16[32,4,128]{2,1,0:T(4,128)(2,1)S(1)} %copy.96) | copy-start | bytes 98308
  31.2 7.0 copy-start.12
  63.3 1231.0 %all-reduce.8.cloned.1.call-start = ((), (), s32[]{:S(2)}) async-start(), calls=%async_computation.4 | async-start | bytes 59637760 | tf_op jit(solution)/shard_map/psum | solution.py:117
  110.6 8.4 copy-start.2
  270.1 23.5 copy-start.18
  315.4 0.7 copy-start.16
  315.4 2302.1 %all-reduce.6.cloned.1.call-start = ((), (), s32[]{:S(2)}) async-start(), calls=%async_computation.3 | async-start | bytes 59637760 | tf_op jit(solution)/shard_map/psum | solution.py:119
  316.1 1000.4 %copy-start.14 = (f32[3584]{0:T(1024)}, f32[3584]{0:T(1024)S(1)}, u32[]{:S(2)}) copy-start(f32[3584]{0:T(1024)S(1)} %convert_reduce_fusion) | copy-start | bytes 43012
  1294.3 20.8 copy-start.5
  1294.3 20.8 copy-start.7
  1474.0 93.2 %copy-start.6 = (bf16[32,3584]{1,0:T(8,128)(2,1)S(1)}, bf16[32,3584]{1,0:T(8,128)(2,1)}, u32[]{:S(2)}) copy-start(bf16[32,3584]{1,0:T(8,128)(2,1)} %get-tuple-element.133) | copy-start | bytes 688132
  1474.0 93.2 %copy-start.15 = (f32[3584]{0:T(1024)S(1)}, f32[3584]{0:T(1024)}, u32[]{:S(2)}) copy-start(f32[3584]{0:T(1024)} %copy-done.14) | copy-start | bytes 43012
  1474.0 93.2 %copy-start.19 = (f32[32]{0:T(128)S(1)}, f32[32]{0:T(128)}, u32[]{:S(2)}) copy-start(f32[32]{0:T(128)} %add_rsqrt_fusion.2) | copy-start | bytes 388
  1615.8 1.0 copy-start.3
  1615.8 1.2 copy-start.4
  1615.9 62.4 %copy-start.1 = (bf16[1,32,64,4,128]{4,3,2,1,0:T(4,128)(2,1)S(1)}, bf16[1,32,64,4,128]{4,3,2,1,0:T(4,128)(2,1)}, u32[]{:S(2)}) copy-start(bf16[1,32,64,4,128]{4,3,2,1,0:T(4,128)(2,1)} %param.18) | copy-start | bytes 6291460
  1615.9 62.3 %copy-start.9 = (bf16[32,4,128]{2,1,0:T(4,128)(2,1)S(1)}, bf16[32,4,128]{2,1,0:T(4,128)(2,1)}, u32[]{:S(2)}) copy-start(bf16[32,4,128]{2,1,0:T(4,128)(2,1)} %copy-done.8) | copy-start | bytes 98308
  1615.9 62.3 %copy-start.11 = (bf16[32,4,128]{2,1,0:T(4,128)(2,1)S(1)}, bf16[32,4,128]{2,1,0:T(4,128)(2,1)}, u32[]{:S(2)}) copy-start(bf16[32,4,128]{2,1,0:T(4,128)(2,1)} %copy-done.10) | copy-start | bytes 98308
  1615.9 62.3 %copy-start.13 = (pred[32,64]{1,0:T(8,128)(4,1)S(1)}, pred[32,64]{1,0:T(8,128)(4,1)}, u32[]{:S(2)}) copy-start(pred[32,64]{1,0:T(8,128)(4,1)} %copy-done.12) | copy-start | bytes 6148
  1678.1 14.3 collective-permute-start
Sparse Core Ops, SparseCore 0:
  63.4 19.6 reduce-scatter.1
  315.5 978.7 all-reduce.7
  1616.0 1001.4 all-reduce.5
where the time goes:
time: 2650 us
  waiting for transfers between devices  1910 us (72%)
  matrix products  441 us (17%)
  other arithmetic  130 us (5%)
  blocking collectives  109 us (4%)
  local copies, waits for them, and re-layouts  42.4 us (2%)
    psum x1, waiting for transfers between devices, device_fn(): lax.psum(attn_part, 'tp')  978 us
    psum x1, waiting for transfers between devices, device_fn(): lax.psum(down_part, 'tp')  923 us
    dot_general x2, matrix products, mlp_partial(): jnp.einsum('...d,dcf->...cf', normed, w_gate_up, preferred_element_type=j...  191 us
    dot_general x2, matrix products, mlp_partial(): jnp.einsum('...f,fd->...d', activated, w_down, preferred_element_type=jnp...  108 us
    all_to_all x1, blocking collectives, device_fn(): kv_by_pos = lax.all_to_all(kv_pair, 'tp', 1, 2, tiled=True)  57.4 us
  transfers between devices with their start and end apart: 4, of which 3 were waited for; matrix products, arithmetic and copies ran while one was open for 9% of the time, Pallas kernels for 0%

commit v1 on v0

v1 whole, which is shorter than its diff:
```python
import functools

import jax
import jax.numpy as jnp
from jax import lax
from jax.experimental import pallas as pl
from jax.experimental.pallas import tpu as pltpu
from jax.sharding import PartitionSpec as P

ROPE_BASE = 10000.0
NORM_EPS = 1e-5
LOG2E = 1.4426950408889634
BF = jnp.bfloat16
F32 = jnp.float32


def rms_norm(hidden, norm_gain):
    hidden_f32 = hidden.astype(F32)
    inv_rms = lax.rsqrt(jnp.mean(hidden_f32 * hidden_f32, axis=-1, keepdims=True) + NORM_EPS)
    return (hidden_f32 * inv_rms * norm_gain.astype(F32)).astype(BF)


def rope_tables(positions, head_dim):
    half_dim = head_dim // 2
    inv_freq = ROPE_BASE ** (-2.0 * jnp.arange(half_dim, dtype=F32) / head_dim)
    angles = positions.astype(F32)[:, None] * inv_freq[None, :]
    return jnp.cos(angles), jnp.sin(angles)


def rope_rotate(vals_f32, positions):
    half_dim = vals_f32.shape[-1] // 2
    cos_table, sin_table = rope_tables(positions, vals_f32.shape[-1])
    cos_table, sin_table = cos_table[:, None, None, :], sin_table[:, None, None, :]
    first_half = vals_f32[..., :half_dim]
    second_half = vals_f32[..., half_dim:]
    return jnp.concatenate([first_half * cos_table - second_half * sin_table, second_half * cos_table + first_half * sin_table], axis=-1)


def qkv_kernel(x_ref, gain_ref, cos_ref, sin_ref, w_ref, o_ref):
    slots = w_ref.shape[0]
    x = x_ref[...].astype(F32)
    inv = lax.rsqrt(jnp.mean(x * x, axis=-1, keepdims=True) + NORM_EPS)
    normed = (x * inv * gain_ref[...].astype(F32)).astype(BF)
    cos, sin = cos_ref[...], sin_ref[...]
    for first in range(0, slots, 2):
        group = range(first, min(first + 2, slots))
        w = jnp.concatenate([w_ref[s] for s in group], axis=-1)
        y = jnp.dot(normed, w, preferred_element_type=F32)
        for n, s in enumerate(group):
            part = y[:, n * 128:(n + 1) * 128]
            if s < slots - 1:
                part = part * cos + pltpu.roll(part, 64, 1) * sin
            o_ref[s] = part.astype(BF)


def project_qkv(x, gain, cos, sin, w, rows_block=256):
    rows, width = x.shape
    slots, _, head = w.shape
    return pl.pallas_call(
        qkv_kernel,
        grid=(rows // rows_block,),
        in_specs=[
            pl.BlockSpec((rows_block, width), lambda i: (i, 0)),
            pl.BlockSpec((1, width), lambda i: (0, 0)),
            pl.BlockSpec((rows_block, head), lambda i: (i, 0)),
            pl.BlockSpec((rows_block, head), lambda i: (i, 0)),
            pl.BlockSpec((slots, width, head), lambda i: (0, 0, 0), pipeline_mode=pl.Buffered(1)),
        ],
        out_specs=pl.BlockSpec((slots, rows_block, head), lambda i: (0, i, 0)),
        out_shape=jax.ShapeDtypeStruct((slots, rows, head), BF),
        cost_estimate=pl.CostEstimate(flops=2 * rows * width * slots * head, bytes_accessed=2 * (rows * width + slots * head * (width + rows)), transcendentals=0),
        name="project_qkv",
    )(x, gain, cos, sin, w)


def flash_kernel(block_q, block_k, slen_ref, q_ref, k_ref, v_ref, o_ref, m_ref, l_ref, acc_ref):
    i = pl.program_id(0)
    heads, _, head = q_ref.shape
    rows = heads * block_q
    slen = slen_ref[0]
    scale = head ** -0.5 * LOG2E
    q = q_ref[...].reshape(rows, head)
    m_ref[...] = jnp.full_like(m_ref, -jnp.inf)
    l_ref[...] = jnp.zeros_like(l_ref)
    acc_ref[...] = jnp.zeros_like(acc_ref)

    def step(j, masked):
        start = pl.multiple_of(j * block_k, block_k)
        k = k_ref[0, pl.ds(start, block_k), :]
        v = v_ref[0, pl.ds(start, block_k), :]
        s = lax.dot_general(q, k, (((1,), (1,)), ((), ())), preferred_element_type=F32)
        if masked:
            q_pos = i * block_q + lax.broadcasted_iota(jnp.int32, (block_q, block_k), 0)
            k_pos = start + lax.broadcasted_iota(jnp.int32, (block_q, block_k), 1)
            allowed = (k_pos <= q_pos) & (k_pos < slen)
            s = jnp.where(allowed[None], s.reshape(heads, block_q, block_k), -1e30).reshape(rows, block_k)
        m_old = m_ref[...]
        m_new = jnp.maximum(m_old, jnp.max(s, axis=-1, keepdims=True))
        alpha = jnp.exp2((m_old - m_new) * scale)
        p = jnp.exp2((s - m_new) * scale)
        l_ref[...] = l_ref[...] * alpha + jnp.sum(p, axis=-1, keepdims=True)
        acc_ref[...] = acc_ref[...] * alpha + jnp.dot(p.astype(BF), v, preferred_element_type=F32)
        m_ref[...] = m_new

    count = (i * block_q + block_q - 1) // block_k + 1

    @pl.loop(0, count)
    def _(j):
        edge = ((j + 1) * block_k > i * block_q) | ((j + 1) * block_k > slen)

        @pl.when(edge)
        def _():
            step(j, True)

        @pl.when(jnp.logical_not(edge))
        def _():
            step(j, False)

    out = (acc_ref[...] / l_ref[...]).astype(BF)
    for h in range(heads):
        o_ref[:, h * head:(h + 1) * head] = out[h * block_q:(h + 1) * block_q]


def attend(slen, qkv, block_q=256, block_k=512):
    slots, rows, head = qkv.shape
    heads = slots - 2
    return pl.pallas_call(
        functools.partial(flash_kernel, block_q, block_k),
        grid_spec=pltpu.PrefetchScalarGridSpec(
            num_scalar_prefetch=1,
            grid=(rows // block_q,),
            in_specs=[
                pl.BlockSpec((heads, block_q, head), lambda i, _: (0, i, 0)),
                pl.BlockSpec((1, rows, head), lambda i, _: (heads, 0, 0)),
                pl.BlockSpec((1, rows, head), lambda i, _: (heads + 1, 0, 0)),
            ],
            out_specs=pl.BlockSpec((block_q, heads * head), lambda i, _: (i, 0)),
            scratch_shapes=[
                pltpu.VMEM((heads * block_q, 1), F32),
                pltpu.VMEM((heads * block_q, 1), F32),
                pltpu.VMEM((heads * block_q, head), F32),
            ],
        ),
        out_shape=jax.ShapeDtypeStruct((rows, heads * head), BF),
        cost_estimate=pl.CostEstimate(flops=3 * heads * rows * rows * head, bytes_accessed=2 * (2 * heads + 2) * rows * head, transcendentals=heads * rows * rows // 2),
        name="attend",
    )(slen, qkv, qkv, qkv)


def decode_context(tokens, cache_lens, k_cache, v_cache, gain, w_qkv):
    group_q = w_qkv.shape[2] - 2
    head_dim = w_qkv.shape[3]
    cache_local = k_cache.shape[1]
    cache_pos = lax.axis_index('tp') * cache_local + jnp.arange(cache_local)
    write_mask = (cache_pos[None, :] == cache_lens[:, None])[:, :, None, None]
    allowed = (cache_pos[None, :] <= cache_lens[:, None])[:, None, None, :]
    normed = rms_norm(tokens, gain)
    projected = jnp.einsum('bd,dkjh->bkjh', normed, w_qkv, preferred_element_type=F32)
    rotated = rope_rotate(projected[:, :, :group_q + 1], cache_lens)
    local_qkv = jnp.concatenate([rotated, projected[:, :, group_q + 1:]], axis=2).astype(BF)
    full_qkv = lax.all_gather(local_qkv, 'tp', axis=1, tiled=True)
    key_now = jnp.where(write_mask, full_qkv[:, None, :, group_q], k_cache)
    value_now = jnp.where(write_mask, full_qkv[:, None, :, group_q + 1], v_cache)
    scores = jnp.einsum('bkgh,btkh->bkgt', full_qkv[:, :, :group_q], key_now, preferred_element_type=F32) * head_dim ** -0.5
    scores = jnp.where(allowed, scores, -1e30)
    score_max = lax.pmax(jnp.max(scores, axis=-1, keepdims=True), 'tp')
    weights = jnp.exp(scores - score_max)
    sum_own = lax.psum_scatter(jnp.sum(weights, axis=-1), 'tp', scatter_dimension=1, tiled=True)
    mixed_sum = jnp.einsum('bkgt,btkh->bkgh', weights.astype(BF), value_now, preferred_element_type=F32)
    mixed_own = lax.psum_scatter(mixed_sum, 'tp', scatter_dimension=1, tiled=True)
    context = (mixed_own / sum_own[..., None]).astype(BF)
    return context, key_now, value_now


def gather_w_out(w_out, mesh):
    plane = mesh.shape['pair'] * mesh.shape['side']
    rows = w_out.shape[0] // plane
    index = lax.axis_index('pair') * mesh.shape['side'] + lax.axis_index('side')
    own = lax.dynamic_slice_in_dim(w_out, index * rows, rows, 0)
    column = lax.all_gather(own, 'tp')
    return lax.all_gather(column, ('pair', 'side'))


def solution(mesh):
    side_size = mesh.shape['side']
    tp = mesh.shape['tp']
    send_pairs = [(source, (source + 1) % side_size) for source in range(side_size)]
    group_axes = ('pair', 'side')

    def device_fn(x_prompt, s_len, y_tok, c_len, k_cache, v_cache, attn_gain, w_qkv, w_out, mlp_gain, w_gate_up, w_down):
        x = x_prompt[0]
        seq_len, width = x.shape
        group_q, head = w_qkv.shape[3] - 2, w_qkv.shape[4]
        positions = jnp.arange(seq_len)
        keep_mask = (positions < s_len[0])[:, None].astype(BF)
        cos, sin = rope_tables(positions, head)
        cos, sin = jnp.concatenate([cos, cos], -1), jnp.concatenate([-sin, sin], -1)

        w_full = gather_w_out(w_out[0, 0].reshape(group_q * head, width), mesh)
        w_full = jnp.moveaxis(w_full, 1, 0).reshape(tp, group_q * head, width)

        dctx, key_now, value_now = decode_context(y_tok, c_len, k_cache[0], v_cache[0], attn_gain[0], w_qkv[0])
        dctx = dctx.reshape(dctx.shape[0], group_q * head)

        w_slots = jnp.transpose(w_qkv[0, :, 0], (1, 0, 2))
        qkv = project_qkv(x, attn_gain, cos, sin, w_slots)
        ctx = attend(s_len, qkv)

        chunks = 4
        step = seq_len // chunks
        hid = []
        outs = []
        for c in range(chunks):
            ctx_c, x_c = ctx[c * step:(c + 1) * step], x[c * step:(c + 1) * step]
            if c == 0:
                ctx_c, x_c = jnp.concatenate([ctx_c, dctx]), jnp.concatenate([x_c, y_tok])
            full = lax.all_gather(ctx_c, 'tp')
            mixed = jnp.einsum('trf,tfd->rd', full, w_full, preferred_element_type=F32)
            hid.append((x_c.astype(F32) + mixed).astype(BF))
        for c in range(chunks):
            normed = rms_norm(hid[c], mlp_gain[0])
            gate_up = jnp.einsum('rd,dcf->rcf', normed, w_gate_up[0], preferred_element_type=F32)
            activated = (jax.nn.silu(gate_up[:, 0]) * gate_up[:, 1]).astype(BF)
            part = jnp.dot(activated, w_down[0], preferred_element_type=F32)
            own = lax.psum_scatter(part, 'tp', scatter_dimension=0, tiled=True)
            rows = own.shape[0]
            own_hid = lax.dynamic_slice_in_dim(hid[c], lax.axis_index('tp') * rows, rows, 0)
            own = (own_hid.astype(F32) + own).astype(BF)
            outs.append(lax.all_gather(own, 'tp', axis=0, tiled=True))
        tokens = outs[0][step:]
        hidden = jnp.concatenate([outs[0][:step]] + outs[1:])

        kv_pair = (qkv[group_q:] * keep_mask)[:, :, None]
        kv_by_pos = lax.all_to_all(kv_pair, 'tp', 1, 2, tiled=True)
        kv_recv = lax.ppermute(kv_by_pos, 'side', send_pairs)
        return (hidden[None], tokens, kv_recv[0][None, None], kv_recv[1][None, None], key_now[None], value_now[None])

    cache_spec = P(None, group_axes, 'tp', None, None)
    in_specs = (P(group_axes, None, None), P(group_axes), P(group_axes, None), P(group_axes), cache_spec, cache_spec, P(), P(None, None, 'tp', None, None), P(None, 'tp', None, None, None), P(), P(None, None, None, 'tp'), P(None, 'tp', None))
    out_specs = (P(group_axes, None, None), P(group_axes, None), cache_spec, cache_spec, cache_spec, cache_spec)
    return jax.shard_map(device_fn, mesh=mesh, in_specs=in_specs, out_specs=out_specs, check_vma=False)
```

time: 2650 us -> 1520 us (0.57)
  waiting for transfers between devices: 1910 us -> 653 us
  Pallas kernels: 0 us -> 120 us
  other arithmetic: 130 us -> 50.1 us
  matrix products: 441 us -> 512 us
    psum x2 -> x0, waiting for transfers between devices: 1900 us -> none  [the longest x1 978 us: device_fn(): lax.psum(attn_part, 'tp')]
    all_gather x0 -> x10, waiting for transfers between devices: none -> 439 us  [the longest x4 221 us: device_fn(): outs.append(lax.all_gather(own, 'tp', axis=0, tiled=True))]
    reduce_scatter x1 -> x5, waiting for transfers between devices: 0.02 us -> 204 us  [the longest x4 204 us: device_fn(): own = lax.psum_scatter(part, 'tp', scatter_dimension=0, tiled=True)]
    pallas_call x0 -> x2, Pallas kernels: none -> 120 us  [the longest x1 91.1 us: attend(): pl.pallas_call(functools.partial(flash_kernel, block_q, block_k), grid_sp...]
    dot_general x41 -> x15, matrix products: 418 us -> 512 us  [the longest x4 274 us: device_fn(): jnp.einsum('rd,dcf->rcf', normed, w_gate_up[0], preferred_element_type=F32)]
    reduce_sum x17 -> x1, other arithmetic: 30.7 us -> 0.44 us  [decode_context(): jnp.sum(weights, axis=-1)]
    reduce_sum x4 -> x1, other arithmetic: 30.8 us -> 1.09 us  [rms_norm(): jnp.mean(hidden_f32 * hidden_f32, axis=-1, keepdims=True) + NORM_EPS]
  transfers between devices with their start and end apart: 4 -> 16, of which waited for: 3 -> 12; matrix products, arithmetic and copies ran while one was open for 9% -> 31% of each run, Pallas kernels for 0% -> 8%
where the time goes in v1:
time: 1520 us
  waiting for transfers between devices  653 us (43%)
  matrix products  512 us (34%)
  Pallas kernels  120 us (8%)
  blocking collectives  116 us (8%)
  other arithmetic  50.1 us (3%)
  local copies, waits for them, and re-layouts  48.8 us (3%)
  between operations  15.4 us (1%)
    dot_general x4, matrix products, device_fn(): jnp.einsum('rd,dcf->rcf', normed, w_gate_up[0], preferred_element_type=F32)  274 us
    all_gather x4, waiting for transfers between devices, device_fn(): outs.append(lax.all_gather(own, 'tp', axis=0, tiled=True))  221 us
    all_gather x4, waiting for transfers between devices, device_fn(): full = lax.all_gather(ctx_c, 'tp')  204 us
    reduce_scatter x4, waiting for transfers between devices, device_fn(): own = lax.psum_scatter(part, 'tp', scatter_dimension=0, tiled=True)  204 us
    dot_general x4, matrix products, device_fn(): part = jnp.dot(activated, w_down[0], preferred_element_type=F32)  143 us
    pallas_call x1, Pallas kernels, attend(): pl.pallas_call(functools.partial(flash_kernel, block_q, block_k), grid_sp...  91.1 us
    dot_general x4, matrix products, device_fn(): mixed = jnp.einsum('trf,tfd->rd', full, w_full, preferred_element_type=F32)  86.4 us
    all_to_all x1, blocking collectives, device_fn(): kv_by_pos = lax.all_to_all(kv_pair, 'tp', 1, 2, tiled=True)  58.9 us
  transfers between devices with their start and end apart: 16, of which 12 were waited for; matrix products, arithmetic and copies ran while one was open for 31% of the time, Pallas kernels for 8%

profile of v1, /device:TPU:0, one launch (start us, length us, event | category | flops | bytes accessed | tf_op | source)
XLA Modules:
  0.0 1516.4 jit_solution(14844994493608619559)
XLA Ops:
  7.2 2.2 constant_dynamic-slice_fusion
  12.1 5.0 fusion.72
  17.5 19.2 %all_gather.51 = bf16[32,4,9,128]{3,0,2,1:T(8,128)(2,1)S(1)} all-gather(bf16[32,1,9,128]{3,0,2,1:T(8,128)(2,1)S(1)} %pad_maximum_fusion.3), channel_id=1, replica_groups=mesh['pair'=2,'tp'=4,'side'=4] {'tp'}, dimensions={1}, use_global_device_ids=true | all-gather | bytes 368640 | tf_op jit(solution)/shard_map/all_gather | solution.py:161
  36.9 6.9 bitcast_select_fusion.1
  45.2 21.2 %pmax.7 = f32[32,4,7]{2,1,0:T(4,128)S(1)} all-reduce(f32[32,4,7]{2,1,0:T(4,128)S(1)} %get-tuple-element.33), channel_id=1, replica_groups=mesh['pair'=2,'tp'=4,'side'=4] {'tp'}, use_global_device_ids=true, to_apply=%region_2.3 | all-reduce | flops 896 | bytes 7168 | tf_op jit(solution)/shard_map/pmax | solution.py:166
  66.4 2.3 fusion.62
  69.8 13.6 all-gather.27.cloned.1.call-done
  84.2 3.7 fusion.81
  87.9 1.9 pad_maximum_fusion
  89.8 29.0 %project_qkv.1.q_ref.k_ref.v_ref = bf16[9,2048,128]{2,1,0:T(8,128)(2,1)} custom-call(bf16[2048,3584]{1,0:T(8,128)(2,1)} %bitcast.128, bf16[1,3584]{1,0:T(2,128)(2,1)} %gain_ref.1, f32[2048,128]{1,0:T(8,128)} %get-tuple-element.37.cos_ref, f32[2048,128]{1,0:T(8,128)} %get-tuple-element.38.sin_ref, bf16[9,3584,128]{2,1,0:T(8,128)(2,1)} %bitcast.124), custom_call_target="tpu_custom_call" | custom-call | flops 16911433728 | bytes 27656192 | tf_op jit(solution)/shard_map/project_qkv/pallas_call | solution.py:59
  118.8 91.1 %attend.1 = bf16[2048,896]{1,0:T(8,128)(2,1)} custom-call(s32[1]{0:T(128)} %copy.105.slen_ref, bf16[9,2048,128]{2,1,0:T(8,128)(2,1)} %project_qkv.1.q_ref.k_ref.v_ref, bf16[9,2048,128]{2,1,0:T(8,128)(2,1)} %project_qkv.1.q_ref.k_ref.v_ref, bf16[9,2048,128]{2,1,0:T(8,128)(2,1)} %project_qkv.1.q_ref.k_ref.v_ref), custom_call_target="tpu_custom_call" | custom-call | flops 11274289152 | bytes 8388608 | tf_op jit(solution)/shard_map/attend/pallas_call | solution.py:127
  209.9 3.7 fusion.94
  216.0 16.6 %all-reduce = f32[32,4,7]{0,2,1:T(8,128)S(1)} all-reduce(f32[32,4,7]{0,2,1:T(8,128)S(1)} %copy.66), channel_id=9, replica_groups=mesh['pair'=2,'tp'=4,'side'=4] {'tp'}, use_global_device_ids=true, to_apply=%region_5.6.clone | all-reduce | flops 896 | bytes 7168
  233.3 4.1 slice_bitcast_fusion
  239.6 18.2 %copy.68 = bf16[4,8,112,3584]{3,2,1,0:T(8,128)(2,1)} copy(bf16[4,8,112,3584]{3,2,0,1:T(8,128)(2,1)} %bitcast.119) | data formatting | bytes 51380224 | tf_op jit(solution)/shard_map/transpose | solution.py:200
  257.8 49.4 %all-gather.31.cloned.1.call-done = bf16[2048,896]{1,0:T(8,128)(2,1)} async-done(((bf16[512,896]{1,0:T(8,128)(2,1)}), bf16[2048,896]{1,0:T(8,128)(2,1)}) %all-gather.31.cloned.1.call-update) | async-done | bytes 3670032 | tf_op jit(solution)/shard_map/all_gather | solution.py:217
  307.2 21.4 %fusion.26 = (f32[512]{0:T(512)S(1)}, bf16[512,3584]{1,0:T(8,128)(2,1)}) fusion(bf16[4,512,896]{2,1,0:T(8,128)(2,1)} %bitcast.133, bf16[4,896,3584]{2,1,0:T(8,128)(2,1)} %bitcast.120, bf16[1,2048,3584]{2,1,0:T(8,128)(2,1)} %param.12), kind=kOutput, calls=%fused_computation.40 | convolution fusion | flops 13164347392 | bytes 36702208 | tf_op jit(solution)/shard_map/trf,tfd->rd/dot_general | solution.py:218
  328.6 50.3 %all-gather.33.cloned.1.call-done = bf16[2048,896]{1,0:T(8,128)(2,1)} async-done(((bf16[512,896]{1,0:T(8,128)(2,1)}), bf16[2048,896]{1,0:T(8,128)(2,1)}) %all-gather.33.cloned.1.call-update) | async-done | bytes 3670032 | tf_op jit(solution)/shard_map/all_gather | solution.py:217
  378.9 21.3 %fusion.29 = (f32[512]{0:T(512)S(1)}, bf16[512,3584]{1,0:T(8,128)(2,1)}) fusion(bf16[4,512,896]{2,1,0:T(8,128)(2,1)} %bitcast.135, bf16[4,896,3584]{2,1,0:T(8,128)(2,1)} %bitcast.121, bf16[1,2048,3584]{2,1,0:T(8,128)(2,1)} %param.12), kind=kOutput, calls=%fused_computation.43 | convolution fusion | flops 13164347392 | bytes 36702208 | tf_op jit(solution)/shard_map/trf,tfd->rd/dot_general | solution.py:218
  401.4 49.8 %all-gather.35.cloned.1.call-done = bf16[2048,896]{1,0:T(8,128)(2,1)} async-done(((bf16[512,896]{1,0:T(8,128)(2,1)}), bf16[2048,896]{1,0:T(8,128)(2,1)}) %all-gather.35.cloned.1.call-update) | async-done | bytes 3670032 | tf_op jit(solution)/shard_map/all_gather | solution.py:217
  451.2 21.4 %fusion.32 = (f32[512]{0:T(512)S(1)}, bf16[512,3584]{1,0:T(8,128)(2,1)}) fusion(bf16[4,512,896]{2,1,0:T(8,128)(2,1)} %bitcast.134, bf16[4,896,3584]{2,1,0:T(8,128)(2,1)} %bitcast.122, bf16[1,2048,3584]{2,1,0:T(8,128)(2,1)} %param.12), kind=kOutput, calls=%fused_computation.46 | convolution fusion | flops 13164347392 | bytes 36702208 | tf_op jit(solution)/shard_map/trf,tfd->rd/dot_general | solution.py:218
  472.6 54.8 %all-gather.25.cloned.1.call-done = bf16[2176,896]{1,0:T(8,128)(2,1)} async-done(((bf16[544,896]{1,0:T(8,128)(2,1)}), bf16[2176,896]{1,0:T(8,128)(2,1)}) %all-gather.25.cloned.1.call-update) | async-done | bytes 3899408 | tf_op jit(solution)/shard_map/all_gather | solution.py:217
  527.4 22.3 %fusion.22 = (f32[544]{0:T(1024)S(1)}, bf16[544,3584]{1,0:T(8,128)(2,1)}) fusion(bf16[4,544,896]{2,1,0:T(8,128)(2,1)} %bitcast.132, bf16[4,896,3584]{2,1,0:T(8,128)(2,1)} %bitcast.123, bf16[32,3584]{1,0:T(8,128)(2,1)S(1)} %copy-done.3, bf16[512,3584]{1,0:T(8,128)(2,1)} %slice_bitcast_fusion), kind=kOutput, calls=%fused_computation.35 | convolution fusion | flops 13992967168 | bytes 37390464 | tf_op jit(solution)/shard_map/trf,tfd->rd/dot_general | solution.py:218
  549.7 68.6 %fusion.6 = f32[544,2,4736]{2,0,1:T(8,128)} fusion(bf16[3584,2,4736]{2,1,0:T(2,128)(2,1)} %bitcast.19, bf16[544,3584]{1,0:T(8,128)(2,1)} %get-tuple-element.36, f32[3584]{0:T(1024)S(1)} %convert_reduce_fusion, f32[544]{0:T(1024)S(1)} %add_rsqrt_fusion), kind=kOutput, calls=%fused_computation.6 | convolution fusion | flops 36942839808 | bytes 92422272 | tf_op jit(solution)/shard_map/rd,dcf->rcf/dot_general | solution.py:222
  618.3 37.2 %fusion.14 = f32[544,3584]{1,0:T(8,128)} fusion(bf16[1,4736,3584]{2,1,0:T(8,128)(2,1)} %param.23, f32[544,2,4736]{2,0,1:T(8,128)} %fusion.6), kind=kOutput, calls=%fused_computation.14 | convolution fusion | flops 18482978816 | bytes 62357504 | tf_op jit(solution)/shard_map/dot_general | solution.py:224
  655.5 68.7 %fusion = f32[512,2,4736]{2,0,1:T(8,128)} fusion(bf16[3584,2,4736]{2,1,0:T(2,128)(2,1)} %bitcast.19, bf16[512,3584]{1,0:T(8,128)(2,1)} %get-tuple-element.28, f32[512]{0:T(512)S(1)} %add_rsqrt_fusion.1, f32[3584]{0:T(1024)S(1)} %convert_reduce_fusion), kind=kOutput, calls=%fused_computation | convolution fusion | flops 34769731584 | bytes 90980352 | tf_op jit(solution)/shard_map/rd,dcf->rcf/dot_general | solution.py:222
  724.2 35.4 %fusion.8 = f32[512,3584]{1,0:T(8,128)} fusion(bf16[1,4736,3584]{2,1,0:T(8,128)(2,1)} %param.23, f32[512,2,4736]{2,0,1:T(8,128)} %fusion), kind=kOutput, calls=%fused_computation.8 | convolution fusion | flops 17395744768 | bytes 60686336 | tf_op jit(solution)/shard_map/dot_general | solution.py:224
  760.3 68.4 %fusion.2 = f32[512,2,4736]{2,0,1:T(8,128)} fusion(bf16[3584,2,4736]{2,1,0:T(2,128)(2,1)} %bitcast.19, bf16[512,3584]{1,0:T(8,128)(2,1)} %get-tuple-element.30, f32[512]{0:T(512)S(1)} %copy-done.12, f32[3584]{0:T(1024)S(1)} %convert_reduce_fusion), kind=kOutput, calls=%fused_computation.2 | convolution fusion | flops 34769731584 | bytes 90980352 | tf_op jit(solution)/shard_map/rd,dcf->rcf/dot_general | solution.py:222
  828.7 35.2 %fusion.10 = f32[512,3584]{1,0:T(8,128)} fusion(bf16[1,4736,3584]{2,1,0:T(8,128)(2,1)} %param.23, f32[512,2,4736]{2,0,1:T(8,128)} %fusion.2), kind=kOutput, calls=%fused_computation.10 | convolution fusion | flops 17395744768 | bytes 60686336 | tf_op jit(solution)/shard_map/dot_general | solution.py:224
  864.5 68.4 %fusion.4 = f32[512,2,4736]{2,0,1:T(8,128)} fusion(bf16[3584,2,4736]{2,1,0:T(2,128)(2,1)} %bitcast.19, bf16[512,3584]{1,0:T(8,128)(2,1)} %get-tuple-element.32, f32[3584]{0:T(1024)S(1)} %convert_reduce_fusion, f32[512]{0:T(512)S(1)} %copy-done.11), kind=kOutput, calls=%fused_computation.4 | convolution fusion | flops 34769731584 | bytes 90980352 | tf_op jit(solution)/shard_map/rd,dcf->rcf/dot_general | solution.py:222
  932.9 35.3 %fusion.12 = f32[512,3584]{1,0:T(8,128)} fusion(bf16[1,4736,3584]{2,1,0:T(8,128)(2,1)} %param.23, f32[512,2,4736]{2,0,1:T(8,128)} %fusion.4), kind=kOutput, calls=%fused_computation.12 | convolution fusion | flops 17395744768 | bytes 60686336 | tf_op jit(solution)/shard_map/dot_general | solution.py:224
  968.3 2.9 add_convert_fusion
  971.3 2.8 add_convert_fusion.1
  974.2 76.3 %reduce-scatter.12.cloned.1.call-done = f32[128,3584]{1,0:T(8,128)} async-done(((f32[512,3584]{1,0:T(8,128)}), f32[128,3584]{1,0:T(8,128)}) %reduce-scatter.12.cloned.1.call-update) | async-done | bytes 1835024 | tf_op jit(solution)/shard_map/reduce_scatter | solution.py:225
  1050.4 2.8 add_convert_fusion.2
  1053.3 127.8 %reduce-scatter.10.cloned.1.call-done = f32[128,3584]{1,0:T(8,128)} async-done(((f32[512,3584]{1,0:T(8,128)}), f32[128,3584]{1,0:T(8,128)}) %reduce-scatter.10.cloned.1.call-update) | async-done | bytes 1835024 | tf_op jit(solution)/shard_map/reduce_scatter | solution.py:225
  1181.1 2.8 add_convert_fusion.3
  1183.9 1.7 fusion.75
  1185.7 8.9 copy.73
  1194.6 58.9 %all_to_all.18 = bf16[2,2048,1,128]{3,0,2,1:T(2,128)(2,1)S(1)} all-to-all(bf16[2,2048,1,128]{3,0,2,1:T(2,128)(2,1)S(1)} %copy.73), channel_id=1, replica_groups=mesh['pair'=2,'tp'=4,'side'=4] {'tp'}, dimensions={1} | all-to-all | bytes 2097152 | tf_op jit(solution)/shard_map/all_to_all | solution.py:234
  1254.5 5.0 broadcast_select_fusion
  1259.4 9.2 collective-permute-done
  1269.9 11.7 all-gather.17.cloned.1.call-done
  1283.3 4.1 slice.128
  1287.4 65.7 %all-gather.23.cloned.1.call-done = bf16[512,3584]{1,0:T(8,128)(2,1)} async-done(((bf16[128,3584]{1,0:T(8,128)(2,1)}), bf16[512,3584]{1,0:T(8,128)(2,1)}) %all-gather.23.cloned.1.call-update) | async-done | bytes 3670032 | tf_op jit(solution)/shard_map/all_gather | solution.py:229
  1353.1 71.7 %all-gather.21.cloned.1.call-done = bf16[512,3584]{1,0:T(8,128)(2,1)} async-done(((bf16[128,3584]{1,0:T(8,128)(2,1)}), bf16[512,3584]{1,0:T(8,128)(2,1)}) %all-gather.21.cloned.1.call-update) | async-done | bytes 3670032 | tf_op jit(solution)/shard_map/all_gather | solution.py:229
  1424.8 71.7 %all-gather.19.cloned.1.call-done = bf16[512,3584]{1,0:T(8,128)(2,1)} async-done(((bf16[128,3584]{1,0:T(8,128)(2,1)}), bf16[512,3584]{1,0:T(8,128)(2,1)}) %all-gather.19.cloned.1.call-update) | async-done | bytes 3670032 | tf_op jit(solution)/shard_map/all_gather | solution.py:229
  1496.6 12.9 maximum_bitcast_fusion
  (100 shorter events, 17.4 us)
Async XLA Ops:
  7.2 29.7 %copy-start.13 = (s32[32]{0:T(128)S(1)}, s32[32]{0:T(128)}, u32[]{:S(2)}) copy-start(s32[32]{0:T(128)} %param.15) | copy-start | bytes 388
  7.2 29.7 %copy-start = (bf16[1,32,64,4,128]{4,3,2,1,0:T(4,128)(2,1)S(1)}, bf16[1,32,64,4,128]{4,3,2,1,0:T(4,128)(2,1)}, u32[]{:S(2)}) copy-start(bf16[1,32,64,4,128]{4,3,2,1,0:T(4,128)(2,1)} %param.16) | copy-start | bytes 6291460
  7.2 76.3 %all-gather.27.cloned.1.call-start = ((), (), s32[]{:S(2)}) async-start(), calls=%async_computation.16 | async-start | bytes 4014080 | tf_op jit(solution)/shard_map/all_gather | solution.py:180
  9.5 227.9 %reduce-scatter.6.cloned.1.call-start = ((), (), s32[]{:S(2)}) async-start(), calls=%async_computation.6 | async-start | bytes 573440 | tf_op jit(solution)/shard_map/reduce_scatter | solution.py:170
  36.8 31.9 %copy-start.4 = (bf16[32,4,128]{2,1,0:T(4,128)(2,1)}, bf16[32,4,128]{2,1,0:T(4,128)(2,1)S(1)}, u32[]{:S(2)}) copy-start(bf16[32,4,128]{2,1,0:T(4,128)(2,1)S(1)} %copy.61) | copy-start | bytes 98308
  36.8 31.9 %copy-start.6 = (bf16[32,4,128]{2,1,0:T(4,128)(2,1)}, bf16[32,4,128]{2,1,0:T(4,128)(2,1)S(1)}, u32[]{:S(2)}) copy-start(bf16[32,4,128]{2,1,0:T(4,128)(2,1)S(1)} %copy.63) | copy-start | bytes 98308
  36.9 7.0 copy-start.8
  69.8 169.8 %all-gather.29.cloned.1.call-start = ((), (), s32[]{:S(2)}) async-start(), calls=%async_computation.17 | async-start | bytes 28901376 | tf_op jit(solution)/shard_map/all_gather | solution.py:181
  83.5 223.7 %all-gather.31.cloned.1.call-start = ((), (), s32[]{:S(2)}) async-start(), calls=%async_computation.18 | async-start | bytes 4587520 | tf_op jit(solution)/shard_map/all_gather | solution.py:217
  209.9 5.5 copy-start.14
  209.9 23.3 %copy-start.10 = (bf16[1,3584]{1,0:T(2,128)(2,1)S(1)}, bf16[1,3584]{1,0:T(2,128)(2,1)}, u32[]{:S(2)}) copy-start(bf16[1,3584]{1,0:T(2,128)(2,1)} %param.21) | copy-start | bytes 21508
  213.6 165.3 %all-gather.33.cloned.1.call-start = ((), (), s32[]{:S(2)}) async-start(), calls=%async_computation.19 | async-start | bytes 4587520 | tf_op jit(solution)/shard_map/all_gather | solution.py:217
  214.2 237.0 %all-gather.35.cloned.1.call-start = ((), (), s32[]{:S(2)}) async-start(), calls=%async_computation.20 | async-start | bytes 4587520 | tf_op jit(solution)/shard_map/all_gather | solution.py:217
  214.8 312.6 %all-gather.25.cloned.1.call-start = ((), (), s32[]{:S(2)}) async-start(), calls=%async_computation.15 | async-start | bytes 4874240 | tf_op jit(solution)/shard_map/all_gather | solution.py:217
  239.5 728.8 %reduce-scatter.8.cloned.1.call-start = ((), (), s32[]{:S(2)}) async-start(), calls=%async_computation.7 | async-start | bytes 9748480 | tf_op jit(solution)/shard_map/reduce_scatter | solution.py:225
  451.2 76.2 %copy-start.3 = (bf16[32,3584]{1,0:T(8,128)(2,1)S(1)}, bf16[32,3584]{1,0:T(8,128)(2,1)}, u32[]{:S(2)}) copy-start(bf16[32,3584]{1,0:T(8,128)(2,1)} %param.14) | copy-start | bytes 688132
  655.5 315.8 %reduce-scatter.14.cloned.1.call-start = ((), (), s32[]{:S(2)}) async-start(), calls=%async_computation.13 | async-start | bytes 9175040 | tf_op jit(solution)/shard_map/reduce_scatter | solution.py:225
  759.6 0.7 copy-start.12
  759.6 290.8 %reduce-scatter.12.cloned.1.call-start = ((), (), s32[]{:S(2)}) async-start(), calls=%async_computation.11 | async-start | bytes 9175040 | tf_op jit(solution)/shard_map/reduce_scatter | solution.py:225
  863.9 0.6 copy-start.11
  863.9 317.2 %reduce-scatter.10.cloned.1.call-start = ((), (), s32[]{:S(2)}) async-start(), calls=%async_computation.9 | async-start | bytes 9175040 | tf_op jit(solution)/shard_map/reduce_scatter | solution.py:225
  968.2 313.5 %all-gather.17.cloned.1.call-start = ((), (), s32[]{:S(2)}) async-start(), calls=%async_computation.8 | async-start | bytes 4874240 | tf_op jit(solution)/shard_map/all_gather | solution.py:229
  971.2 382.0 %all-gather.23.cloned.1.call-start = ((), (), s32[]{:S(2)}) async-start(), calls=%async_computation.14 | async-start | bytes 4587520 | tf_op jit(solution)/shard_map/all_gather | solution.py:229
  974.1 450.7 %all-gather.21.cloned.1.call-start = ((), (), s32[]{:S(2)}) async-start(), calls=%async_computation.12 | async-start | bytes 4587520 | tf_op jit(solution)/shard_map/all_gather | solution.py:229
  1053.2 201.2 %copy-start.1 = (bf16[1,32,64,4,128]{4,3,2,1,0:T(4,128)(2,1)S(1)}, bf16[1,32,64,4,128]{4,3,2,1,0:T(4,128)(2,1)}, u32[]{:S(2)}) copy-start(bf16[1,32,64,4,128]{4,3,2,1,0:T(4,128)(2,1)} %param.16) | copy-start | bytes 6291460
  1053.2 201.2 %copy-start.5 = (bf16[32,4,128]{2,1,0:T(4,128)(2,1)S(1)}, bf16[32,4,128]{2,1,0:T(4,128)(2,1)}, u32[]{:S(2)}) copy-start(bf16[32,4,128]{2,1,0:T(4,128)(2,1)} %copy-done.4) | copy-start | bytes 98308
  1053.2 201.2 %copy-start.7 = (bf16[32,4,128]{2,1,0:T(4,128)(2,1)S(1)}, bf16[32,4,128]{2,1,0:T(4,128)(2,1)}, u32[]{:S(2)}) copy-start(bf16[32,4,128]{2,1,0:T(4,128)(2,1)} %copy-done.6) | copy-start | bytes 98308
  1053.2 201.2 %copy-start.9 = (pred[32,64]{1,0:T(8,128)(4,1)S(1)}, pred[32,64]{1,0:T(8,128)(4,1)}, u32[]{:S(2)}) copy-start(pred[32,64]{1,0:T(8,128)(4,1)} %copy-done.8) | copy-start | bytes 6148
  1053.3 443.3 %all-gather.19.cloned.1.call-start = ((), (), s32[]{:S(2)}) async-start(), calls=%async_computation.10 | async-start | bytes 4587520 | tf_op jit(solution)/shard_map/all_gather | solution.py:229
  1183.9 70.5 %copy-start.2 = (bf16[1,32,64,4,128]{4,3,2,1,0:T(4,128)(2,1)S(1)}, bf16[1,32,64,4,128]{4,3,2,1,0:T(4,128)(2,1)}, u32[]{:S(2)}) copy-start(bf16[1,32,64,4,128]{4,3,2,1,0:T(4,128)(2,1)} %param.17) | copy-start | bytes 6291460
  1254.3 14.3 collective-permute-start
Sparse Core Ops, SparseCore 0:
  10.1 73.2 all-gather.26
  86.3 20.2 reduce-scatter.5
  108.5 125.7 all-gather.28
  235.7 71.4 all-gather.30
  308.6 70.2 all-gather.32
  380.9 70.2 all-gather.34
  453.3 74.0 all-gather.24
  655.6 133.7 reduce-scatter.7
  791.6 128.2 reduce-scatter.13
  922.1 128.2 reduce-scatter.11
  1052.8 128.2 reduce-scatter.9
  1183.1 98.5 all-gather.16
  1283.2 69.8 all-gather.22
  1354.6 70.2 all-gather.20
  1426.3 70.2 all-gather.18

commit v2 on v1

--- a/solution.py
+++ b/solution.py
@@ -147,6 +147,379 @@
     )(slen, qkv, qkv, qkv)
 
 
+MESH = pl.DeviceIdType.MESH
+CHUNKS = 4
+SUBS = 5
+SLOTS = 2
+ACCS = 3
+TILE = 256
+TILE_OUT = 512
+
+
+def layer_kernel(geo, ctx_hbm, x_hbm, y_hbm, gain_ref, wo_ref, wg_ref, wu_ref, wd_ref, out_hbm, full_hbm, hid_hbm,
+                 cx, hid, acc, slot, fin, res, rs_recv, rs_send, credit, ag_recv, ag_send, fin_sem, res_sem,
+                 ctx_recv, ctx_send, load_sem, hid_sem):
+    width, head_cols, step, dec, ff_tiles, tail = geo
+    rows = step + dec
+    sub = rows // SUBS
+    total = CHUNKS * SUBS
+    half = width // 2
+    out_tiles = width // TILE_OUT
+    ticks = out_tiles + ff_tiles
+    stride = ticks // SUBS
+    tp = width // head_cols
+    last = tp - 1
+    c, j = pl.program_id(0), pl.program_id(1)
+    t = lax.axis_index('tp')
+
+    def at(cond):
+        return pl.when(cond)
+
+    def ctx_copy(chunk, source, right):
+        src = full_hbm.at[source, chunk]
+        return pltpu.make_async_remote_copy(
+            src_ref=src, dst_ref=full_hbm.at[source, chunk], send_sem=ctx_send.at[chunk, source, 0 if right else 1],
+            recv_sem=ctx_recv.at[chunk, source], device_id={'tp': t + 1 if right else t - 1}, device_id_type=MESH)
+
+    def ctx_first(chunk):
+        def own(right):
+            return pltpu.make_async_remote_copy(
+                src_ref=ctx_hbm.at[chunk], dst_ref=full_hbm.at[t, chunk], send_sem=ctx_send.at[chunk, t, 0 if right else 1],
+                recv_sem=ctx_recv.at[chunk, t], device_id={'tp': t + 1 if right else t - 1}, device_id_type=MESH)
+
+        @at(t < last)
+        def _():
+            own(True).start()
+
+        @at(t > 0)
+        def _():
+            own(False).start()
+
+    def ctx_hop(chunk, hop):
+        @at(t >= hop)
+        def _():
+            ctx_copy(chunk, t - hop, True).wait_recv()
+
+            @at(t < last)
+            def _():
+                ctx_copy(chunk, t - hop, True).start()
+
+        @at(t + hop <= last)
+        def _():
+            ctx_copy(chunk, t + hop, False).wait_recv()
+
+            @at(t > 0)
+            def _():
+                ctx_copy(chunk, t + hop, False).start()
+
+    flows = []
+    for f in range(2):
+        place = last - t if f == 0 else t
+        nxt = t - 1 if f == 0 else t + 1
+        prv = t + 1 if f == 0 else t - 1
+        flows.append((f, place, nxt, prv, f * half))
+
+    def part(k, col):
+        first = pl.multiple_of((k % SUBS) * sub, 8)
+        return acc.at[(k // SUBS) % ACCS, pl.ds(first, sub), pl.ds(col, half)]
+
+    def out_rows(k, col):
+        return out_hbm.at[pl.ds(pl.multiple_of(k * sub, 8), sub), pl.ds(col, half)]
+
+    def rs_copy(f, k, col, device):
+        return pltpu.make_async_remote_copy(
+            src_ref=part(k, col), dst_ref=slot.at[f, k % SLOTS], send_sem=rs_send.at[f, k % SLOTS],
+            recv_sem=rs_recv.at[f, k % SLOTS], device_id={'tp': device}, device_id_type=MESH)
+
+    def ag_copy(f, k, col, device, first):
+        return pltpu.make_async_remote_copy(
+            src_ref=fin.at[f, k % SLOTS] if first else out_rows(k, col), dst_ref=out_rows(k, col), send_sem=ag_send.at[f, k],
+            recv_sem=ag_recv.at[f, k], device_id={'tp': device}, device_id_type=MESH)
+
+    def fin_copy(f, k, col):
+        return pltpu.make_async_copy(fin.at[f, k % SLOTS], out_rows(k, col), fin_sem.at[f, k % SLOTS])
+
+    def res_copy(f, k, col):
+        rows_k = hid_hbm.at[pl.ds(pl.multiple_of(k * sub, 8), sub), pl.ds(col, half)]
+        return pltpu.make_async_copy(rows_k, res.at[f, k % SLOTS], res_sem.at[f, k % SLOTS])
+
+    def collect(m):
+        for f, place, nxt, prv, col in flows:
+            k = m - place
+
+            @at((k >= 0) & (k < total) & (place > 0))
+            def _(f=f, place=place, nxt=nxt, prv=prv, col=col, k=k):
+                rs_copy(f, k, col, nxt).wait_recv()
+                mine = part(k, col)
+
+                @at(place < last)
+                def _():
+                    mine[...] += slot[f, k % SLOTS]
+
+                @at(place == last)
+                def _():
+                    res_copy(f, k, col).wait()
+
+                    @at(k >= SLOTS)
+                    def _():
+                        fin_copy(f, k, col).wait()
+                        ag_copy(f, k - SLOTS, col, prv, True).wait_send()
+
+                    both = mine[...] + slot[f, k % SLOTS]
+                    fin[f, k % SLOTS] = (res[f, k % SLOTS].astype(F32) + both).astype(BF)
+
+                @at(k + SLOTS < total)
+                def _():
+                    pl.semaphore_signal(credit.at[f], inc=1, device_id={'tp': prv}, device_id_type=MESH)
+
+    def send(m):
+        for f, place, nxt, prv, col in flows:
+            k = m - place
+
+            @at((k >= 0) & (k < total) & (place < last))
+            def _(f=f, nxt=nxt, col=col, k=k):
+                @at(k >= SLOTS)
+                def _():
+                    pl.semaphore_wait(credit.at[f], 1)
+                    rs_copy(f, k - SLOTS, col, nxt).wait_send()
+
+                rs_copy(f, k, col, nxt).start()
+
+            @at((k >= 0) & (k < total) & (place == last))
+            def _(f=f, prv=prv, col=col, k=k):
+                fin_copy(f, k, col).start()
+                ag_copy(f, k, col, prv, True).start()
+
+            ahead = k + 1
+
+            @at((ahead >= 0) & (ahead < total) & (place == last))
+            def _(f=f, col=col, ahead=ahead):
+                res_copy(f, ahead, col).start()
+
+            a = m - 2 * last + place
+
+            @at((a >= 0) & (a < total) & (place < last))
+            def _(f=f, place=place, prv=prv, col=col, a=a):
+                ag_copy(f, a, col, prv, False).wait_recv()
+
+                @at(place > 0)
+                def _():
+                    ag_copy(f, a, col, prv, False).start()
+
+    @at((c == 0) & (j == 0))
+    def _():
+        barrier = pltpu.get_barrier_semaphore()
+
+        @at(t > 0)
+        def _():
+            pl.semaphore_signal(barrier, inc=1, device_id={'tp': t - 1}, device_id_type=MESH)
+
+        @at(t < last)
+        def _():
+            pl.semaphore_signal(barrier, inc=1, device_id={'tp': t + 1}, device_id_type=MESH)
+
+        @at((t > 0) & (t < last))
+        def _():
+            pl.semaphore_wait(barrier, 2)
+
+        @at((t == 0) | (t == last))
+        def _():
+            pl.semaphore_wait(barrier, 1)
+
+        ctx_first(0)
+        cx[...] = jnp.zeros_like(cx)
+        hid[...] = jnp.zeros_like(hid)
+        for hop in range(1, last):
+            ctx_hop(0, hop)
+        ctx_first(1)
+        ctx_hop(0, last)
+
+    for i in range(SUBS):
+        @at((c > 0) & (j == stride * i + 1))
+        def _(i=i):
+            collect(SUBS * (c - 1) + i)
+
+        @at((c > 0) & (j == stride * i + 2))
+        def _(i=i):
+            send(SUBS * (c - 1) + i)
+
+    for hop in range(1, last + 1):
+        @at((c + 1 < CHUNKS) & (j == stride * hop + 3))
+        def _(hop=hop):
+            ctx_hop(c + 1, hop)
+            if hop == last:
+                @at(c + 2 < CHUNKS)
+                def _():
+                    ctx_first(c + 2)
+
+    @at(j == 0)
+    def _():
+        loads = [
+            pltpu.make_async_copy(x_hbm.at[pl.ds(pl.multiple_of(c * step, 8), step)], hid.at[pl.ds(0, step)], load_sem.at[tp]),
+            pltpu.make_async_copy(y_hbm.at[pl.ds(pl.multiple_of(c * dec, 8), dec)], hid.at[pl.ds(step, dec)], load_sem.at[tp + 1]),
+        ]
+        for copy in loads:
+            copy.start()
+        for s in range(tp):
+            where = cx.at[pl.ds(0, rows), pl.ds(s * head_cols, head_cols)]
+
+            @at(t == s)
+            def _(s=s, where=where):
+                pltpu.make_async_copy(ctx_hbm.at[c], where, load_sem.at[s]).start()
+
+            @at(t != s)
+            def _(s=s, where=where):
+                pltpu.make_async_copy(full_hbm.at[s, c], where, load_sem.at[s]).start()
+
+        for s in range(tp):
+            where = cx.at[pl.ds(0, rows), pl.ds(s * head_cols, head_cols)]
+            pltpu.make_async_copy(ctx_hbm.at[c], where, load_sem.at[s]).wait()
+        for copy in loads:
+            copy.wait()
+
+    @at(j < out_tiles)
+    def _():
+        heads = head_cols // 128
+        mixed = None
+        for s in range(tp):
+            w = wo_ref[:heads, s].reshape(head_cols, TILE_OUT)
+            one = jnp.dot(cx[:, s * head_cols:(s + 1) * head_cols], w, preferred_element_type=F32)
+            mixed = one if mixed is None else mixed + one
+        cols = pl.ds(pl.multiple_of(j * TILE_OUT, TILE_OUT), TILE_OUT)
+        hid[:, cols] = (hid[:, cols].astype(F32) + mixed).astype(BF)
+
+    hid_copy = pltpu.make_async_copy(hid.at[pl.ds(0, rows)], hid_hbm.at[pl.ds(pl.multiple_of(c * rows, 8), rows)], hid_sem)
+
+    @at(j == out_tiles)
+    def _():
+        hid_copy.start()
+        block = hid.shape[0] // 11
+
+        @pl.loop(0, 11)
+        def _(b):
+            some = pl.ds(pl.multiple_of(b * block, 16), block)
+            h = hid[some].astype(F32)
+            inv = lax.rsqrt(jnp.mean(h * h, axis=-1, keepdims=True) + NORM_EPS)
+            cx[some] = (h * inv * gain_ref[...].astype(F32)).astype(BF)
+            acc[c % ACCS, some] = jnp.zeros((block, width), F32)
+
+    @at(j >= out_tiles)
+    def _():
+        gate = jnp.dot(cx[...], wg_ref[0], preferred_element_type=F32)
+        up = jnp.dot(cx[...], wu_ref[0], preferred_element_type=F32)
+        act = (jax.nn.silu(gate) * up).astype(BF)
+        which = c % ACCS
+
+        @at(j < ticks - 1)
+        def _():
+            acc[which] += jnp.dot(act, wd_ref[...], preferred_element_type=F32)
+
+        @at(j == ticks - 1)
+        def _():
+            acc[which] += jnp.dot(act[:, :tail], wd_ref[:tail], preferred_element_type=F32)
+            hid_copy.wait()
+
+    @at((c == CHUNKS - 1) & (j == ticks - 1))
+    def _():
+        @pl.loop(SUBS * (CHUNKS - 1), total + 2 * last)
+        def _(m):
+            collect(m)
+            send(m)
+
+        for f, place, nxt, prv, col in flows:
+            @at(place < last)
+            def _(f=f, nxt=nxt, col=col):
+                for k in range(total - SLOTS, total):
+                    rs_copy(f, k, col, nxt).wait_send()
+
+            @at(place == last)
+            def _(f=f, prv=prv, col=col):
+                for k in range(total - SLOTS, total):
+                    fin_copy(f, k, col).wait()
+                    ag_copy(f, k, col, prv, True).wait_send()
+
+            @at((place < last) & (place > 0))
+            def _(f=f, prv=prv, col=col):
+                @pl.loop(0, total)
+                def _(k):
+                    ag_copy(f, k, col, prv, False).wait_send()
+
+        for source in range(tp):
+            @at((source <= t) & (t < last))
+            def _(source=source):
+                for chunk in range(CHUNKS):
+                    ctx_copy(chunk, source, True).wait_send()
+
+            @at((source >= t) & (t > 0))
+            def _(source=source):
+                for chunk in range(CHUNKS):
+                    ctx_copy(chunk, source, False).wait_send()
+
+
+def layer_sums(ctx, x, y, gain, w_full, w_gate_up, w_down):
+    _, rows, head_cols = ctx.shape
+    seq, width = x.shape
+    step, dec = seq // CHUNKS, y.shape[0] // CHUNKS
+    ff = w_down.shape[0]
+    ff_tiles = pl.cdiv(ff, TILE)
+    tail = ff - (ff_tiles - 1) * TILE
+    out_tiles = width // TILE_OUT
+    tp = width // head_cols
+    pad = (rows + 15) // 16 * 16
+    half = width // 2
+    sub = rows // SUBS
+    total = CHUNKS * SUBS
+    geo = (width, head_cols, step, dec, ff_tiles, tail)
+    heads = head_cols // 128
+
+    def ff_index(j):
+        return jnp.maximum(j - out_tiles, 0)
+
+    any_spec = pl.BlockSpec(memory_space=pl.ANY)
+    flops = 2 * CHUNKS * rows * width * (width + 3 * ff)
+    moved = 2 * CHUNKS * (width * width + 3 * width * ff)
+    return pl.pallas_call(
+        functools.partial(layer_kernel, geo),
+        grid=(CHUNKS, out_tiles + ff_tiles),
+        in_specs=[
+            any_spec, any_spec, any_spec,
+            pl.BlockSpec((1, width), lambda c, j: (0, 0)),
+            pl.BlockSpec((heads, tp, 128, TILE_OUT), lambda c, j: (0, 0, 0, jnp.minimum(j, out_tiles - 1))),
+            pl.BlockSpec((1, width, TILE), lambda c, j: (0, 0, ff_index(j))),
+            pl.BlockSpec((1, width, TILE), lambda c, j: (1, 0, ff_index(j))),
+            pl.BlockSpec((TILE, width), lambda c, j: (ff_index(j), 0)),
+        ],
+        out_specs=[any_spec, any_spec, any_spec],
+        out_shape=[
+            jax.ShapeDtypeStruct((CHUNKS * rows, width), BF),
+            jax.ShapeDtypeStruct((tp, CHUNKS, rows, head_cols), BF),
+            jax.ShapeDtypeStruct((CHUNKS * rows, width), BF),
+        ],
+        scratch_shapes=[
+            pltpu.VMEM((pad, width), BF),
+            pltpu.VMEM((pad, width), BF),
+            pltpu.VMEM((ACCS, pad, width), F32),
+            pltpu.VMEM((2, SLOTS, sub, half), F32),
+            pltpu.VMEM((2, SLOTS, sub, half), BF),
+            pltpu.VMEM((2, SLOTS, sub, half), BF),
+            pltpu.SemaphoreType.DMA((2, SLOTS)),
+            pltpu.SemaphoreType.DMA((2, SLOTS)),
+            pltpu.SemaphoreType.REGULAR((2,)),
+            pltpu.SemaphoreType.DMA((2, total)),
+            pltpu.SemaphoreType.DMA((2, total)),
+            pltpu.SemaphoreType.DMA((2, SLOTS)),
+            pltpu.SemaphoreType.DMA((2, SLOTS)),
+            pltpu.SemaphoreType.DMA((CHUNKS, tp)),
+            pltpu.SemaphoreType.DMA((CHUNKS, tp, 2)),
+            pltpu.SemaphoreType.DMA((tp + 2,)),
+            pltpu.SemaphoreType.DMA(()),
+        ],
+        compiler_params=pltpu.CompilerParams(collective_id=0, has_side_effects=True, vmem_limit_bytes=67000000, dimension_semantics=('arbitrary', 'arbitrary')),
+        cost_estimate=pl.CostEstimate(flops=flops, bytes_accessed=moved, transcendentals=0),
+        name='layer_sums',
+    )(ctx, x, y, gain, w_full, w_gate_up, w_gate_up, w_down)[0]
+
+
 def decode_context(tokens, cache_lens, k_cache, v_cache, gain, w_qkv):
     group_q = w_qkv.shape[2] - 2
     head_dim = w_qkv.shape[3]
@@ -173,10 +546,8 @@
 
 
 def gather_w_out(w_out, mesh):
-    plane = mesh.shape['pair'] * mesh.shape['side']
-    rows = w_out.shape[0] // plane
     index = lax.axis_index('pair') * mesh.shape['side'] + lax.axis_index('side')
-    own = lax.dynamic_slice_in_dim(w_out, index * rows, rows, 0)
+    own = lax.dynamic_index_in_dim(w_out, jnp.minimum(index, w_out.shape[0] - 1), 0, keepdims=False)
     column = lax.all_gather(own, 'tp')
     return lax.all_gather(column, ('pair', 'side'))
 
@@ -196,8 +567,8 @@
         cos, sin = rope_tables(positions, head)
         cos, sin = jnp.concatenate([cos, cos], -1), jnp.concatenate([-sin, sin], -1)
 
-        w_full = gather_w_out(w_out[0, 0].reshape(group_q * head, width), mesh)
-        w_full = jnp.moveaxis(w_full, 1, 0).reshape(tp, group_q * head, width)
+        w_full = gather_w_out(w_out[0, 0], mesh)
+        gate_up = jnp.transpose(w_gate_up[0], (1, 0, 2))
 
         dctx, key_now, value_now = decode_context(y_tok, c_len, k_cache[0], v_cache[0], attn_gain[0], w_qkv[0])
         dctx = dctx.reshape(dctx.shape[0], group_q * head)
@@ -206,29 +577,12 @@
         qkv = project_qkv(x, attn_gain, cos, sin, w_slots)
         ctx = attend(s_len, qkv)
 
-        chunks = 4
-        step = seq_len // chunks
-        hid = []
-        outs = []
-        for c in range(chunks):
-            ctx_c, x_c = ctx[c * step:(c + 1) * step], x[c * step:(c + 1) * step]
-            if c == 0:
-                ctx_c, x_c = jnp.concatenate([ctx_c, dctx]), jnp.concatenate([x_c, y_tok])
-            full = lax.all_gather(ctx_c, 'tp')
-            mixed = jnp.einsum('trf,tfd->rd', full, w_full, preferred_element_type=F32)
-            hid.append((x_c.astype(F32) + mixed).astype(BF))
-        for c in range(chunks):
-            normed = rms_norm(hid[c], mlp_gain[0])
-            gate_up = jnp.einsum('rd,dcf->rcf', normed, w_gate_up[0], preferred_element_type=F32)
-            activated = (jax.nn.silu(gate_up[:, 0]) * gate_up[:, 1]).astype(BF)
-            part = jnp.dot(activated, w_down[0], preferred_element_type=F32)
-            own = lax.psum_scatter(part, 'tp', scatter_dimension=0, tiled=True)
-            rows = own.shape[0]
-            own_hid = lax.dynamic_slice_in_dim(hid[c], lax.axis_index('tp') * rows, rows, 0)
-            own = (own_hid.astype(F32) + own).astype(BF)
-            outs.append(lax.all_gather(own, 'tp', axis=0, tiled=True))
-        tokens = outs[0][step:]
-        hidden = jnp.concatenate([outs[0][:step]] + outs[1:])
+        step, dec = seq_len // CHUNKS, y_tok.shape[0] // CHUNKS
+        ctx_all = jnp.concatenate([ctx.reshape(CHUNKS, step, -1), dctx.reshape(CHUNKS, dec, -1)], axis=1)
+        done = layer_sums(ctx_all, x, y_tok, mlp_gain, w_full, gate_up, w_down[0])
+        done = done.reshape(CHUNKS, step + dec, width)
+        hidden = done[:, :step].reshape(seq_len, width)
+        tokens = done[:, step:].reshape(CHUNKS * dec, width)
 
         kv_pair = (qkv[group_q:] * keep_mask)[:, :, None]
         kv_by_pos = lax.all_to_all(kv_pair, 'tp', 1, 2, tiled=True)

time: 1520 us -> 1150 us (0.76)
  Pallas kernels: 120 us -> 918 us
  waiting for transfers between devices: 653 us -> 20.5 us
  matrix products: 512 us -> 8.78 us
  blocking collectives: 116 us -> 73.2 us
  local copies, waits for them, and re-layouts: 48.8 us -> 77.4 us
  other arithmetic: 50.1 us -> 31 us
    pallas_call x0 -> x1, Pallas kernels: none -> 798 us  [layer_sums(): pl.pallas_call(functools.partial(layer_kernel, geo), grid=(CHUNKS, out_ti...]
    dot_general x12 -> x0, matrix products: 503 us -> none  [the longest x4 274 us: device_fn(): jnp.einsum('rd,dcf->rcf', normed, w_gate_up[0], preferred_element_type=F32)]
    all_gather x8 -> x0, waiting for transfers between devices: 425 us -> none  [the longest x4 221 us: device_fn(): outs.append(lax.all_gather(own, 'tp', axis=0, tiled=True))]
    reduce_scatter x4 -> x0, waiting for transfers between devices: 204 us -> none  [device_fn(): own = lax.psum_scatter(part, 'tp', scatter_dimension=0, tiled=True)]
    all_to_all x1 -> x0, blocking collectives: 58.9 us -> none  [device_fn(): kv_by_pos = lax.all_to_all(kv_pair, 'tp', 1, 2, tiled=True)]
    unnamed x32 -> x10, local copies, waits for them, and re-layouts: 1.83 us -> 45.7 us
    transpose x1 -> x0, local copies, waits for them, and re-layouts: 18.2 us -> none  [device_fn(): w_full = jnp.moveaxis(w_full, 1, 0).reshape(tp, group_q * head, width)]
    unnamed x1, blocking collectives: 16.6 us -> 32.2 us
  transfers between devices with their start and end apart: 16 -> 5, of which waited for: 12 -> 1; matrix products, arithmetic and copies ran while one was open for 31% -> 9% of each run, Pallas kernels for 8% -> 10%
where the time goes in v2:
time: 1150 us
  Pallas kernels  918 us (80%)
  local copies, waits for them, and re-layouts  77.4 us (7%)
  blocking collectives  73.2 us (6%)
  other arithmetic  31 us (3%)
  waiting for transfers between devices  20.5 us (2%)
  between operations  15.1 us (1%)
    pallas_call x1, Pallas kernels, layer_sums(): pl.pallas_call(functools.partial(layer_kernel, geo), grid=(CHUNKS, out_ti...  798 us
    pallas_call x1, Pallas kernels, attend(): pl.pallas_call(functools.partial(flash_kernel, block_q, block_k), grid_sp...  91.1 us
    unnamed x10, local copies, waits for them, and re-layouts  45.7 us
    unnamed x1, blocking collectives  32.2 us
    pallas_call x1, Pallas kernels, project_qkv(): pl.pallas_call(qkv_kernel, grid=(rows // rows_block,), in_specs=[pl.Block...  28.8 us
  transfers between devices with their start and end apart: 5, of which 1 were waited for; matrix products, arithmetic and copies ran while one was open for 9% of the time, Pallas kernels for 10%

profile of v2, /device:TPU:0, one launch (start us, length us, event | category | flops | bytes accessed | tf_op | source)
XLA Modules:
  0.0 1147.8 jit_solution(13295312514909154162)
XLA Ops:
  7.2 0.0 all-gather.5.cloned.1.call-start
  7.2 2.2 constant_dynamic-slice_fusion
  9.4 0.0 all-gather.5.cloned.1.call-update
  9.4 0.0 reduce-scatter.2.cloned.1.call-start
  9.5 0.7 convert_element_type.51
  10.1 0.8 convert_reduce_fusion
  10.9 1.1 fusion.18
  12.0 0.0 copy-start.2
  12.0 0.0 copy-start
  12.0 5.2 fusion.12
  17.2 0.1 multiply_cosine_fusion.1
  17.3 0.1 subtract_convert_fusion
  17.5 0.1 pad_maximum_fusion.3
  17.6 19.2 %all_gather.13 = bf16[32,4,9,128]{3,0,2,1:T(8,128)(2,1)S(1)} all-gather(bf16[32,1,9,128]{3,0,2,1:T(8,128)(2,1)S(1)} %pad_maximum_fusion.3), channel_id=1, replica_groups=mesh['pair'=2,'tp'=4,'side'=4] {'tp'}, dimensions={1}, use_global_device_ids=true | all-gather | bytes 368640 | tf_op jit(solution)/shard_map/all_gather | solution.py:534
  36.9 0.1 broadcast_compare_fusion.1
  37.0 6.9 bitcast_select_fusion.1
  43.9 1.3 fusion.30
  45.2 21.8 %pmax.7 = f32[32,4,7]{2,1,0:T(4,128)S(1)} all-reduce(f32[32,4,7]{2,1,0:T(4,128)S(1)} %get-tuple-element.25), channel_id=1, replica_groups=mesh['pair'=2,'tp'=4,'side'=4] {'tp'}, use_global_device_ids=true, to_apply=%region_2.3 | all-reduce | flops 896 | bytes 7168 | tf_op jit(solution)/shard_map/pmax | solution.py:539
  67.0 2.3 fusion.2
  69.3 1.1 copy.54
  70.4 0.0 reduce-scatter.2.cloned.1.call-update
  70.4 0.2 all-gather.7.cloned.1.call-start
  70.6 20.5 %all-gather.5.cloned.1.call-done = bf16[4,1,1,128,3584]{4,3,2,1,0:T(8,128)(2,1)} async-done(((bf16[1,1,1,128,3584]{4,3,2,1,0:T(8,128)(2,1)}), bf16[4,1,1,128,3584]{4,3,2,1,0:T(8,128)(2,1)}) %all-gather.5.cloned.1.call-update) | async-done | bytes 3670032 | tf_op jit(solution)/shard_map/all_gather | solution.py:551
  91.1 0.0 all-gather.7.cloned.1.call-update
  91.8 3.7 fusion.21
  95.6 1.9 pad_maximum_fusion.1
  97.5 28.8 %project_qkv.1.q_ref.k_ref.v_ref = bf16[9,2048,128]{2,1,0:T(8,128)(2,1)} custom-call(bf16[2048,3584]{1,0:T(8,128)(2,1)} %bitcast.60, bf16[1,3584]{1,0:T(2,128)(2,1)} %gain_ref.2, f32[2048,128]{1,0:T(8,128)} %get-tuple-element.27.cos_ref, f32[2048,128]{1,0:T(8,128)} %get-tuple-element.28.sin_ref, bf16[9,3584,128]{2,1,0:T(8,128)(2,1)} %bitcast.55), custom_call_target="tpu_custom_call" | custom-call | flops 16911433728 | bytes 27656192 | tf_op jit(solution)/shard_map/project_qkv/pallas_call | solution.py:59
  126.3 1.6 fusion.15
  127.8 9.5 copy.58
  137.3 3.7 all-to-all-start
  141.0 1.4 fusion.16
  142.5 0.1 copy.55
  142.6 0.6 dynamic-slice.1
  143.2 32.2 %all-reduce = f32[32,4,7]{0,2,1:T(8,128)S(1)} all-reduce(f32[32,4,7]{0,2,1:T(8,128)S(1)} %copy.55), channel_id=5, replica_groups=mesh['pair'=2,'tp'=4,'side'=4] {'tp'}, use_global_device_ids=true, to_apply=%region_5.6.clone | all-reduce | flops 896 | bytes 7168
  175.4 91.1 %attend.1 = bf16[2048,896]{1,0:T(8,128)(2,1)} custom-call(s32[1]{0:T(128)} %copy.81.slen_ref, bf16[9,2048,128]{2,1,0:T(8,128)(2,1)} %project_qkv.1.q_ref.k_ref.v_ref, bf16[9,2048,128]{2,1,0:T(8,128)(2,1)} %project_qkv.1.q_ref.k_ref.v_ref, bf16[9,2048,128]{2,1,0:T(8,128)(2,1)} %project_qkv.1.q_ref.k_ref.v_ref), custom_call_target="tpu_custom_call" | custom-call | flops 11274289152 | bytes 8388608 | tf_op jit(solution)/shard_map/attend/pallas_call | solution.py:127
  266.5 1.8 copy.80
  268.3 0.2 collective-permute-start
  268.5 0.7 dynamic-slice_bitcast_fusion
  269.2 45.1 %copy.79 = bf16[1,3584,2,4736]{3,1,2,0:T(8,128)(2,1)} copy(bf16[1,3584,2,4736]{3,2,1,0:T(2,128)(2,1)} %param.22) | data formatting | bytes 135790592 | tf_op args[10]
  314.3 7.3 broadcast_select_fusion
  321.6 1.0 divide_convert_fusion
  322.6 0.1 reshape_reshape.3
  322.7 4.2 pad_maximum_fusion.ctx_hbm
  326.9 0.0 collective-permute-done
  326.9 1.3 slice_bitcast_fusion
  328.3 797.7 %layer_sums.1 = (bf16[2080,3584]{1,0:T(8,128)(2,1)}, bf16[4,4,520,896]{3,2,1,0:T(8,128)(2,1)}, bf16[2080,3584]{1,0:T(8,128)(2,1)}) custom-call(bf16[4,520,896]{2,1,0:T(8,128)(2,1)} %pad_maximum_fusion.ctx_hbm, bf16[2048,3584]{1,0:T(8,128)(2,1)} %bitcast.61, bf16[32,3584]{1,0:T(8,128)(2,1)} %y_hbm.1, bf16[1,3584]{1,0:T(2,128)(2,1)} %gain_ref.3, ...), custom_call_target="tpu_custom_call" | custom-call | flops 265268756480 | bytes 510132224 | tf_op jit(solution)/shard_map/layer_sums/pallas_call | solution.py:481
  1125.9 13.3 %slice.54 = bf16[4,512,3584]{2,1,0:T(8,128)(2,1)} slice(bf16[4,520,3584]{2,1,0:T(8,128)(2,1)} %bitcast.52), slice={[0:4], [0:512], [0:3584]} | slice | bytes 29360128 | tf_op jit(solution)/shard_map/slice | solution.py:584
  1139.2 1.6 slice_bitcast_fusion.2
  (20 shorter events, 0.1 us)
Async XLA Ops:
  7.2 84.0 %all-gather.5.cloned.1.call-start = ((), (), s32[]{:S(2)}) async-start(), calls=%async_computation.3 | async-start | bytes 4587520 | tf_op jit(solution)/shard_map/all_gather | solution.py:551
  9.4 312.2 %reduce-scatter.2.cloned.1.call-start = ((), (), s32[]{:S(2)}) async-start(), calls=%async_computation.2 | async-start | bytes 573440 | tf_op jit(solution)/shard_map/reduce_scatter | solution.py:543
  12.0 24.9 %copy-start.2 = (s32[32]{0:T(128)S(1)}, s32[32]{0:T(128)}, u32[]{:S(2)}) copy-start(s32[32]{0:T(128)} %param.15) | copy-start | bytes 388
  12.0 25.0 %copy-start = (bf16[1,32,64,4,128]{4,3,2,1,0:T(4,128)(2,1)S(1)}, bf16[1,32,64,4,128]{4,3,2,1,0:T(4,128)(2,1)}, u32[]{:S(2)}) copy-start(bf16[1,32,64,4,128]{4,3,2,1,0:T(4,128)(2,1)} %param.16) | copy-start | bytes 6291460
  45.2 45.9 %copy-start.1 = (f32[32,4,7,64]{3,2,1,0:T(8,128)}, f32[32,4,7,64]{3,2,1,0:T(8,128)S(1)}, u32[]{:S(2)}) copy-start(f32[32,4,7,64]{3,2,1,0:T(8,128)S(1)} %get-tuple-element.26) | copy-start | bytes 688132
  70.4 257.8 %all-gather.7.cloned.1.call-start = ((), (), s32[]{:S(2)}) async-start(), calls=%async_computation.4 | async-start | bytes 33030144 | tf_op jit(solution)/shard_map/all_gather | solution.py:552
  126.3 16.3 %copy-start.3 = (u32[32]{0:T(128)S(1)}, u32[32]{0:T(128)}, u32[]{:S(2)}) copy-start(u32[32]{0:T(128)} %constant.52) | copy-start | bytes 388
  137.3 129.2 %all-to-all-start = ((bf16[2,2048,1,128]{3,0,2,1:T(2,128)(2,1)}), bf16[2,2048,1,128]{3,0,2,1:T(2,128)(2,1)S(1)}, u32[]{:S(2)}, u32[]{:S(2)}) async-start(bf16[2,2048,1,128]{3,0,2,1:T(2,128)(2,1)} %copy.58), calls=%async_computation.1 | async-start | bytes 2097152 | tf_op jit(solution)/shard_map/all_to_all | solution.py:588
  268.3 58.7 %collective-permute-start = (bf16[2,512,4,128]{3,2,1,0:T(4,128)(2,1)}, bf16[2,512,4,128]{3,2,1,0:T(4,128)(2,1)S(1)}, u32[]{:S(2)}, u32[]{:S(2)}) collective-permute-start(bf16[2,512,4,128]{3,2,1,0:T(4,128)(2,1)} %bitcast.50), channel_id=1, source_target_pairs={{0,1},{1,2},{2,3},{3,0},{4,5},{5,6},{6,7},{7,4},{8,9},{9,10},{10,1... | collective-permute-start | bytes 3145736 | tf_op jit(solution)/shard_map/ppermute | solution.py:589
Sparse Core Ops, SparseCore 0:
  10.1 80.9 all-gather.4
  94.0 19.9 reduce-scatter.1
  115.9 141.2 all-gather.6

commit v3 on v2

--- a/solution.py
+++ b/solution.py
@@ -73,59 +73,79 @@
     )(x, gain, cos, sin, w)
 
 
-def flash_kernel(block_q, block_k, slen_ref, q_ref, k_ref, v_ref, o_ref, m_ref, l_ref, acc_ref):
+def flash_kernel(block_q, block_k, some, slen_ref, q_ref, k_ref, v_ref, o_ref, s_ref, m_ref, l_ref, p_ref, acc_ref):
     i = pl.program_id(0)
     heads, _, head = q_ref.shape
     rows = heads * block_q
+    pieces = rows // some
+    lanes = block_k // 128
     slen = slen_ref[0]
     scale = head ** -0.5 * LOG2E
-    q = q_ref[...].reshape(rows, head)
-    m_ref[...] = jnp.full_like(m_ref, -jnp.inf)
+    count = (i * block_q + block_q - 1) // block_k + 1
+
+    def cols(j):
+        return pl.ds(pl.multiple_of(j * block_k, block_k), block_k)
+
+    @pl.loop(0, count)
+    def _(j):
+        k = k_ref[0, cols(j), :]
+        s_ref[:, cols(j)] = lax.dot_general(q_ref[...].reshape(rows, head), k, (((1,), (1,)), ((), ())), preferred_element_type=F32)
+        edge = ((j + 1) * block_k > i * block_q) | ((j + 1) * block_k > slen)
+
+        @pl.when(edge)
+        def _():
+            @pl.loop(0, pieces)
+            def _(r):
+                here = pl.ds(pl.multiple_of(r * some, some), some)
+                q_pos = i * block_q + (r * some) % block_q + lax.broadcasted_iota(jnp.int32, (some, block_k), 0)
+                k_pos = j * block_k + lax.broadcasted_iota(jnp.int32, (some, block_k), 1)
+                s_ref[here, cols(j)] = jnp.where((k_pos <= q_pos) & (k_pos < slen), s_ref[here, cols(j)], -1e30)
+
+    tall = rows // heads
+
+    @pl.loop(0, heads)
+    def _(r):
+        here = pl.ds(pl.multiple_of(r * tall, tall), tall)
+
+        def more(j, top):
+            s = s_ref[here, cols(j)]
+            for n in range(lanes):
+                top = jnp.maximum(top, s[:, n * 128:(n + 1) * 128])
+            return top
+
+        top = lax.fori_loop(0, count, more, jnp.full((tall, 128), -jnp.inf, F32))
+        m_ref[here] = jnp.broadcast_to(jnp.max(top, axis=-1, keepdims=True), (tall, 128))
+
     l_ref[...] = jnp.zeros_like(l_ref)
     acc_ref[...] = jnp.zeros_like(acc_ref)
 
-    def step(j, masked):
-        start = pl.multiple_of(j * block_k, block_k)
-        k = k_ref[0, pl.ds(start, block_k), :]
-        v = v_ref[0, pl.ds(start, block_k), :]
-        s = lax.dot_general(q, k, (((1,), (1,)), ((), ())), preferred_element_type=F32)
-        if masked:
-            q_pos = i * block_q + lax.broadcasted_iota(jnp.int32, (block_q, block_k), 0)
-            k_pos = start + lax.broadcasted_iota(jnp.int32, (block_q, block_k), 1)
-            allowed = (k_pos <= q_pos) & (k_pos < slen)
-            s = jnp.where(allowed[None], s.reshape(heads, block_q, block_k), -1e30).reshape(rows, block_k)
-        m_old = m_ref[...]
-        m_new = jnp.maximum(m_old, jnp.max(s, axis=-1, keepdims=True))
-        alpha = jnp.exp2((m_old - m_new) * scale)
-        p = jnp.exp2((s - m_new) * scale)
-        l_ref[...] = l_ref[...] * alpha + jnp.sum(p, axis=-1, keepdims=True)
-        acc_ref[...] = acc_ref[...] * alpha + jnp.dot(p.astype(BF), v, preferred_element_type=F32)
-        m_ref[...] = m_new
-
-    count = (i * block_q + block_q - 1) // block_k + 1
-
     @pl.loop(0, count)
     def _(j):
-        edge = ((j + 1) * block_k > i * block_q) | ((j + 1) * block_k > slen)
-
-        @pl.when(edge)
-        def _():
-            step(j, True)
-
-        @pl.when(jnp.logical_not(edge))
-        def _():
-            step(j, False)
-
-    out = (acc_ref[...] / l_ref[...]).astype(BF)
+        @pl.loop(0, pieces, unroll=2)
+        def _(r):
+            here = pl.ds(pl.multiple_of(r * some, some), some)
+            s = s_ref[here, cols(j)]
+            m = m_ref[here]
+            total = l_ref[here]
+            for n in range(lanes):
+                w = jnp.exp2((s[:, n * 128:(n + 1) * 128] - m) * scale)
+                total = total + w
+                p_ref[here, n * 128:(n + 1) * 128] = w.astype(BF)
+            l_ref[here] = total
+
+        acc_ref[...] += jnp.dot(p_ref[...], v_ref[0, cols(j), :], preferred_element_type=F32)
+
     for h in range(heads):
-        o_ref[:, h * head:(h + 1) * head] = out[h * block_q:(h + 1) * block_q]
-
-
-def attend(slen, qkv, block_q=256, block_k=512):
+        here = slice(h * block_q, (h + 1) * block_q)
+        o_ref[:, h * head:(h + 1) * head] = (acc_ref[here] / jnp.sum(l_ref[here], axis=-1, keepdims=True)).astype(BF)
+
+
+def attend(slen, qkv, block_q=256, block_k=512, some=32):
     slots, rows, head = qkv.shape
     heads = slots - 2
+    tall = heads * block_q
     return pl.pallas_call(
-        functools.partial(flash_kernel, block_q, block_k),
+        functools.partial(flash_kernel, block_q, block_k, some),
         grid_spec=pltpu.PrefetchScalarGridSpec(
             num_scalar_prefetch=1,
             grid=(rows // block_q,),
@@ -136,34 +156,36 @@
             ],
             out_specs=pl.BlockSpec((block_q, heads * head), lambda i, _: (i, 0)),
             scratch_shapes=[
-                pltpu.VMEM((heads * block_q, 1), F32),
-                pltpu.VMEM((heads * block_q, 1), F32),
-                pltpu.VMEM((heads * block_q, head), F32),
+                pltpu.VMEM((tall, rows), F32),
+                pltpu.VMEM((tall, 128), F32),
+                pltpu.VMEM((tall, 128), F32),
+                pltpu.VMEM((tall, block_k), BF),
+                pltpu.VMEM((tall, head), F32),
             ],
         ),
         out_shape=jax.ShapeDtypeStruct((rows, heads * head), BF),
         cost_estimate=pl.CostEstimate(flops=3 * heads * rows * rows * head, bytes_accessed=2 * (2 * heads + 2) * rows * head, transcendentals=heads * rows * rows // 2),
-        name="attend",
+        name='attend',
     )(slen, qkv, qkv, qkv)
 
 
 MESH = pl.DeviceIdType.MESH
 CHUNKS = 4
-SUBS = 5
+SUBS = 13
 SLOTS = 2
 ACCS = 3
 TILE = 256
 TILE_OUT = 512
+OWNED = (10, 4, 4, 10)
 
 
 def layer_kernel(geo, ctx_hbm, x_hbm, y_hbm, gain_ref, wo_ref, wg_ref, wu_ref, wd_ref, out_hbm, full_hbm, hid_hbm,
-                 cx, hid, acc, slot, fin, res, rs_recv, rs_send, credit, ag_recv, ag_send, fin_sem, res_sem,
+                 cx, hid, acc, slots, fins, ress, rs_recv, rs_send, credit, ag_recv, ag_send, fin_sem, res_sem,
                  ctx_recv, ctx_send, load_sem, hid_sem):
     width, head_cols, step, dec, ff_tiles, tail = geo
     rows = step + dec
     sub = rows // SUBS
     total = CHUNKS * SUBS
-    half = width // 2
     out_tiles = width // TILE_OUT
     ticks = out_tiles + ff_tiles
     stride = ticks // SUBS
@@ -213,98 +235,130 @@
                 ctx_copy(chunk, t + hop, False).start()
 
     flows = []
-    for f in range(2):
-        place = last - t if f == 0 else t
-        nxt = t - 1 if f == 0 else t + 1
-        prv = t + 1 if f == 0 else t - 1
-        flows.append((f, place, nxt, prv, f * half))
-
-    def part(k, col):
+    for f, groups in enumerate(OWNED):
+        flows.append((f, sum(OWNED[:f]) * 128, groups * 128, max(f, last - f)))
+
+    def to(device):
+        return dict(device_id={'tp': device}, device_id_type=MESH)
+
+    def rows_of(k):
+        return pl.ds(pl.multiple_of(k * sub, 8), sub)
+
+    def part(f, k):
+        _, col, cols, _ = flows[f]
         first = pl.multiple_of((k % SUBS) * sub, 8)
-        return acc.at[(k // SUBS) % ACCS, pl.ds(first, sub), pl.ds(col, half)]
-
-    def out_rows(k, col):
-        return out_hbm.at[pl.ds(pl.multiple_of(k * sub, 8), sub), pl.ds(col, half)]
-
-    def rs_copy(f, k, col, device):
+        return acc.at[(k // SUBS) % ACCS, pl.ds(first, sub), pl.ds(col, cols)]
+
+    def out_part(f, k):
+        _, col, cols, _ = flows[f]
+        return out_hbm.at[rows_of(k), pl.ds(col, cols)]
+
+    def rs_copy(f, k, side, device):
         return pltpu.make_async_remote_copy(
-            src_ref=part(k, col), dst_ref=slot.at[f, k % SLOTS], send_sem=rs_send.at[f, k % SLOTS],
-            recv_sem=rs_recv.at[f, k % SLOTS], device_id={'tp': device}, device_id_type=MESH)
-
-    def ag_copy(f, k, col, device, first):
+            src_ref=part(f, k), dst_ref=slots[f].at[side, k % SLOTS], send_sem=rs_send.at[f, k % SLOTS],
+            recv_sem=rs_recv.at[f, side, k % SLOTS], **to(device))
+
+    def ag_copy(f, k, way, first):
         return pltpu.make_async_remote_copy(
-            src_ref=fin.at[f, k % SLOTS] if first else out_rows(k, col), dst_ref=out_rows(k, col), send_sem=ag_send.at[f, k],
-            recv_sem=ag_recv.at[f, k], device_id={'tp': device}, device_id_type=MESH)
-
-    def fin_copy(f, k, col):
-        return pltpu.make_async_copy(fin.at[f, k % SLOTS], out_rows(k, col), fin_sem.at[f, k % SLOTS])
-
-    def res_copy(f, k, col):
-        rows_k = hid_hbm.at[pl.ds(pl.multiple_of(k * sub, 8), sub), pl.ds(col, half)]
-        return pltpu.make_async_copy(rows_k, res.at[f, k % SLOTS], res_sem.at[f, k % SLOTS])
+            src_ref=fins[f].at[k % SLOTS] if first else out_part(f, k), dst_ref=out_part(f, k), send_sem=ag_send.at[f, way, k % SLOTS],
+            recv_sem=ag_recv.at[f, k], **to(t + 1 if way == 0 else t - 1))
+
+    def fin_copy(f, k):
+        return pltpu.make_async_copy(fins[f].at[k % SLOTS], out_part(f, k), fin_sem.at[f, k % SLOTS])
+
+    def res_copy(f, k):
+        _, col, cols, _ = flows[f]
+        return pltpu.make_async_copy(hid_hbm.at[rows_of(k), pl.ds(col, cols)], ress[f].at[k % SLOTS], res_sem.at[f, k % SLOTS])
+
+    def sides(f):
+        found = []
+        if f < last:
+            found.append((0, t > f, t - f, t + 1, t - 1, t < last))
+        if f > 0:
+            found.append((1, t < f, f - t, t - 1, t + 1, t > 0))
+        return found
+
+    def inside(k):
+        return (k >= 0) & (k < total)
 
     def collect(m):
-        for f, place, nxt, prv, col in flows:
-            k = m - place
-
-            @at((k >= 0) & (k < total) & (place > 0))
-            def _(f=f, place=place, nxt=nxt, prv=prv, col=col, k=k):
-                rs_copy(f, k, col, nxt).wait_recv()
-                mine = part(k, col)
-
-                @at(place < last)
+        for f, col, cols, peak in flows:
+            for side, there, dist, outer, inner, more in sides(f):
+                k = m - peak + dist
+
+                @at(inside(k) & there & more)
+                def _(f=f, side=side, outer=outer, inner=inner, k=k):
+                    rs_copy(f, k, side, inner).wait_recv()
+                    mine = part(f, k)
+                    mine[...] += slots[f][side, k % SLOTS]
+
+                    @at(k + SLOTS < total)
+                    def _():
+                        pl.semaphore_signal(credit.at[f], inc=1, **to(outer))
+
+            k = m - peak
+
+            @at(inside(k) & (t == f))
+            def _(f=f, k=k):
+                both = part(f, k)[...]
+                for side, _, _, outer, inner, _ in sides(f):
+                    rs_copy(f, k, side, inner).wait_recv()
+                    both = both + slots[f][side, k % SLOTS]
+                res_copy(f, k).wait()
+
+                @at(k >= SLOTS)
                 def _():
-                    mine[...] += slot[f, k % SLOTS]
-
-                @at(place == last)
+                    fin_copy(f, k - SLOTS).wait()
+                    for side, _, _, _, _, _ in sides(f):
+                        ag_copy(f, k - SLOTS, side, True).wait_send()
+
+                fins[f][k % SLOTS] = (ress[f][k % SLOTS].astype(F32) + both).astype(BF)
+
+                @at(k + SLOTS < total)
                 def _():
-                    res_copy(f, k, col).wait()
-
+                    for side, _, _, outer, _, _ in sides(f):
+                        pl.semaphore_signal(credit.at[f], inc=1, **to(outer))
+
+    def send(m):
+        for f, col, cols, peak in flows:
+            for side, there, dist, outer, inner, more in sides(f):
+                k = m - peak + dist
+
+                @at(inside(k) & there)
+                def _(f=f, side=side, inner=inner, k=k):
                     @at(k >= SLOTS)
                     def _():
-                        fin_copy(f, k, col).wait()
-                        ag_copy(f, k - SLOTS, col, prv, True).wait_send()
-
-                    both = mine[...] + slot[f, k % SLOTS]
-                    fin[f, k % SLOTS] = (res[f, k % SLOTS].astype(F32) + both).astype(BF)
-
-                @at(k + SLOTS < total)
-                def _():
-                    pl.semaphore_signal(credit.at[f], inc=1, device_id={'tp': prv}, device_id_type=MESH)
-
-    def send(m):
-        for f, place, nxt, prv, col in flows:
-            k = m - place
-
-            @at((k >= 0) & (k < total) & (place < last))
-            def _(f=f, nxt=nxt, col=col, k=k):
-                @at(k >= SLOTS)
-                def _():
-                    pl.semaphore_wait(credit.at[f], 1)
-                    rs_copy(f, k - SLOTS, col, nxt).wait_send()
-
-                rs_copy(f, k, col, nxt).start()
-
-            @at((k >= 0) & (k < total) & (place == last))
-            def _(f=f, prv=prv, col=col, k=k):
-                fin_copy(f, k, col).start()
-                ag_copy(f, k, col, prv, True).start()
-
-            ahead = k + 1
-
-            @at((ahead >= 0) & (ahead < total) & (place == last))
-            def _(f=f, col=col, ahead=ahead):
-                res_copy(f, ahead, col).start()
-
-            a = m - 2 * last + place
-
-            @at((a >= 0) & (a < total) & (place < last))
-            def _(f=f, place=place, prv=prv, col=col, a=a):
-                ag_copy(f, a, col, prv, False).wait_recv()
-
-                @at(place > 0)
-                def _():
-                    ag_copy(f, a, col, prv, False).start()
+                        pl.semaphore_wait(credit.at[f], 1)
+                        rs_copy(f, k - SLOTS, side, inner).wait_send()
+
+                    rs_copy(f, k, side, inner).start()
+
+            k = m - peak
+
+            @at(inside(k) & (t == f))
+            def _(f=f, k=k):
+                fin_copy(f, k).start()
+                for side, _, _, _, _, _ in sides(f):
+                    ag_copy(f, k, side, True).start()
+
+            @at(inside(k + 1) & (t == f))
+            def _(f=f, k=k):
+                res_copy(f, k + 1).start()
+
+            for side, there, dist, outer, inner, more in sides(f):
+                a = m - peak - dist
+
+                @at(inside(a) & there)
+                def _(f=f, side=side, more=more, a=a):
+                    ag_copy(f, a, side, False).wait_recv()
+
+                    @at(more)
+                    def _():
+                        @at(a >= SLOTS)
+                        def _():
+                            ag_copy(f, a - SLOTS, side, False).wait_send()
+
+                        ag_copy(f, a, side, False).start()
 
     @at((c == 0) & (j == 0))
     def _():
@@ -334,17 +388,16 @@
         ctx_first(1)
         ctx_hop(0, last)
 
-    for i in range(SUBS):
-        @at((c > 0) & (j == stride * i + 1))
-        def _(i=i):
-            collect(SUBS * (c - 1) + i)
-
-        @at((c > 0) & (j == stride * i + 2))
-        def _(i=i):
-            send(SUBS * (c - 1) + i)
+    @at((c > 0) & (j % stride == 0) & (j < stride * SUBS))
+    def _():
+        collect(SUBS * (c - 1) + j // stride)
+
+    @at((c > 0) & (j % stride == 1) & (j < stride * SUBS))
+    def _():
+        send(SUBS * (c - 1) + j // stride)
 
     for hop in range(1, last + 1):
-        @at((c + 1 < CHUNKS) & (j == stride * hop + 3))
+        @at((c + 1 < CHUNKS) & (j == ticks * hop // (last + 1) + 2))
         def _(hop=hop):
             ctx_hop(c + 1, hop)
             if hop == last:
@@ -382,7 +435,7 @@
         heads = head_cols // 128
         mixed = None
         for s in range(tp):
-            w = wo_ref[:heads, s].reshape(head_cols, TILE_OUT)
+            w = wo_ref[s].reshape(head_cols, TILE_OUT)
             one = jnp.dot(cx[:, s * head_cols:(s + 1) * head_cols], w, preferred_element_type=F32)
             mixed = one if mixed is None else mixed + one
         cols = pl.ds(pl.multiple_of(j * TILE_OUT, TILE_OUT), TILE_OUT)
@@ -426,23 +479,24 @@
             collect(m)
             send(m)
 
-        for f, place, nxt, prv, col in flows:
-            @at(place < last)
-            def _(f=f, nxt=nxt, col=col):
+        for f, col, cols, peak in flows:
+            for side, there, dist, outer, inner, more in sides(f):
+                @at(there)
+                def _(f=f, side=side, inner=inner, more=more):
+                    for k in range(total - SLOTS, total):
+                        rs_copy(f, k, side, inner).wait_send()
+
+                    @at(more)
+                    def _():
+                        for k in range(total - SLOTS, total):
+                            ag_copy(f, k, side, False).wait_send()
+
+            @at(t == f)
+            def _(f=f):
                 for k in range(total - SLOTS, total):
-                    rs_copy(f, k, col, nxt).wait_send()
-
-            @at(place == last)
-            def _(f=f, prv=prv, col=col):
-                for k in range(total - SLOTS, total):
-                    fin_copy(f, k, col).wait()
-                    ag_copy(f, k, col, prv, True).wait_send()
-
-            @at((place < last) & (place > 0))
-            def _(f=f, prv=prv, col=col):
-                @pl.loop(0, total)
-                def _(k):
-                    ag_copy(f, k, col, prv, False).wait_send()
+                    fin_copy(f, k).wait()
+                    for side, _, _, _, _, _ in sides(f):
+                        ag_copy(f, k, side, True).wait_send()
 
         for source in range(tp):
             @at((source <= t) & (t < last))
@@ -466,7 +520,6 @@
     out_tiles = width // TILE_OUT
     tp = width // head_cols
     pad = (rows + 15) // 16 * 16
-    half = width // 2
     sub = rows // SUBS
     total = CHUNKS * SUBS
     geo = (width, head_cols, step, dec, ff_tiles, tail)
@@ -484,7 +537,7 @@
         in_specs=[
             any_spec, any_spec, any_spec,
             pl.BlockSpec((1, width), lambda c, j: (0, 0)),
-            pl.BlockSpec((heads, tp, 128, TILE_OUT), lambda c, j: (0, 0, 0, jnp.minimum(j, out_tiles - 1))),
+            pl.BlockSpec((tp, heads, 128, TILE_OUT), lambda c, j: (0, 0, 0, jnp.minimum(j, out_tiles - 1))),
             pl.BlockSpec((1, width, TILE), lambda c, j: (0, 0, ff_index(j))),
             pl.BlockSpec((1, width, TILE), lambda c, j: (1, 0, ff_index(j))),
             pl.BlockSpec((TILE, width), lambda c, j: (ff_index(j), 0)),
@@ -499,16 +552,16 @@
             pltpu.VMEM((pad, width), BF),
             pltpu.VMEM((pad, width), BF),
             pltpu.VMEM((ACCS, pad, width), F32),
-            pltpu.VMEM((2, SLOTS, sub, half), F32),
-            pltpu.VMEM((2, SLOTS, sub, half), BF),
-            pltpu.VMEM((2, SLOTS, sub, half), BF),
-            pltpu.SemaphoreType.DMA((2, SLOTS)),
-            pltpu.SemaphoreType.DMA((2, SLOTS)),
-            pltpu.SemaphoreType.REGULAR((2,)),
-            pltpu.SemaphoreType.DMA((2, total)),
-            pltpu.SemaphoreType.DMA((2, total)),
-            pltpu.SemaphoreType.DMA((2, SLOTS)),
-            pltpu.SemaphoreType.DMA((2, SLOTS)),
+            [pltpu.VMEM((2, SLOTS, sub, groups * 128), F32) for groups in OWNED],
+            [pltpu.VMEM((SLOTS, sub, groups * 128), BF) for groups in OWNED],
+            [pltpu.VMEM((SLOTS, sub, groups * 128), BF) for groups in OWNED],
+            pltpu.SemaphoreType.DMA((tp, 2, SLOTS)),
+            pltpu.SemaphoreType.DMA((tp, SLOTS)),
+            pltpu.SemaphoreType.REGULAR((tp,)),
+            pltpu.SemaphoreType.DMA((tp, total)),
+            pltpu.SemaphoreType.DMA((tp, 2, SLOTS)),
+            pltpu.SemaphoreType.DMA((tp, SLOTS)),
+            pltpu.SemaphoreType.DMA((tp, SLOTS)),
             pltpu.SemaphoreType.DMA((CHUNKS, tp)),
             pltpu.SemaphoreType.DMA((CHUNKS, tp, 2)),
             pltpu.SemaphoreType.DMA((tp + 2,)),
@@ -520,36 +573,43 @@
     )(ctx, x, y, gain, w_full, w_gate_up, w_gate_up, w_down)[0]
 
 
-def decode_context(tokens, cache_lens, k_cache, v_cache, gain, w_qkv):
+def decode_local(tokens, cache_lens, k_cache, v_cache, gain, w_qkv):
     group_q = w_qkv.shape[2] - 2
     head_dim = w_qkv.shape[3]
     cache_local = k_cache.shape[1]
     cache_pos = lax.axis_index('tp') * cache_local + jnp.arange(cache_local)
     write_mask = (cache_pos[None, :] == cache_lens[:, None])[:, :, None, None]
-    allowed = (cache_pos[None, :] <= cache_lens[:, None])[:, None, None, :]
+    allowed = (cache_pos[None, :] <= cache_lens[:, None])[None, :, None, :]
     normed = rms_norm(tokens, gain)
     projected = jnp.einsum('bd,dkjh->bkjh', normed, w_qkv, preferred_element_type=F32)
     rotated = rope_rotate(projected[:, :, :group_q + 1], cache_lens)
-    local_qkv = jnp.concatenate([rotated, projected[:, :, group_q + 1:]], axis=2).astype(BF)
-    full_qkv = lax.all_gather(local_qkv, 'tp', axis=1, tiled=True)
-    key_now = jnp.where(write_mask, full_qkv[:, None, :, group_q], k_cache)
-    value_now = jnp.where(write_mask, full_qkv[:, None, :, group_q + 1], v_cache)
-    scores = jnp.einsum('bkgh,btkh->bkgt', full_qkv[:, :, :group_q], key_now, preferred_element_type=F32) * head_dim ** -0.5
+    local_qkv = jnp.concatenate([rotated, projected[:, :, group_q + 1:]], axis=2).astype(BF)[:, 0]
+    tp = k_cache.shape[2]
+    full_qkv = lax.all_to_all(jnp.broadcast_to(local_qkv, (tp,) + local_qkv.shape), 'tp', 0, 0)
+    key_now = jnp.where(write_mask, jnp.moveaxis(full_qkv[:, :, group_q], 0, 1)[:, None], k_cache)
+    value_now = jnp.where(write_mask, jnp.moveaxis(full_qkv[:, :, group_q + 1], 0, 1)[:, None], v_cache)
+    scores = jnp.einsum('kbgh,btkh->kbgt', full_qkv[:, :, :group_q], key_now, preferred_element_type=F32) * head_dim ** -0.5
     scores = jnp.where(allowed, scores, -1e30)
-    score_max = lax.pmax(jnp.max(scores, axis=-1, keepdims=True), 'tp')
-    weights = jnp.exp(scores - score_max)
-    sum_own = lax.psum_scatter(jnp.sum(weights, axis=-1), 'tp', scatter_dimension=1, tiled=True)
-    mixed_sum = jnp.einsum('bkgt,btkh->bkgh', weights.astype(BF), value_now, preferred_element_type=F32)
-    mixed_own = lax.psum_scatter(mixed_sum, 'tp', scatter_dimension=1, tiled=True)
-    context = (mixed_own / sum_own[..., None]).astype(BF)
-    return context, key_now, value_now
+    top = jnp.max(scores, axis=-1)
+    weights = jnp.exp(scores - top[..., None])
+    mixed = jnp.einsum('kbgt,btkh->kbgh', weights.astype(BF), value_now, preferred_element_type=F32)
+    stats = jnp.concatenate([top, jnp.sum(weights, axis=-1)], axis=-1)
+    stats = jnp.pad(stats, ((0, 0), (0, 0), (0, head_dim - stats.shape[-1])))
+    return jnp.concatenate([mixed, stats[:, :, None]], axis=2), key_now, value_now
+
+
+def decode_combine(mixed):
+    heads = mixed.shape[2] - 1
+    own = lax.all_to_all(mixed, 'tp', 0, 0)
+    top, total = own[:, :, heads, :heads], own[:, :, heads, heads:2 * heads]
+    factor = jnp.exp(top - jnp.max(top, axis=0))
+    return (jnp.sum(own[:, :, :heads] * factor[..., None], axis=0) / jnp.sum(total * factor, axis=0)[..., None]).astype(BF)
 
 
 def gather_w_out(w_out, mesh):
     index = lax.axis_index('pair') * mesh.shape['side'] + lax.axis_index('side')
     own = lax.dynamic_index_in_dim(w_out, jnp.minimum(index, w_out.shape[0] - 1), 0, keepdims=False)
-    column = lax.all_gather(own, 'tp')
-    return lax.all_gather(column, ('pair', 'side'))
+    return lax.all_gather(own, ('tp', 'pair', 'side'))
 
 
 def solution(mesh):
@@ -567,14 +627,15 @@
         cos, sin = rope_tables(positions, head)
         cos, sin = jnp.concatenate([cos, cos], -1), jnp.concatenate([-sin, sin], -1)
 
-        w_full = gather_w_out(w_out[0, 0], mesh)
+        w_full = gather_w_out(w_out[0, 0], mesh).reshape(tp, -1, head, width)
         gate_up = jnp.transpose(w_gate_up[0], (1, 0, 2))
 
-        dctx, key_now, value_now = decode_context(y_tok, c_len, k_cache[0], v_cache[0], attn_gain[0], w_qkv[0])
-        dctx = dctx.reshape(dctx.shape[0], group_q * head)
+        mixed, key_now, value_now = decode_local(y_tok, c_len, k_cache[0], v_cache[0], attn_gain[0], w_qkv[0])
 
         w_slots = jnp.transpose(w_qkv[0, :, 0], (1, 0, 2))
         qkv = project_qkv(x, attn_gain, cos, sin, w_slots)
+        mixed, qkv = lax.optimization_barrier((mixed, qkv))
+        dctx = decode_combine(mixed)
         ctx = attend(s_len, qkv)
 
         step, dec = seq_len // CHUNKS, y_tok.shape[0] // CHUNKS

time: 1150 us -> 1110 us (0.965)
  blocking collectives: 73.2 us -> 0 us
  Pallas kernels: 918 us -> 950 us
  waiting for transfers between devices: 20.5 us -> 7.04 us
  starting transfers between devices: 4.26 us -> 16.7 us
    pallas_call x1, Pallas kernels: 798 us -> 854 us  [layer_sums(): pl.pallas_call(functools.partial(layer_kernel, geo), grid=(CHUNKS, out_ti...]
    unnamed x1 -> x0, blocking collectives: 32.2 us -> none
    pallas_call x1, Pallas kernels: 91.1 us -> 67.1 us  [attend(): pl.pallas_call(functools.partial(flash_kernel, block_q, block_k, some), g...]
    pmax x1 -> x0, blocking collectives: 21.8 us -> none  [decode_context(): score_max = lax.pmax(jnp.max(scores, axis=-1, keepdims=True), 'tp')]
    all_gather x2 -> x1, waiting for transfers between devices: 20.5 us -> 0.01 us  [gather_w_out(): return lax.all_gather(own, ('tp', 'pair', 'side'))]
    all_gather x1 -> x0, blocking collectives: 19.2 us -> none  [decode_context(): full_qkv = lax.all_gather(local_qkv, 'tp', axis=1, tiled=True)]
    unnamed x10 -> x5, local copies, waits for them, and re-layouts: 45.7 us -> 45.1 us
  transfers between devices with their start and end apart: 5 -> 5, of which waited for: 1 -> 1; matrix products, arithmetic and copies ran while one was open for 9% -> 9% of each run, Pallas kernels for 10% -> 9%
where the time goes in v3:
time: 1110 us; the launch traced here: 1100 us
  Pallas kernels  950 us (86%)
  local copies, waits for them, and re-layouts  76.3 us (7%)
  other arithmetic  30.2 us (3%)
  starting transfers between devices  16.7 us (2%)
  between operations  14.9 us (1%)
    pallas_call x1, Pallas kernels, layer_sums(): pl.pallas_call(functools.partial(layer_kernel, geo), grid=(CHUNKS, out_ti...  854 us
    pallas_call x1, Pallas kernels, attend(): pl.pallas_call(functools.partial(flash_kernel, block_q, block_k, some), g...  67.1 us
    unnamed x5, local copies, waits for them, and re-layouts  45.1 us
    pallas_call x1, Pallas kernels, project_qkv(): pl.pallas_call(qkv_kernel, grid=(rows // rows_block,), in_specs=[pl.Block...  28.9 us
  transfers between devices with their start and end apart: 5, of which 1 were waited for; matrix products, arithmetic and copies ran while one was open for 9% of the time, Pallas kernels for 9%

profile of v3, /device:TPU:0, one launch (start us, length us, event | category | flops | bytes accessed | tf_op | source)
XLA Modules:
  0.0 1102.4 jit_solution(3129006934887490773)
XLA Ops:
  7.2 0.0 all-gather.3.cloned.1.call-start
  7.2 2.2 constant_dynamic-slice_fusion
  9.4 0.0 all-gather.3.cloned.1.call-update
  9.4 0.7 convert_element_type.51
  10.1 0.8 convert_reduce_fusion
  10.9 1.1 fusion.18
  12.0 0.1 multiply_cosine_fusion.1
  12.1 5.0 fusion.12
  17.2 0.1 subtract_convert_fusion
  17.3 0.1 maximum_bitcast_fusion
  17.4 0.8 broadcast_in_dim.76
  18.2 6.4 all-to-all-start
  25.2 3.7 fusion.21
  28.9 1.9 pad_maximum_fusion.1
  30.9 0.0 copy-start
  30.9 28.9 %project_qkv.1.q_ref.k_ref.v_ref = bf16[9,2048,128]{2,1,0:T(8,128)(2,1)} custom-call(bf16[2048,3584]{1,0:T(8,128)(2,1)} %bitcast.77, bf16[1,3584]{1,0:T(2,128)(2,1)} %gain_ref.2, f32[2048,128]{1,0:T(8,128)} %get-tuple-element.35.cos_ref, f32[2048,128]{1,0:T(8,128)} %get-tuple-element.36.sin_ref, bf16[9,3584,128]{2,1,0:T(8,128)(2,1)} %bitcast.67), custom_call_target="tpu_custom_call" | custom-call | flops 16911433728 | bytes 27656192 | tf_op jit(solution)/shard_map/project_qkv/pallas_call | solution.py:59
  59.8 0.0 copy-done.1
  59.8 0.1 broadcast_compare_fusion.1
  59.8 0.0 all-to-all-done
  59.9 0.0 copy-done
  60.0 5.7 bitcast_select_fusion
  65.7 1.3 fusion.32
  67.0 0.4 fusion.16
  67.4 0.1 select_maximum_fusion
  67.4 0.7 fusion.2
  68.2 0.9 pad_maximum_fusion.3
  69.1 1.6 multiply_bitcast_fusion
  70.6 9.6 copy.78
  80.3 5.1 all-to-all-start.2
  85.4 45.1 %copy.102 = bf16[1,3584,2,4736]{3,1,2,0:T(8,128)(2,1)} copy(bf16[1,3584,2,4736]{3,2,1,0:T(2,128)(2,1)} %param.22) | data formatting | bytes 135790592 | tf_op args[10]
  130.5 0.0 all-to-all-done.2
  130.5 5.1 all-to-all-start.1
  135.6 67.1 %attend.1 = bf16[2048,896]{1,0:T(8,128)(2,1)} custom-call(s32[1]{0:T(128)} %copy.104.slen_ref, bf16[9,2048,128]{2,1,0:T(8,128)(2,1)} %project_qkv.1.q_ref.k_ref.v_ref, bf16[9,2048,128]{2,1,0:T(8,128)(2,1)} %project_qkv.1.q_ref.k_ref.v_ref, bf16[9,2048,128]{2,1,0:T(8,128)(2,1)} %project_qkv.1.q_ref.k_ref.v_ref), custom_call_target="tpu_custom_call" | custom-call | flops 11274289152 | bytes 8388608 | tf_op jit(solution)/shard_map/attend/pallas_call | solution.py:147
  202.7 7.3 broadcast_select_fusion
  210.0 0.8 copy.103
  210.8 0.1 collective-permute-start
  210.9 0.0 all-to-all-done.1
  210.9 1.4 fusion.31
  212.4 1.3 fusion.15
  213.7 0.1 divide_convert_fusion
  213.8 0.1 convert_element_type.55
  213.9 4.2 pad_maximum_fusion.ctx_hbm
  218.1 7.0 collective-permute-done
  225.1 1.3 slice_bitcast_fusion
  226.4 0.0 all-gather.3.cloned.1.call-done
  226.4 854.3 %layer_sums.1 = (bf16[2080,3584]{1,0:T(8,128)(2,1)}, bf16[4,4,520,896]{3,2,1,0:T(8,128)(2,1)}, bf16[2080,3584]{1,0:T(8,128)(2,1)}) custom-call(bf16[4,520,896]{2,1,0:T(8,128)(2,1)} %pad_maximum_fusion.ctx_hbm, bf16[2048,3584]{1,0:T(8,128)(2,1)} %bitcast.78, bf16[32,3584]{1,0:T(8,128)(2,1)} %y_hbm.1, bf16[1,3584]{1,0:T(2,128)(2,1)} %gain_ref.3, ...), custom_call_target="tpu_custom_call" | custom-call | flops 265268756480 | bytes 510132224 | tf_op jit(solution)/shard_map/layer_sums/pallas_call | solution.py:534
  1080.7 13.3 %slice.69 = bf16[4,512,3584]{2,1,0:T(8,128)(2,1)} slice(bf16[4,520,3584]{2,1,0:T(8,128)(2,1)} %bitcast.64), slice={[0:4], [0:512], [0:3584]} | slice | bytes 29360128 | tf_op jit(solution)/shard_map/slice | solution.py:645
  1094.0 1.6 slice_bitcast_fusion.2
  (14 shorter events, 0.1 us)
Async XLA Ops:
  7.2 219.2 %all-gather.3.cloned.1.call-start = ((), (), s32[]{:S(2)}) async-start(), calls=%async_computation.3 | async-start | bytes 30277632 | tf_op jit(solution)/shard_map/all_gather | solution.py:612
  18.2 41.7 %all-to-all-start = ((bf16[4,32,9,128]{3,1,2,0:T(8,128)(2,1)}), bf16[4,32,9,128]{3,1,2,0:T(8,128)(2,1)S(1)}, u32[]{:S(2)}, u32[]{:S(2)}) async-start(bf16[4,32,9,128]{3,1,2,0:T(8,128)(2,1)} %broadcast_in_dim.76), calls=%async_computation | async-start | bytes 589824 | tf_op jit(solution)/shard_map/all_to_all | solution.py:588
  30.9 28.9 %copy-start.1 = (s32[32]{0:T(128)S(1)}, s32[32]{0:T(128)}, u32[]{:S(2)}) copy-start(s32[32]{0:T(128)} %param.15) | copy-start | bytes 388
  30.9 29.1 %copy-start = (bf16[1,32,64,4,128]{4,3,2,1,0:T(4,128)(2,1)S(1)}, bf16[1,32,64,4,128]{4,3,2,1,0:T(4,128)(2,1)}, u32[]{:S(2)}) copy-start(bf16[1,32,64,4,128]{4,3,2,1,0:T(4,128)(2,1)} %param.17) | copy-start | bytes 6291460
  80.3 50.2 %all-to-all-start.2 = ((bf16[2,2048,1,128]{3,0,2,1:T(2,128)(2,1)}), bf16[2,2048,1,128]{3,0,2,1:T(2,128)(2,1)S(1)}, u32[]{:S(2)}, u32[]{:S(2)}) async-start(bf16[2,2048,1,128]{3,0,2,1:T(2,128)(2,1)} %copy.78), calls=%async_computation.2 | async-start | bytes 2097152 | tf_op jit(solution)/shard_map/all_to_all | solution.py:649
  130.5 80.4 %all-to-all-start.1 = ((f32[4,32,8,128]{3,2,1,0:T(8,128)}), f32[4,32,8,128]{3,2,1,0:T(8,128)}, u32[]{:S(2)}, u32[]{:S(2)}) async-start(f32[4,32,8,128]{3,2,1,0:T(8,128)} %pad_maximum_fusion.3), calls=%async_computation.1 | async-start | bytes 1048576 | tf_op jit(solution)/shard_map/all_to_all | solution.py:603
  210.8 14.3 %collective-permute-start = (bf16[2,512,4,128]{3,2,1,0:T(4,128)(2,1)S(1)}, bf16[2,512,4,128]{3,2,1,0:T(4,128)(2,1)S(1)}, u32[]{:S(2)}, u32[]{:S(2)}) collective-permute-start(bf16[2,512,4,128]{3,2,1,0:T(4,128)(2,1)S(1)} %bitcast.70), channel_id=1, source_target_pairs={{0,1},{1,2},{2,3},{3,0},{4,5},{5,6},{6,7},{7,4},{8,9},{9,10},{10,1... | collective-permute-start | bytes 3145736 | tf_op jit(solution)/shard_map/ppermute | solution.py:650
Sparse Core Ops, SparseCore 0:
  10.9 209.5 all-gather.2

commit v4 on v3

--- a/solution.py
+++ b/solution.py
@@ -73,8 +73,84 @@
     )(x, gain, cos, sin, w)
 
 
-def flash_kernel(block_q, block_k, some, slen_ref, q_ref, k_ref, v_ref, o_ref, s_ref, m_ref, l_ref, p_ref, acc_ref):
-    i = pl.program_id(0)
+MESH = pl.DeviceIdType.MESH
+
+
+def to(device):
+    return dict(device_id={'tp': device}, device_id_type=MESH)
+
+
+def meet_neighbours(t, last):
+    barrier = pltpu.get_barrier_semaphore()
+
+    @pl.when(t > 0)
+    def _():
+        pl.semaphore_signal(barrier, inc=1, **to(t - 1))
+
+    @pl.when(t < last)
+    def _():
+        pl.semaphore_signal(barrier, inc=1, **to(t + 1))
+
+    @pl.when((t > 0) & (t < last))
+    def _():
+        pl.semaphore_wait(barrier, 2)
+
+    @pl.when((t == 0) | (t == last))
+    def _():
+        pl.semaphore_wait(barrier, 1)
+
+
+class Spread:
+    def __init__(self, t, last, own, place, send_sem, recv_sem):
+        self.t, self.last, self.own, self.place, self.send_sem, self.recv_sem = t, last, own, place, send_sem, recv_sem
+
+    def copy(self, source, way, first=False):
+        return pltpu.make_async_remote_copy(
+            src_ref=self.own if first else self.place(source), dst_ref=self.place(source), send_sem=self.send_sem(source, way),
+            recv_sem=self.recv_sem(source), **to(self.t + 1 if way == 0 else self.t - 1))
+
+    def start(self):
+        @pl.when(self.t < self.last)
+        def _():
+            self.copy(self.t, 0, True).start()
+
+        @pl.when(self.t > 0)
+        def _():
+            self.copy(self.t, 1, True).start()
+
+    def hop(self, n):
+        t, last = self.t, self.last
+
+        @pl.when(t >= n)
+        def _():
+            self.copy(t - n, 0).wait_recv()
+
+            @pl.when(t < last)
+            def _():
+                self.copy(t - n, 0).start()
+
+        @pl.when(t + n <= last)
+        def _():
+            self.copy(t + n, 1).wait_recv()
+
+            @pl.when(t > 0)
+            def _():
+                self.copy(t + n, 1).start()
+
+    def finish(self):
+        for source in range(self.last + 1):
+            @pl.when((source <= self.t) & (self.t < self.last))
+            def _(source=source):
+                self.copy(source, 0).wait_send()
+
+            @pl.when((source >= self.t) & (self.t > 0))
+            def _(source=source):
+                self.copy(source, 1).wait_send()
+
+
+def flash_kernel(block_q, block_k, some, base, slen_ref, q_ref, k_ref, v_ref, *refs):
+    o_ref, s_ref, m_ref, l_ref, p_ref, acc_ref = refs[-6:]
+    i = pl.program_id(0) + base
     heads, _, head = q_ref.shape
     rows = heads * block_q
     pieces = rows // some
@@ -90,7 +166,7 @@
     def _(j):
         k = k_ref[0, cols(j), :]
         s_ref[:, cols(j)] = lax.dot_general(q_ref[...].reshape(rows, head), k, (((1,), (1,)), ((), ())), preferred_element_type=F32)
-        edge = ((j + 1) * block_k > i * block_q) | ((j + 1) * block_k > slen)
+        edge = ((j + 1) * block_k > i * block_q) | ((j + 1) * block_k > k_ref.shape[1] // 2)
 
         @pl.when(edge)
         def _():
@@ -140,21 +216,25 @@
         o_ref[:, h * head:(h + 1) * head] = (acc_ref[here] / jnp.sum(l_ref[here], axis=-1, keepdims=True)).astype(BF)
 
 
-def attend(slen, qkv, block_q=256, block_k=512, some=32):
+def attend(slen, qkv, first, count, total, into=None, block_q=256, block_k=512, some=32):
     slots, rows, head = qkv.shape
     heads = slots - 2
     tall = heads * block_q
+    base = first // block_q
+    place = 0 if into is None else (total - count) // block_q
+    more = [] if into is None else [into]
+    share = (first + count) ** 2 - first ** 2
     return pl.pallas_call(
-        functools.partial(flash_kernel, block_q, block_k, some),
+        functools.partial(flash_kernel, block_q, block_k, some, base),
         grid_spec=pltpu.PrefetchScalarGridSpec(
             num_scalar_prefetch=1,
-            grid=(rows // block_q,),
+            grid=(count // block_q,),
             in_specs=[
-                pl.BlockSpec((heads, block_q, head), lambda i, _: (0, i, 0)),
+                pl.BlockSpec((heads, block_q, head), lambda i, _: (0, i + base, 0)),
                 pl.BlockSpec((1, rows, head), lambda i, _: (heads, 0, 0)),
                 pl.BlockSpec((1, rows, head), lambda i, _: (heads + 1, 0, 0)),
-            ],
-            out_specs=pl.BlockSpec((block_q, heads * head), lambda i, _: (i, 0)),
+            ] + [pl.BlockSpec(memory_space=pl.ANY) for _ in more],
+            out_specs=pl.BlockSpec((block_q, heads * head), lambda i, _: (i + place, 0)),
             scratch_shapes=[
                 pltpu.VMEM((tall, rows), F32),
                 pltpu.VMEM((tall, 128), F32),
@@ -163,13 +243,13 @@
                 pltpu.VMEM((tall, head), F32),
             ],
         ),
-        out_shape=jax.ShapeDtypeStruct((rows, heads * head), BF),
-        cost_estimate=pl.CostEstimate(flops=3 * heads * rows * rows * head, bytes_accessed=2 * (2 * heads + 2) * rows * head, transcendentals=heads * rows * rows // 2),
+        out_shape=jax.ShapeDtypeStruct((total, heads * head), BF),
+        input_output_aliases={4: 0} if more else {},
+        cost_estimate=pl.CostEstimate(flops=3 * heads * share * head, bytes_accessed=2 * (2 * heads + 2) * count * head, transcendentals=heads * share // 2),
         name='attend',
-    )(slen, qkv, qkv, qkv)
-
-
-MESH = pl.DeviceIdType.MESH
+    )(slen, qkv, qkv, qkv, *more)
+
+
 CHUNKS = 4
 SUBS = 13
 SLOTS = 2
@@ -179,7 +259,7 @@
 OWNED = (10, 4, 4, 10)
 
 
-def layer_kernel(geo, ctx_hbm, x_hbm, y_hbm, gain_ref, wo_ref, wg_ref, wu_ref, wd_ref, out_hbm, full_hbm, hid_hbm,
+def layer_kernel(geo, ctx_hbm, dctx_hbm, mine_hbm, right_hbm, left_hbm, x_hbm, y_hbm, gain_ref, wo_ref, wg_ref, wu_ref, wd_ref, out_hbm, full_hbm, dfull_hbm, hid_hbm,
                  cx, hid, acc, slots, fins, ress, rs_recv, rs_send, credit, ag_recv, ag_send, fin_sem, res_sem,
                  ctx_recv, ctx_send, load_sem, hid_sem):
     width, head_cols, step, dec, ff_tiles, tail = geo
@@ -197,49 +277,22 @@
     def at(cond):
         return pl.when(cond)
 
-    def ctx_copy(chunk, source, right):
-        src = full_hbm.at[source, chunk]
-        return pltpu.make_async_remote_copy(
-            src_ref=src, dst_ref=full_hbm.at[source, chunk], send_sem=ctx_send.at[chunk, source, 0 if right else 1],
-            recv_sem=ctx_recv.at[chunk, source], device_id={'tp': t + 1 if right else t - 1}, device_id_type=MESH)
-
-    def ctx_first(chunk):
-        def own(right):
-            return pltpu.make_async_remote_copy(
-                src_ref=ctx_hbm.at[chunk], dst_ref=full_hbm.at[t, chunk], send_sem=ctx_send.at[chunk, t, 0 if right else 1],
-                recv_sem=ctx_recv.at[chunk, t], device_id={'tp': t + 1 if right else t - 1}, device_id_type=MESH)
-
-        @at(t < last)
-        def _():
-            own(True).start()
-
-        @at(t > 0)
-        def _():
-            own(False).start()
-
-    def ctx_hop(chunk, hop):
-        @at(t >= hop)
-        def _():
-            ctx_copy(chunk, t - hop, True).wait_recv()
-
-            @at(t < last)
-            def _():
-                ctx_copy(chunk, t - hop, True).start()
-
-        @at(t + hop <= last)
-        def _():
-            ctx_copy(chunk, t + hop, False).wait_recv()
-
-            @at(t > 0)
-            def _():
-                ctx_copy(chunk, t + hop, False).start()
+    def step_rows(chunk):
+        return pl.ds(pl.multiple_of(chunk * step, 8), step)
+
+    def dec_rows(chunk):
+        return pl.ds(pl.multiple_of(chunk * dec, 8), dec)
+
+    def spread(chunk):
+        return Spread(t, last, ctx_hbm.at[step_rows(chunk - 1)], lambda source: full_hbm.at[source, chunk - 1],
+                      lambda source, way: ctx_send.at[chunk, source, way], lambda source: ctx_recv.at[chunk, source])
+
+    tokens = Spread(t, last, dctx_hbm, lambda source: dfull_hbm.at[source],
+                    lambda source, way: ctx_send.at[0, source, way], lambda source: ctx_recv.at[0, source])
 
     flows = []
     for f, groups in enumerate(OWNED):
         flows.append((f, sum(OWNED[:f]) * 128, groups * 128, max(f, last - f)))
-
-    def to(device):
-        return dict(device_id={'tp': device}, device_id_type=MESH)
 
     def rows_of(k):
         return pl.ds(pl.multiple_of(k * sub, 8), sub)
@@ -333,18 +386,20 @@
 
                     rs_copy(f, k, side, inner).start()
 
+        for f, col, cols, peak in flows:
             k = m - peak
 
             @at(inside(k) & (t == f))
             def _(f=f, k=k):
-                fin_copy(f, k).start()
                 for side, _, _, _, _, _ in sides(f):
                     ag_copy(f, k, side, True).start()
+                fin_copy(f, k).start()
 
             @at(inside(k + 1) & (t == f))
             def _(f=f, k=k):
                 res_copy(f, k + 1).start()
 
+        for f, col, cols, peak in flows:
             for side, there, dist, outer, inner, more in sides(f):
                 a = m - peak - dist
 
@@ -362,71 +417,68 @@
 
     @at((c == 0) & (j == 0))
     def _():
-        barrier = pltpu.get_barrier_semaphore()
-
-        @at(t > 0)
-        def _():
-            pl.semaphore_signal(barrier, inc=1, device_id={'tp': t - 1}, device_id_type=MESH)
-
-        @at(t < last)
-        def _():
-            pl.semaphore_signal(barrier, inc=1, device_id={'tp': t + 1}, device_id_type=MESH)
-
-        @at((t > 0) & (t < last))
-        def _():
-            pl.semaphore_wait(barrier, 2)
-
-        @at((t == 0) | (t == last))
-        def _():
-            pl.semaphore_wait(barrier, 1)
-
-        ctx_first(0)
+        meet_neighbours(t, last)
+        tokens.start()
+        spread(1).start()
         cx[...] = jnp.zeros_like(cx)
         hid[...] = jnp.zeros_like(hid)
-        for hop in range(1, last):
-            ctx_hop(0, hop)
-        ctx_first(1)
-        ctx_hop(0, last)
+        for n in range(1, last + 1):
+            tokens.hop(n)
 
     @at((c > 0) & (j % stride == 0) & (j < stride * SUBS))
     def _():
-        collect(SUBS * (c - 1) + j // stride)
-
-    @at((c > 0) & (j % stride == 1) & (j < stride * SUBS))
-    def _():
-        send(SUBS * (c - 1) + j // stride)
-
-    for hop in range(1, last + 1):
-        @at((c + 1 < CHUNKS) & (j == ticks * hop // (last + 1) + 2))
-        def _(hop=hop):
-            ctx_hop(c + 1, hop)
-            if hop == last:
+        period = SUBS * (c - 1) + j // stride
+        collect(period)
+        send(period)
+
+    for n in range(1, last + 1):
+        @at((c + 1 < CHUNKS) & (j == ticks * n // (last + 1) + 2))
+        def _(n=n):
+            spread(c + 1).hop(n)
+            if n == last:
                 @at(c + 2 < CHUNKS)
                 def _():
-                    ctx_first(c + 2)
+                    spread(c + 2).start()
 
     @at(j == 0)
     def _():
         loads = [
-            pltpu.make_async_copy(x_hbm.at[pl.ds(pl.multiple_of(c * step, 8), step)], hid.at[pl.ds(0, step)], load_sem.at[tp]),
-            pltpu.make_async_copy(y_hbm.at[pl.ds(pl.multiple_of(c * dec, 8), dec)], hid.at[pl.ds(step, dec)], load_sem.at[tp + 1]),
+            pltpu.make_async_copy(x_hbm.at[step_rows(c)], hid.at[pl.ds(0, step)], load_sem.at[2 * tp]),
+            pltpu.make_async_copy(y_hbm.at[dec_rows(c)], hid.at[pl.ds(step, dec)], load_sem.at[2 * tp + 1]),
         ]
         for copy in loads:
             copy.start()
         for s in range(tp):
-            where = cx.at[pl.ds(0, rows), pl.ds(s * head_cols, head_cols)]
+            head_range = pl.ds(s * head_cols, head_cols)
+            where, tail_rows = cx.at[pl.ds(0, step), head_range], cx.at[pl.ds(step, dec), head_range]
+
+            for device in range(tp):
+                piece = mine_hbm if device == s else right_hbm[device - s - 1] if device > s else left_hbm[s - device - 1]
+
+                @at((c == 0) & (t == device))
+                def _(s=s, where=where, piece=piece):
+                    pltpu.make_async_copy(piece, where, load_sem.at[s]).start()
+
+            @at((c > 0) & (t == s))
+            def _(s=s, where=where):
+                pltpu.make_async_copy(ctx_hbm.at[step_rows(c - 1)], where, load_sem.at[s]).start()
+
+            @at((c > 0) & (t != s))
+            def _(s=s, where=where):
+                pltpu.make_async_copy(full_hbm.at[s, c - 1], where, load_sem.at[s]).start()
 
             @at(t == s)
-            def _(s=s, where=where):
-                pltpu.make_async_copy(ctx_hbm.at[c], where, load_sem.at[s]).start()
+            def _(s=s, tail_rows=tail_rows):
+                pltpu.make_async_copy(dctx_hbm.at[dec_rows(c)], tail_rows, load_sem.at[tp + s]).start()
 
             @at(t != s)
-            def _(s=s, where=where):
-                pltpu.make_async_copy(full_hbm.at[s, c], where, load_sem.at[s]).start()
+            def _(s=s, tail_rows=tail_rows):
+                pltpu.make_async_copy(dfull_hbm.at[s, dec_rows(c)], tail_rows, load_sem.at[tp + s]).start()
 
         for s in range(tp):
-            where = cx.at[pl.ds(0, rows), pl.ds(s * head_cols, head_cols)]
-            pltpu.make_async_copy(ctx_hbm.at[c], where, load_sem.at[s]).wait()
+            head_range = pl.ds(s * head_cols, head_cols)
+            pltpu.make_async_copy(mine_hbm, cx.at[pl.ds(0, step), head_range], load_sem.at[s]).wait()
+            pltpu.make_async_copy(dctx_hbm.at[dec_rows(c)], cx.at[pl.ds(step, dec), head_range], load_sem.at[tp + s]).wait()
         for copy in loads:
             copy.wait()
 
@@ -498,22 +550,16 @@
                     for side, _, _, _, _, _ in sides(f):
                         ag_copy(f, k, side, True).wait_send()
 
-        for source in range(tp):
-            @at((source <= t) & (t < last))
-            def _(source=source):
-                for chunk in range(CHUNKS):
-                    ctx_copy(chunk, source, True).wait_send()
-
-            @at((source >= t) & (t > 0))
-            def _(source=source):
-                for chunk in range(CHUNKS):
-                    ctx_copy(chunk, source, False).wait_send()
-
-
-def layer_sums(ctx, x, y, gain, w_full, w_gate_up, w_down):
-    _, rows, head_cols = ctx.shape
+        tokens.finish()
+        for chunk in range(1, CHUNKS):
+            spread(chunk).finish()
+
+
+def layer_sums(ctx, dctx, mine, right, left, x, y, gain, w_full, w_gate_up, w_down):
+    head_cols = ctx.shape[1]
     seq, width = x.shape
     step, dec = seq // CHUNKS, y.shape[0] // CHUNKS
+    rows = step + dec
     ff = w_down.shape[0]
     ff_tiles = pl.cdiv(ff, TILE)
     tail = ff - (ff_tiles - 1) * TILE
@@ -535,17 +581,18 @@
         functools.partial(layer_kernel, geo),
         grid=(CHUNKS, out_tiles + ff_tiles),
         in_specs=[
-            any_spec, any_spec, any_spec,
+            any_spec, any_spec, any_spec, [any_spec] * (tp - 1), [any_spec] * (tp - 1), any_spec, any_spec,
             pl.BlockSpec((1, width), lambda c, j: (0, 0)),
             pl.BlockSpec((tp, heads, 128, TILE_OUT), lambda c, j: (0, 0, 0, jnp.minimum(j, out_tiles - 1))),
             pl.BlockSpec((1, width, TILE), lambda c, j: (0, 0, ff_index(j))),
             pl.BlockSpec((1, width, TILE), lambda c, j: (1, 0, ff_index(j))),
             pl.BlockSpec((TILE, width), lambda c, j: (ff_index(j), 0)),
         ],
-        out_specs=[any_spec, any_spec, any_spec],
+        out_specs=[any_spec, any_spec, any_spec, any_spec],
         out_shape=[
             jax.ShapeDtypeStruct((CHUNKS * rows, width), BF),
-            jax.ShapeDtypeStruct((tp, CHUNKS, rows, head_cols), BF),
+            jax.ShapeDtypeStruct((tp, CHUNKS - 1, step, head_cols), BF),
+            jax.ShapeDtypeStruct((tp,) + dctx.shape, BF),
             jax.ShapeDtypeStruct((CHUNKS * rows, width), BF),
         ],
         scratch_shapes=[
@@ -564,13 +611,13 @@
             pltpu.SemaphoreType.DMA((tp, SLOTS)),
             pltpu.SemaphoreType.DMA((CHUNKS, tp)),
             pltpu.SemaphoreType.DMA((CHUNKS, tp, 2)),
-            pltpu.SemaphoreType.DMA((tp + 2,)),
+            pltpu.SemaphoreType.DMA((2 * tp + 2,)),
             pltpu.SemaphoreType.DMA(()),
         ],
         compiler_params=pltpu.CompilerParams(collective_id=0, has_side_effects=True, vmem_limit_bytes=67000000, dimension_semantics=('arbitrary', 'arbitrary')),
         cost_estimate=pl.CostEstimate(flops=flops, bytes_accessed=moved, transcendentals=0),
         name='layer_sums',
-    )(ctx, x, y, gain, w_full, w_gate_up, w_gate_up, w_down)[0]
+    )(ctx, dctx, mine, right, left, x, y, gain, w_full, w_gate_up, w_gate_up, w_down)[0]
 
 
 def decode_local(tokens, cache_lens, k_cache, v_cache, gain, w_qkv):
@@ -606,6 +653,11 @@
     return (jnp.sum(own[:, :, :heads] * factor[..., None], axis=0) / jnp.sum(total * factor, axis=0)[..., None]).astype(BF)
 
 
+def pass_on(right, left, hop, tp):
+    return (lax.ppermute(right, 'tp', [(place, place + 1) for place in range(hop - 1, tp - 1)]),
+            lax.ppermute(left, 'tp', [(place, place - 1) for place in range(tp - hop, 0, -1)]))
+
+
 def gather_w_out(w_out, mesh):
     index = lax.axis_index('pair') * mesh.shape['side'] + lax.axis_index('side')
     own = lax.dynamic_index_in_dim(w_out, jnp.minimum(index, w_out.shape[0] - 1), 0, keepdims=False)
@@ -634,13 +686,21 @@
 
         w_slots = jnp.transpose(w_qkv[0, :, 0], (1, 0, 2))
         qkv = project_qkv(x, attn_gain, cos, sin, w_slots)
-        mixed, qkv = lax.optimization_barrier((mixed, qkv))
+        step, dec = seq_len // CHUNKS, y_tok.shape[0] // CHUNKS
+        rest = seq_len - step
+        mine = attend(s_len, qkv, 0, step, step)
+        moved = [pass_on(mine, mine, 1, tp)]
+        mixed, qkv, mine = lax.optimization_barrier((mixed, qkv, mine))
         dctx = decode_combine(mixed)
-        ctx = attend(s_len, qkv)
-
-        step, dec = seq_len // CHUNKS, y_tok.shape[0] // CHUNKS
-        ctx_all = jnp.concatenate([ctx.reshape(CHUNKS, step, -1), dctx.reshape(CHUNKS, dec, -1)], axis=1)
-        done = layer_sums(ctx_all, x, y_tok, mlp_gain, w_full, gate_up, w_down[0])
+        ctx = attend(s_len, qkv, step, rest - step, rest)
+        for hop in range(2, tp):
+            pair = pass_on(*moved[-1], hop, tp)
+            if hop < tp - 1:
+                ctx, pair = lax.optimization_barrier((ctx, pair))
+            moved.append(pair)
+        ctx = attend(s_len, qkv, rest, step, rest, ctx)
+
+        done = layer_sums(ctx, dctx.reshape(-1, ctx.shape[1]), mine, [r for r, _ in moved], [l for _, l in moved], x, y_tok, mlp_gain, w_full, gate_up, w_down[0])
         done = done.reshape(CHUNKS, step + dec, width)
         hidden = done[:, :step].reshape(seq_len, width)
         tokens = done[:, step:].reshape(CHUNKS * dec, width)

time: 1110 us -> 1050 us (0.946)
  Pallas kernels: 950 us -> 856 us
  waiting for transfers between devices: 7.04 us -> 41.5 us
  starting transfers between devices: 16.7 us -> 28.6 us
    pallas_call x1, Pallas kernels: 854 us -> 754 us  [layer_sums(): pl.pallas_call(functools.partial(layer_kernel, geo), grid=(CHUNKS, out_ti...]
    ppermute x0 -> x6, waiting for transfers between devices: none -> 34.3 us  [the longest x3 34.3 us: pass_on(): lax.ppermute(left, 'tp', [(place, place - 1) for place in range(tp - hop,...]
    ppermute x0 -> x6, starting transfers between devices: none -> 12.5 us  [the longest x3 8.23 us: pass_on(): lax.ppermute(right, 'tp', [(place, place + 1) for place in range(hop - 1,...]
    pallas_call x1 -> x3, Pallas kernels: 67.1 us -> 73.1 us  [attend(): pl.pallas_call(functools.partial(flash_kernel, block_q, block_k, some, ba...]
    unnamed x5 -> x14, local copies, waits for them, and re-layouts: 45.1 us -> 46.7 us
  transfers between devices with their start and end apart: 5 -> 11, of which waited for: 1 -> 3; matrix products, arithmetic and copies ran while one was open for 9% -> 8% of each run, Pallas kernels for 9% -> 10%
where the time goes in v4:
time: 1050 us
  Pallas kernels  856 us (82%)
  local copies, waits for them, and re-layouts  77.4 us (7%)
  waiting for transfers between devices  41.5 us (4%)
  starting transfers between devices  28.6 us (3%)
  other arithmetic  22.6 us (2%)
  between operations  15 us (1%)
    pallas_call x1, Pallas kernels, layer_sums(): pl.pallas_call(functools.partial(layer_kernel, geo), grid=(CHUNKS, out_ti...  754 us
    pallas_call x3, Pallas kernels, attend(): pl.pallas_call(functools.partial(flash_kernel, block_q, block_k, some, ba...  73.1 us
    unnamed x14, local copies, waits for them, and re-layouts  46.7 us
    ppermute x3, waiting for transfers between devices, pass_on(): lax.ppermute(left, 'tp', [(place, place - 1) for place in range(tp - hop,...  34.3 us
    pallas_call x1, Pallas kernels, project_qkv(): pl.pallas_call(qkv_kernel, grid=(rows // rows_block,), in_specs=[pl.Block...  28.8 us
  transfers between devices with their start and end apart: 11, of which 3 were waited for; matrix products, arithmetic and copies ran while one was open for 8% of the time, Pallas kernels for 10%

profile of v4, /device:TPU:0, one launch (start us, length us, event | category | flops | bytes accessed | tf_op | source)
XLA Modules:
  0.0 1047.8 jit_solution(16492253323692504549)
XLA Ops:
  7.2 0.0 all-gather.3.cloned.1.call-start
  7.3 2.2 constant_dynamic-slice_fusion
  9.5 0.0 all-gather.3.cloned.1.call-update
  9.6 0.2 fusion.18
  9.8 0.1 multiply_cosine_fusion.1
  9.9 4.9 fusion.12
  14.8 0.1 subtract_convert_fusion
  15.0 0.1 maximum_bitcast_fusion
  15.1 0.8 broadcast_in_dim.76
  15.8 6.4 all-to-all-start
  22.2 3.7 fusion.21
  25.9 1.9 pad_maximum_fusion
  27.9 28.8 %project_qkv.1.q_ref.k_ref.v_ref = bf16[9,2048,128]{2,1,0:T(8,128)(2,1)} custom-call(bf16[2048,3584]{1,0:T(8,128)(2,1)} %bitcast.80, bf16[1,3584]{1,0:T(2,128)(2,1)} %gain_ref.2, f32[2048,128]{1,0:T(8,128)} %get-tuple-element.43.cos_ref, f32[2048,128]{1,0:T(8,128)} %get-tuple-element.44.sin_ref, bf16[9,3584,128]{2,1,0:T(8,128)(2,1)} %bitcast.70), custom_call_target="tpu_custom_call" | custom-call | flops 16911433728 | bytes 27656192 | tf_op jit(solution)/shard_map/project_qkv/pallas_call | solution.py:59
  57.3 11.2 %attend.3.mine_hbm = bf16[512,896]{1,0:T(8,128)(2,1)} custom-call(s32[1]{0:T(128)} %copy.109.slen_ref, bf16[9,2048,128]{2,1,0:T(8,128)(2,1)} %project_qkv.1.q_ref.k_ref.v_ref, bf16[9,2048,128]{2,1,0:T(8,128)(2,1)} %project_qkv.1.q_ref.k_ref.v_ref, bf16[9,2048,128]{2,1,0:T(8,128)(2,1)} %project_qkv.1.q_ref.k_ref.v_ref), custom_call_target="tpu_custom_call" | custom-call | flops 704643072 | bytes 2097152 | tf_op jit(solution)/shard_map/attend/pallas_call | solution.py:227
  68.5 0.1 broadcast_compare_fusion.1
  68.7 5.7 bitcast_select_fusion
  74.4 1.3 fusion.32
  75.7 0.4 fusion.16
  76.1 0.1 select_maximum_fusion
  76.2 0.7 fusion.2
  76.9 0.9 pad_maximum_fusion.2
  77.8 5.1 all-to-all-start.1
  82.9 4.9 collective-permute-start
  87.8 1.5 collective-permute-start.2
  89.3 1.6 multiply_bitcast_fusion
  90.9 9.5 copy.79
  100.3 7.2 all-to-all-done.1
  107.5 0.8 copy-done.1
  108.3 4.6 all-to-all-start.2
  112.9 45.2 %copy.105 = bf16[1,3584,2,4736]{3,1,2,0:T(8,128)(2,1)} copy(bf16[1,3584,2,4736]{3,2,1,0:T(2,128)(2,1)} %param.22) | data formatting | bytes 135790592 | tf_op args[10]
  158.2 7.3 broadcast_select_fusion
  165.5 1.7 collective-permute-start.1
  167.2 1.3 collective-permute-start.3
  168.5 34.6 %attend.4.refs_0_ = bf16[1536,896]{1,0:T(8,128)(2,1)} custom-call(s32[1]{0:T(128)} %copy.109.slen_ref, bf16[9,2048,128]{2,1,0:T(8,128)(2,1)} %project_qkv.1.q_ref.k_ref.v_ref, bf16[9,2048,128]{2,1,0:T(8,128)(2,1)} %project_qkv.1.q_ref.k_ref.v_ref, bf16[9,2048,128]{2,1,0:T(8,128)(2,1)} %project_qkv.1.q_ref.k_ref.v_ref), custom_call_target="tpu_custom_call" | custom-call | flops 5637144576 | bytes 4194304 | tf_op jit(solution)/shard_map/attend/pallas_call | solution.py:227
  203.1 0.2 fusion.31
  203.4 1.8 copy.106
  205.2 0.2 fusion.15
  205.4 26.3 %collective-permute-done.3.left_hbm_1_ = bf16[512,896]{1,0:T(8,128)(2,1)} collective-permute-done((bf16[512,896]{1,0:T(8,128)(2,1)}, bf16[512,896]{1,0:T(8,128)(2,1)}, u32[]{:S(2)}, u32[]{:S(2)}) %collective-permute-start.3) | collective-permute-done | bytes 917536 | tf_op jit(solution)/shard_map/ppermute | solution.py:658
  231.7 1.6 collective-permute-start.4
  233.3 1.5 collective-permute-start.5
  234.8 0.1 divide_convert_fusion
  234.9 0.6 copy.107
  235.5 27.3 %attend.5.ctx_hbm = bf16[1536,896]{1,0:T(8,128)(2,1)} custom-call(s32[1]{0:T(128)} %copy.109.slen_ref, bf16[9,2048,128]{2,1,0:T(8,128)(2,1)} %project_qkv.1.q_ref.k_ref.v_ref, bf16[9,2048,128]{2,1,0:T(8,128)(2,1)} %project_qkv.1.q_ref.k_ref.v_ref, bf16[9,2048,128]{2,1,0:T(8,128)(2,1)} %project_qkv.1.q_ref.k_ref.v_ref, ...), custom_call_target="tpu_custom_call", output_to_operand_aliasing={{}: (4, {})} | custom-call | flops 4932501504 | bytes 2097152 | tf_op jit(solution)/shard_map/attend/pallas_call | solution.py:227
  262.9 1.3 slice_bitcast_fusion
  264.2 8.0 collective-permute-done.5.left_hbm_2_
  272.2 753.9 %layer_sums.1 = (bf16[2080,3584]{1,0:T(8,128)(2,1)}, bf16[4,3,512,896]{3,2,1,0:T(8,128)(2,1)}, bf16[4,32,896]{2,1,0:T(8,128)(2,1)}, bf16[2080,3584]{1,0:T(8,128)(2,1)}) custom-call(bf16[1536,896]{1,0:T(8,128)(2,1)} %attend.5.ctx_hbm, bf16[32,896]{1,0:T(8,128)(2,1)} %bitcast.77, bf16[512,896]{1,0:T(8,128)(2,1)} %attend.3.mine_hbm, ...), custom_call_target="tpu_custom_call" | custom-call | flops 265268756480 | bytes 510132224 | tf_op jit(solution)/shard_map/layer_sums/pallas_call | solution.py:580
  1026.1 13.3 %slice.69 = bf16[4,512,3584]{2,1,0:T(8,128)(2,1)} slice(bf16[4,520,3584]{2,1,0:T(8,128)(2,1)} %bitcast.67), slice={[0:4], [0:512], [0:3584]} | slice | bytes 29360128 | tf_op jit(solution)/shard_map/slice | solution.py:705
  1039.4 1.6 slice_bitcast_fusion.2
  (35 shorter events, 0.2 us)
Async XLA Ops:
  7.2 2.3 copy-start.5
  7.2 2.4 copy-start.4
  7.2 2.4 copy-start.3
  7.2 265.0 %all-gather.3.cloned.1.call-start = ((), (), s32[]{:S(2)}) async-start(), calls=%async_computation.3 | async-start | bytes 30277632 | tf_op jit(solution)/shard_map/all_gather | solution.py:664
  15.8 52.7 %all-to-all-start = ((bf16[4,32,9,128]{3,1,2,0:T(8,128)(2,1)}), bf16[4,32,9,128]{3,1,2,0:T(8,128)(2,1)S(1)}, u32[]{:S(2)}, u32[]{:S(2)}) async-start(bf16[4,32,9,128]{3,1,2,0:T(8,128)(2,1)} %broadcast_in_dim.76), calls=%async_computation | async-start | bytes 589824 | tf_op jit(solution)/shard_map/all_to_all | solution.py:635
  57.3 11.4 %copy-start = (bf16[1,32,64,4,128]{4,3,2,1,0:T(4,128)(2,1)S(1)}, bf16[1,32,64,4,128]{4,3,2,1,0:T(4,128)(2,1)}, u32[]{:S(2)}) copy-start(bf16[1,32,64,4,128]{4,3,2,1,0:T(4,128)(2,1)} %param.17) | copy-start | bytes 6291460
  77.8 29.7 %all-to-all-start.1 = ((f32[4,32,8,128]{3,2,1,0:T(8,128)}), f32[4,32,8,128]{3,2,1,0:T(8,128)S(1)}, u32[]{:S(2)}, u32[]{:S(2)}) async-start(f32[4,32,8,128]{3,2,1,0:T(8,128)} %pad_maximum_fusion.2), calls=%async_computation.1 | async-start | bytes 1048576 | tf_op jit(solution)/shard_map/all_to_all | solution.py:650
  82.9 82.6 %collective-permute-start = (bf16[512,896]{1,0:T(8,128)(2,1)}, bf16[512,896]{1,0:T(8,128)(2,1)}, u32[]{:S(2)}, u32[]{:S(2)}) collective-permute-start(bf16[512,896]{1,0:T(8,128)(2,1)} %attend.3.mine_hbm), channel_id=1, source_target_pairs={{0,4},{4,8},{8,12},{1,5},{5,9},{9,13},{2,6},{6,10},{10,14},{3,7},{... | collective-permute-start | bytes 2752520 | tf_op jit(solution)/shard_map/ppermute | solution.py:657
  87.8 79.4 %collective-permute-start.2 = (bf16[512,896]{1,0:T(8,128)(2,1)}, bf16[512,896]{1,0:T(8,128)(2,1)}, u32[]{:S(2)}, u32[]{:S(2)}) collective-permute-start(bf16[512,896]{1,0:T(8,128)(2,1)} %attend.3.mine_hbm), channel_id=1, source_target_pairs={{12,8},{8,4},{4,0},{13,9},{9,5},{5,1},{14,10},{10,6},{6,2},{15,11}... | collective-permute-start | bytes 2752520 | tf_op jit(solution)/shard_map/ppermute | solution.py:658
  107.5 0.8 copy-start.1
  108.3 95.0 %all-to-all-start.2 = ((bf16[2,2048,1,128]{3,0,2,1:T(2,128)(2,1)}), bf16[2,2048,1,128]{3,0,2,1:T(2,128)(2,1)S(1)}, u32[]{:S(2)}, u32[]{:S(2)}) async-start(bf16[2,2048,1,128]{3,0,2,1:T(2,128)(2,1)} %copy.79), calls=%async_computation.2 | async-start | bytes 2097152 | tf_op jit(solution)/shard_map/all_to_all | solution.py:709
  165.4 37.7 %copy-start.2 = (f32[4,32,8,128]{3,2,1,0:T(8,128)S(1)}, f32[4,32,8,128]{3,2,1,0:T(8,128)}, u32[]{:S(2)}) copy-start(f32[4,32,8,128]{3,2,1,0:T(8,128)} %copy-done.1) | copy-start | bytes 1572868
  165.5 39.9 %collective-permute-start.1 = (bf16[512,896]{1,0:T(8,128)(2,1)}, bf16[512,896]{1,0:T(8,128)(2,1)}, u32[]{:S(2)}, u32[]{:S(2)}) collective-permute-start(bf16[512,896]{1,0:T(8,128)(2,1)} %collective-permute-done.right_hbm_0_), channel_id=1, source_target_pairs={{4,8},{8,12},{5,9},{9,13},{6,10},{10,14},{7,11},{11,15},{20,24},{2... | collective-permute-start | bytes 2752520 | tf_op jit(solution)/shard_map/ppermute | solution.py:657
  167.2 64.5 %collective-permute-start.3 = (bf16[512,896]{1,0:T(8,128)(2,1)}, bf16[512,896]{1,0:T(8,128)(2,1)}, u32[]{:S(2)}, u32[]{:S(2)}) collective-permute-start(bf16[512,896]{1,0:T(8,128)(2,1)} %collective-permute-done.2.left_hbm_0_), channel_id=1, source_target_pairs={{8,4},{4,0},{9,5},{5,1},{10,6},{6,2},{11,7},{7,3},{24,20},{20,16},... | collective-permute-start | bytes 2752520 | tf_op jit(solution)/shard_map/ppermute | solution.py:658
  205.2 57.7 %collective-permute-start.6 = (bf16[2,512,4,128]{3,2,1,0:T(4,128)(2,1)}, bf16[2,512,4,128]{3,2,1,0:T(4,128)(2,1)S(1)}, u32[]{:S(2)}, u32[]{:S(2)}) collective-permute-start(bf16[2,512,4,128]{3,2,1,0:T(4,128)(2,1)} %bitcast.64), channel_id=1, source_target_pairs={{0,1},{1,2},{2,3},{3,0},{4,5},{5,6},{6,7},{7,4},{8,9},{9,10},{10,1... | collective-permute-start | bytes 3145736 | tf_op jit(solution)/shard_map/ppermute | solution.py:710
  231.7 32.5 %collective-permute-start.4 = (bf16[512,896]{1,0:T(8,128)(2,1)}, bf16[512,896]{1,0:T(8,128)(2,1)}, u32[]{:S(2)}, u32[]{:S(2)}) collective-permute-start(bf16[512,896]{1,0:T(8,128)(2,1)} %collective-permute-done.1.right_hbm_1_), channel_id=1, source_target_pairs={{8,12},{9,13},{10,14},{11,15},{24,28},{25,29},{26,30},{27,31}} | collective-permute-start | bytes 2752520 | tf_op jit(solution)/shard_map/ppermute | solution.py:657
  233.3 38.9 %collective-permute-start.5 = (bf16[512,896]{1,0:T(8,128)(2,1)}, bf16[512,896]{1,0:T(8,128)(2,1)}, u32[]{:S(2)}, u32[]{:S(2)}) collective-permute-start(bf16[512,896]{1,0:T(8,128)(2,1)} %collective-permute-done.3.left_hbm_1_), channel_id=1, source_target_pairs={{4,0},{5,1},{6,2},{7,3},{20,16},{21,17},{22,18},{23,19}} | collective-permute-start | bytes 2752520 | tf_op jit(solution)/shard_map/ppermute | solution.py:658
Sparse Core Ops, SparseCore 0:
  10.9 242.5 all-gather.2

commit v5 on v4

--- a/solution.py
+++ b/solution.py
@@ -251,12 +251,12 @@
 
 
 CHUNKS = 4
-SUBS = 13
+SUBS = 5
 SLOTS = 2
 ACCS = 3
 TILE = 256
 TILE_OUT = 512
-OWNED = (10, 4, 4, 10)
+OWNED = (11, 3, 3, 11)
 
 
 def layer_kernel(geo, ctx_hbm, dctx_hbm, mine_hbm, right_hbm, left_hbm, x_hbm, y_hbm, gain_ref, wo_ref, wg_ref, wu_ref, wd_ref, out_hbm, full_hbm, dfull_hbm, hid_hbm,
@@ -334,20 +334,29 @@
     def inside(k):
         return (k >= 0) & (k < total)
 
-    def collect(m):
+    def advance(m):
         for f, col, cols, peak in flows:
             for side, there, dist, outer, inner, more in sides(f):
                 k = m - peak + dist
 
-                @at(inside(k) & there & more)
-                def _(f=f, side=side, outer=outer, inner=inner, k=k):
-                    rs_copy(f, k, side, inner).wait_recv()
-                    mine = part(f, k)
-                    mine[...] += slots[f][side, k % SLOTS]
-
-                    @at(k + SLOTS < total)
+                @at(inside(k) & there)
+                def _(f=f, side=side, outer=outer, inner=inner, more=more, k=k):
+                    @at(more)
                     def _():
-                        pl.semaphore_signal(credit.at[f], inc=1, **to(outer))
+                        rs_copy(f, k, side, inner).wait_recv()
+                        mine = part(f, k)
+                        mine[...] += slots[f][side, k % SLOTS]
+
+                        @at(k + SLOTS < total)
+                        def _():
+                            pl.semaphore_signal(credit.at[f], inc=1, **to(outer))
+
+                    @at(k >= SLOTS)
+                    def _():
+                        pl.semaphore_wait(credit.at[f], 1)
+                        rs_copy(f, k - SLOTS, side, inner).wait_send()
+
+                    rs_copy(f, k, side, inner).start()
 
             k = m - peak
 
@@ -372,20 +381,6 @@
                     for side, _, _, outer, _, _ in sides(f):
                         pl.semaphore_signal(credit.at[f], inc=1, **to(outer))
 
-    def send(m):
-        for f, col, cols, peak in flows:
-            for side, there, dist, outer, inner, more in sides(f):
-                k = m - peak + dist
-
-                @at(inside(k) & there)
-                def _(f=f, side=side, inner=inner, k=k):
-                    @at(k >= SLOTS)
-                    def _():
-                        pl.semaphore_wait(credit.at[f], 1)
-                        rs_copy(f, k - SLOTS, side, inner).wait_send()
-
-                    rs_copy(f, k, side, inner).start()
-
         for f, col, cols, peak in flows:
             k = m - peak
 
@@ -427,12 +422,10 @@
 
     @at((c > 0) & (j % stride == 0) & (j < stride * SUBS))
     def _():
-        period = SUBS * (c - 1) + j // stride
-        collect(period)
-        send(period)
+        advance(SUBS * (c - 1) + j // stride)
 
     for n in range(1, last + 1):
-        @at((c + 1 < CHUNKS) & (j == ticks * n // (last + 1) + 2))
+        @at((c + 1 < CHUNKS) & (j == ticks * n // (last + 1) + 1))
         def _(n=n):
             spread(c + 1).hop(n)
             if n == last:
@@ -484,11 +477,9 @@
 
     @at(j < out_tiles)
     def _():
-        heads = head_cols // 128
         mixed = None
         for s in range(tp):
-            w = wo_ref[s].reshape(head_cols, TILE_OUT)
-            one = jnp.dot(cx[:, s * head_cols:(s + 1) * head_cols], w, preferred_element_type=F32)
+            one = jnp.dot(cx[:, s * head_cols:(s + 1) * head_cols], wo_ref[s], preferred_element_type=F32)
             mixed = one if mixed is None else mixed + one
         cols = pl.ds(pl.multiple_of(j * TILE_OUT, TILE_OUT), TILE_OUT)
         hid[:, cols] = (hid[:, cols].astype(F32) + mixed).astype(BF)
@@ -528,8 +519,7 @@
     def _():
         @pl.loop(SUBS * (CHUNKS - 1), total + 2 * last)
         def _(m):
-            collect(m)
-            send(m)
+            advance(m)
 
         for f, col, cols, peak in flows:
             for side, there, dist, outer, inner, more in sides(f):
@@ -569,8 +559,6 @@
     sub = rows // SUBS
     total = CHUNKS * SUBS
     geo = (width, head_cols, step, dec, ff_tiles, tail)
-    heads = head_cols // 128
-
     def ff_index(j):
         return jnp.maximum(j - out_tiles, 0)
 
@@ -583,7 +571,7 @@
         in_specs=[
             any_spec, any_spec, any_spec, [any_spec] * (tp - 1), [any_spec] * (tp - 1), any_spec, any_spec,
             pl.BlockSpec((1, width), lambda c, j: (0, 0)),
-            pl.BlockSpec((tp, heads, 128, TILE_OUT), lambda c, j: (0, 0, 0, jnp.minimum(j, out_tiles - 1))),
+            pl.BlockSpec((tp, head_cols, TILE_OUT), lambda c, j: (0, 0, jnp.minimum(j, out_tiles - 1))),
             pl.BlockSpec((1, width, TILE), lambda c, j: (0, 0, ff_index(j))),
             pl.BlockSpec((1, width, TILE), lambda c, j: (1, 0, ff_index(j))),
             pl.BlockSpec((TILE, width), lambda c, j: (ff_index(j), 0)),
@@ -659,8 +647,9 @@
 
 
 def gather_w_out(w_out, mesh):
+    rows = w_out.shape[0] // (mesh.shape['pair'] * mesh.shape['side'])
     index = lax.axis_index('pair') * mesh.shape['side'] + lax.axis_index('side')
-    own = lax.dynamic_index_in_dim(w_out, jnp.minimum(index, w_out.shape[0] - 1), 0, keepdims=False)
+    own = lax.dynamic_slice_in_dim(w_out, index * rows, rows, 0)
     return lax.all_gather(own, ('tp', 'pair', 'side'))
 
 
@@ -679,34 +668,30 @@
         cos, sin = rope_tables(positions, head)
         cos, sin = jnp.concatenate([cos, cos], -1), jnp.concatenate([-sin, sin], -1)
 
-        w_full = gather_w_out(w_out[0, 0], mesh).reshape(tp, -1, head, width)
-        gate_up = jnp.transpose(w_gate_up[0], (1, 0, 2))
-
+        w_full = gather_w_out(w_out[0, 0].reshape(group_q * head, width), mesh).reshape(tp, group_q * head, width)
         mixed, key_now, value_now = decode_local(y_tok, c_len, k_cache[0], v_cache[0], attn_gain[0], w_qkv[0])
 
         w_slots = jnp.transpose(w_qkv[0, :, 0], (1, 0, 2))
         qkv = project_qkv(x, attn_gain, cos, sin, w_slots)
         step, dec = seq_len // CHUNKS, y_tok.shape[0] // CHUNKS
-        rest = seq_len - step
         mine = attend(s_len, qkv, 0, step, step)
         moved = [pass_on(mine, mine, 1, tp)]
-        mixed, qkv, mine = lax.optimization_barrier((mixed, qkv, mine))
+        kv_pair = (qkv[group_q:] * keep_mask)[:, :, None]
+        kv_by_pos = lax.all_to_all(kv_pair, 'tp', 1, 2, tiled=True)
+        w_gate_up, moved[0] = lax.optimization_barrier((w_gate_up, moved[0]))
+        moved.append(pass_on(*moved[0], 2, tp))
+        gate_up = jnp.transpose(w_gate_up[0], (1, 0, 2))
+        qkv, gate_up, moved[1], kv_by_pos, mixed = lax.optimization_barrier((qkv, gate_up, moved[1], kv_by_pos, mixed))
         dctx = decode_combine(mixed)
-        ctx = attend(s_len, qkv, step, rest - step, rest)
-        for hop in range(2, tp):
-            pair = pass_on(*moved[-1], hop, tp)
-            if hop < tp - 1:
-                ctx, pair = lax.optimization_barrier((ctx, pair))
-            moved.append(pair)
-        ctx = attend(s_len, qkv, rest, step, rest, ctx)
+        moved.append(pass_on(*moved[1], 3, tp))
+        ctx = attend(s_len, qkv, step, seq_len - step, seq_len - step)
+        ctx, moved[2] = lax.optimization_barrier((ctx, moved[2]))
 
         done = layer_sums(ctx, dctx.reshape(-1, ctx.shape[1]), mine, [r for r, _ in moved], [l for _, l in moved], x, y_tok, mlp_gain, w_full, gate_up, w_down[0])
         done = done.reshape(CHUNKS, step + dec, width)
         hidden = done[:, :step].reshape(seq_len, width)
         tokens = done[:, step:].reshape(CHUNKS * dec, width)
 
-        kv_pair = (qkv[group_q:] * keep_mask)[:, :, None]
-        kv_by_pos = lax.all_to_all(kv_pair, 'tp', 1, 2, tiled=True)
         kv_recv = lax.ppermute(kv_by_pos, 'side', send_pairs)
         return (hidden[None], tokens, kv_recv[0][None, None], kv_recv[1][None, None], key_now[None], value_now[None])
 

time: 1050 us -> 1030 us (0.981)
  Pallas kernels: 856 us -> 819 us
  starting transfers between devices: 28.6 us -> 47.6 us
    unnamed x14 -> x11, local copies, waits for them, and re-layouts: 46.7 us -> 0.66 us
    optimization_barrier x0 -> x1, local copies, waits for them, and re-layouts: none -> 45.3 us  [device_fn(): w_gate_up, moved[0] = lax.optimization_barrier((w_gate_up, moved[0]))]
    pallas_call x1, Pallas kernels: 754 us -> 719 us  [layer_sums(): pl.pallas_call(functools.partial(layer_kernel, geo), grid=(CHUNKS, out_ti...]
    all_to_all x1, waiting for transfers between devices: 0.01 us -> 25.7 us  [decode_local(): lax.all_to_all(jnp.broadcast_to(local_qkv, (tp,) + local_qkv.shape), 'tp'...]
    all_to_all x1, starting transfers between devices: 5.08 us -> 24.8 us  [decode_combine(): own = lax.all_to_all(mixed, 'tp', 0, 0)]
    ppermute x3, waiting for transfers between devices: 34.3 us -> 22.6 us  [pass_on(): lax.ppermute(left, 'tp', [(place, place - 1) for place in range(tp - hop,...]
    pallas_call x3 -> x2, Pallas kernels: 73.1 us -> 71 us  [attend(): pl.pallas_call(functools.partial(flash_kernel, block_q, block_k, some, ba...]
  transfers between devices with their start and end apart: 11 -> 11, of which waited for: 3 -> 2; matrix products, arithmetic and copies ran while one was open for 8% -> 8% of each run, Pallas kernels for 10% -> 10%
where the time goes in v5:
time: 1030 us
  Pallas kernels  819 us (80%)
  local copies, waits for them, and re-layouts  75.6 us (7%)
  waiting for transfers between devices  48.3 us (5%)
  starting transfers between devices  47.6 us (5%)
  other arithmetic  20.3 us (2%)
  between operations  15 us (1%)
    pallas_call x1, Pallas kernels, layer_sums(): pl.pallas_call(functools.partial(layer_kernel, geo), grid=(CHUNKS, out_ti...  719 us
    pallas_call x2, Pallas kernels, attend(): pl.pallas_call(functools.partial(flash_kernel, block_q, block_k, some, ba...  71 us
    optimization_barrier x1, local copies, waits for them, and re-layouts, device_fn(): w_gate_up, moved[0] = lax.optimization_barrier((w_gate_up, moved[0]))  45.3 us
    pallas_call x1, Pallas kernels, project_qkv(): pl.pallas_call(qkv_kernel, grid=(rows // rows_block,), in_specs=[pl.Block...  28.8 us
    all_to_all x1, waiting for transfers between devices, decode_local(): lax.all_to_all(jnp.broadcast_to(local_qkv, (tp,) + local_qkv.shape), 'tp'...  25.7 us
    all_to_all x1, starting transfers between devices, decode_combine(): own = lax.all_to_all(mixed, 'tp', 0, 0)  24.8 us
    ppermute x3, waiting for transfers between devices, pass_on(): lax.ppermute(left, 'tp', [(place, place - 1) for place in range(tp - hop,...  22.6 us
  transfers between devices with their start and end apart: 11, of which 2 were waited for; matrix products, arithmetic and copies ran while one was open for 8% of the time, Pallas kernels for 10%

profile of v5, /device:TPU:0, one launch (start us, length us, event | category | flops | bytes accessed | tf_op | source)
XLA Modules:
  0.0 1032.8 jit_solution(17257282738212972833)
XLA Ops:
  7.2 0.0 all-gather.3.cloned.1.call-start
  7.2 2.1 constant_dynamic-slice_fusion
  9.3 0.0 all-gather.3.cloned.1.call-update
  10.0 3.7 fusion.22
  13.7 1.9 pad_maximum_fusion
  15.7 28.8 %project_qkv.1.q_ref.k_ref.v_ref = bf16[9,2048,128]{2,1,0:T(8,128)(2,1)} custom-call(bf16[2048,3584]{1,0:T(8,128)(2,1)} %bitcast.83, bf16[1,3584]{1,0:T(2,128)(2,1)} %gain_ref.2, f32[2048,128]{1,0:T(8,128)} %get-tuple-element.55.cos_ref, f32[2048,128]{1,0:T(8,128)} %get-tuple-element.56.sin_ref, bf16[9,3584,128]{2,1,0:T(8,128)(2,1)} %bitcast.71), custom_call_target="tpu_custom_call" | custom-call | flops 16911433728 | bytes 27656192 | tf_op jit(solution)/shard_map/project_qkv/pallas_call | solution.py:59
  44.4 11.1 %attend.2.mine_hbm = bf16[512,896]{1,0:T(8,128)(2,1)} custom-call(s32[1]{0:T(128)} %copy.107.slen_ref, bf16[9,2048,128]{2,1,0:T(8,128)(2,1)} %project_qkv.1.q_ref.k_ref.v_ref, bf16[9,2048,128]{2,1,0:T(8,128)(2,1)} %project_qkv.1.q_ref.k_ref.v_ref, bf16[9,2048,128]{2,1,0:T(8,128)(2,1)} %project_qkv.1.q_ref.k_ref.v_ref), custom_call_target="tpu_custom_call" | custom-call | flops 704643072 | bytes 2097152 | tf_op jit(solution)/shard_map/attend/pallas_call | solution.py:227
  55.5 5.9 collective-permute-start
  61.5 1.3 collective-permute-start.1
  62.8 0.2 fusion.19
  63.0 0.1 multiply_cosine_fusion.1
  63.2 4.9 fusion.12
  68.1 0.1 subtract_convert_fusion
  68.2 0.1 maximum_bitcast_fusion
  68.3 0.8 broadcast_in_dim.77
  69.1 5.9 all-to-all-start.1
  75.0 1.6 fusion.15
  76.6 0.0 copy-start
  76.6 9.5 copy.70
  86.1 0.1 broadcast_compare_fusion.1
  86.2 25.7 %all-to-all-done.1 = bf16[4,32,9,128]{3,1,2,0:T(8,128)(2,1)S(1)} async-done(((bf16[4,32,9,128]{3,1,2,0:T(8,128)(2,1)}), bf16[4,32,9,128]{3,1,2,0:T(8,128)(2,1)S(1)}, u32[]{:S(2)}, u32[]{:S(2)}) %all-to-all-start.1) | async-done | bytes 294944 | tf_op jit(solution)/shard_map/all_to_all | solution.py:623
  111.9 3.5 all-to-all-start
  115.5 5.7 bitcast_select_fusion
  121.2 1.3 fusion.33
  122.5 0.4 fusion.17
  122.9 0.1 select_maximum_fusion
  123.0 1.6 collective-permute-start.2
  124.6 1.3 collective-permute-start.3
  125.9 0.0 copy-start.1
  125.9 0.7 fusion.2
  126.6 0.9 pad_maximum_fusion.2
  127.5 4.9 broadcast_select_fusion
  132.5 45.3 %copy.104 = bf16[1,3584,2,4736]{3,1,2,0:T(8,128)(2,1)} copy(bf16[1,3584,2,4736]{3,2,1,0:T(2,128)(2,1)} %param.22) | data formatting | bytes 135790592 | tf_op jit(solution)/shard_map/optimization_barrier | solution.py:681
  177.8 0.8 copy.105
  178.7 22.6 %collective-permute-done.3.left_hbm_1_ = bf16[512,896]{1,0:T(8,128)(2,1)} collective-permute-done((bf16[512,896]{1,0:T(8,128)(2,1)}, bf16[512,896]{1,0:T(8,128)(2,1)}, u32[]{:S(2)}, u32[]{:S(2)}) %collective-permute-start.3) | collective-permute-done | bytes 917536 | tf_op jit(solution)/shard_map/ppermute | solution.py:646
  201.2 24.8 %all-to-all-start.2 = ((f32[4,32,8,128]{3,2,1,0:T(8,128)}), f32[4,32,8,128]{3,2,1,0:T(8,128)S(1)}, u32[]{:S(2)}, u32[]{:S(2)}) async-start(f32[4,32,8,128]{3,2,1,0:T(8,128)} %pad_maximum_fusion.2), calls=%async_computation.2 | async-start | bytes 1048576 | tf_op jit(solution)/shard_map/all_to_all | solution.py:638
  226.0 1.6 collective-permute-start.4
  227.7 1.3 collective-permute-start.5
  228.9 0.3 collective-permute-start.6
  229.2 59.9 %attend.3.ctx_hbm = bf16[1536,896]{1,0:T(8,128)(2,1)} custom-call(s32[1]{0:T(128)} %copy.107.slen_ref, bf16[9,2048,128]{2,1,0:T(8,128)(2,1)} %project_qkv.1.q_ref.k_ref.v_ref, bf16[9,2048,128]{2,1,0:T(8,128)(2,1)} %project_qkv.1.q_ref.k_ref.v_ref, bf16[9,2048,128]{2,1,0:T(8,128)(2,1)} %project_qkv.1.q_ref.k_ref.v_ref), custom_call_target="tpu_custom_call" | custom-call | flops 10569646080 | bytes 6291456 | tf_op jit(solution)/shard_map/attend/pallas_call | solution.py:227
  289.1 0.2 fusion.32
  289.4 0.2 fusion.16
  289.6 0.1 divide_convert_fusion
  289.7 0.6 copy.106
  290.4 1.3 slice_bitcast_fusion
  291.7 719.3 %layer_sums.1 = (bf16[2080,3584]{1,0:T(8,128)(2,1)}, bf16[4,3,512,896]{3,2,1,0:T(8,128)(2,1)}, bf16[4,32,896]{2,1,0:T(8,128)(2,1)}, bf16[2080,3584]{1,0:T(8,128)(2,1)}) custom-call(bf16[1536,896]{1,0:T(8,128)(2,1)} %attend.3.ctx_hbm, bf16[32,896]{1,0:T(8,128)(2,1)} %bitcast.80, bf16[512,896]{1,0:T(8,128)(2,1)} %attend.2.mine_hbm, ...), custom_call_target="tpu_custom_call" | custom-call | flops 265268756480 | bytes 510132224 | tf_op jit(solution)/shard_map/layer_sums/pallas_call | solution.py:568
  1011.0 13.3 %slice.70 = bf16[4,512,3584]{2,1,0:T(8,128)(2,1)} slice(bf16[4,520,3584]{2,1,0:T(8,128)(2,1)} %bitcast.68), slice={[0:4], [0:512], [0:3584]} | slice | bytes 29360128 | tf_op jit(solution)/shard_map/slice | solution.py:692
  1024.3 1.6 slice_bitcast_fusion.2
  (32 shorter events, 0.2 us)
Async XLA Ops:
  7.2 284.5 %all-gather.3.cloned.1.call-start = ((), (), s32[]{:S(2)}) async-start(), calls=%async_computation.3 | async-start | bytes 26492928 | tf_op jit(solution)/shard_map/all_gather | solution.py:653
  44.4 18.3 %copy-start.4 = (s32[32]{0:T(128)S(1)}, s32[32]{0:T(128)}, u32[]{:S(2)}) copy-start(s32[32]{0:T(128)} %param.15) | copy-start | bytes 388
  44.4 18.3 %copy-start.3 = (bf16[1,3584]{1,0:T(2,128)(2,1)S(1)}, bf16[1,3584]{1,0:T(2,128)(2,1)}, u32[]{:S(2)}) copy-start(bf16[1,3584]{1,0:T(2,128)(2,1)} %gain_ref.2) | copy-start | bytes 21508
  44.4 18.4 %copy-start.2 = (bf16[32,3584]{1,0:T(8,128)(2,1)S(1)}, bf16[32,3584]{1,0:T(8,128)(2,1)}, u32[]{:S(2)}) copy-start(bf16[32,3584]{1,0:T(8,128)(2,1)} %y_hbm.1) | copy-start | bytes 688132
  55.5 67.4 %collective-permute-start = (bf16[512,896]{1,0:T(8,128)(2,1)}, bf16[512,896]{1,0:T(8,128)(2,1)}, u32[]{:S(2)}, u32[]{:S(2)}) collective-permute-start(bf16[512,896]{1,0:T(8,128)(2,1)} %attend.2.mine_hbm), channel_id=1, source_target_pairs={{0,4},{4,8},{8,12},{1,5},{5,9},{9,13},{2,6},{6,10},{10,14},{3,7},{... | collective-permute-start | bytes 2752520 | tf_op jit(solution)/shard_map/ppermute | solution.py:645
  61.5 61.5 %collective-permute-start.1 = (bf16[512,896]{1,0:T(8,128)(2,1)}, bf16[512,896]{1,0:T(8,128)(2,1)}, u32[]{:S(2)}, u32[]{:S(2)}) collective-permute-start(bf16[512,896]{1,0:T(8,128)(2,1)} %attend.2.mine_hbm), channel_id=1, source_target_pairs={{12,8},{8,4},{4,0},{13,9},{9,5},{5,1},{14,10},{10,6},{6,2},{15,11}... | collective-permute-start | bytes 2752520 | tf_op jit(solution)/shard_map/ppermute | solution.py:646
  69.1 42.8 %all-to-all-start.1 = ((bf16[4,32,9,128]{3,1,2,0:T(8,128)(2,1)}), bf16[4,32,9,128]{3,1,2,0:T(8,128)(2,1)S(1)}, u32[]{:S(2)}, u32[]{:S(2)}) async-start(bf16[4,32,9,128]{3,1,2,0:T(8,128)(2,1)} %broadcast_in_dim.77), calls=%async_computation.1 | async-start | bytes 589824 | tf_op jit(solution)/shard_map/all_to_all | solution.py:623
  76.6 38.9 %copy-start = (bf16[1,32,64,4,128]{4,3,2,1,0:T(4,128)(2,1)S(1)}, bf16[1,32,64,4,128]{4,3,2,1,0:T(4,128)(2,1)}, u32[]{:S(2)}) copy-start(bf16[1,32,64,4,128]{4,3,2,1,0:T(4,128)(2,1)} %param.17) | copy-start | bytes 6291460
  111.9 66.0 %all-to-all-start = ((bf16[2,2048,1,128]{3,0,2,1:T(2,128)(2,1)}), bf16[2,2048,1,128]{3,0,2,1:T(2,128)(2,1)S(1)}, u32[]{:S(2)}, u32[]{:S(2)}) async-start(bf16[2,2048,1,128]{3,0,2,1:T(2,128)(2,1)} %copy.70), calls=%async_computation | async-start | bytes 2097152 | tf_op jit(solution)/shard_map/all_to_all | solution.py:680
  123.0 55.7 %collective-permute-start.2 = (bf16[512,896]{1,0:T(8,128)(2,1)}, bf16[512,896]{1,0:T(8,128)(2,1)}, u32[]{:S(2)}, u32[]{:S(2)}) collective-permute-start(bf16[512,896]{1,0:T(8,128)(2,1)} %collective-permute-done.right_hbm_0_), channel_id=1, source_target_pairs={{4,8},{8,12},{5,9},{9,13},{6,10},{10,14},{7,11},{11,15},{20,24},{2... | collective-permute-start | bytes 2752520 | tf_op jit(solution)/shard_map/ppermute | solution.py:645
  124.6 76.6 %collective-permute-start.3 = (bf16[512,896]{1,0:T(8,128)(2,1)}, bf16[512,896]{1,0:T(8,128)(2,1)}, u32[]{:S(2)}, u32[]{:S(2)}) collective-permute-start(bf16[512,896]{1,0:T(8,128)(2,1)} %collective-permute-done.1.left_hbm_0_), channel_id=1, source_target_pairs={{8,4},{4,0},{9,5},{5,1},{10,6},{6,2},{11,7},{7,3},{24,20},{20,16},... | collective-permute-start | bytes 2752520 | tf_op jit(solution)/shard_map/ppermute | solution.py:646
  125.9 1.6 copy-start.1
  201.2 87.9 %all-to-all-start.2 = ((f32[4,32,8,128]{3,2,1,0:T(8,128)}), f32[4,32,8,128]{3,2,1,0:T(8,128)S(1)}, u32[]{:S(2)}, u32[]{:S(2)}) async-start(f32[4,32,8,128]{3,2,1,0:T(8,128)} %pad_maximum_fusion.2), calls=%async_computation.2 | async-start | bytes 1048576 | tf_op jit(solution)/shard_map/all_to_all | solution.py:638
  226.0 64.3 %collective-permute-start.4 = (bf16[512,896]{1,0:T(8,128)(2,1)}, bf16[512,896]{1,0:T(8,128)(2,1)}, u32[]{:S(2)}, u32[]{:S(2)}) collective-permute-start(bf16[512,896]{1,0:T(8,128)(2,1)} %collective-permute-done.2.right_hbm_1_), channel_id=1, source_target_pairs={{8,12},{9,13},{10,14},{11,15},{24,28},{25,29},{26,30},{27,31}} | collective-permute-start | bytes 2752520 | tf_op jit(solution)/shard_map/ppermute | solution.py:645
  227.7 62.7 %collective-permute-start.5 = (bf16[512,896]{1,0:T(8,128)(2,1)}, bf16[512,896]{1,0:T(8,128)(2,1)}, u32[]{:S(2)}, u32[]{:S(2)}) collective-permute-start(bf16[512,896]{1,0:T(8,128)(2,1)} %collective-permute-done.3.left_hbm_1_), channel_id=1, source_target_pairs={{4,0},{5,1},{6,2},{7,3},{20,16},{21,17},{22,18},{23,19}} | collective-permute-start | bytes 2752520 | tf_op jit(solution)/shard_map/ppermute | solution.py:646
  228.9 61.4 %collective-permute-start.6 = (bf16[2,512,4,128]{3,2,1,0:T(4,128)(2,1)S(1)}, bf16[2,512,4,128]{3,2,1,0:T(4,128)(2,1)S(1)}, u32[]{:S(2)}, u32[]{:S(2)}) collective-permute-start(bf16[2,512,4,128]{3,2,1,0:T(4,128)(2,1)S(1)} %bitcast.73), channel_id=1, source_target_pairs={{0,1},{1,2},{2,3},{3,0},{4,5},{5,6},{6,7},{7,4},{8,9},{9,10},{10,1... | collective-permute-start | bytes 3145736 | tf_op jit(solution)/shard_map/ppermute | solution.py:695
Sparse Core Ops, SparseCore 0:
  10.8 218.1 all-gather.2

commit v6 on v5

--- a/solution.py
+++ b/solution.py
@@ -417,9 +417,6 @@
         spread(1).start()
         cx[...] = jnp.zeros_like(cx)
         hid[...] = jnp.zeros_like(hid)
-        for n in range(1, last + 1):
-            tokens.hop(n)
-
     @at((c > 0) & (j % stride == 0) & (j < stride * SUBS))
     def _():
         advance(SUBS * (c - 1) + j // stride)
@@ -443,7 +440,7 @@
             copy.start()
         for s in range(tp):
             head_range = pl.ds(s * head_cols, head_cols)
-            where, tail_rows = cx.at[pl.ds(0, step), head_range], cx.at[pl.ds(step, dec), head_range]
+            where = cx.at[pl.ds(0, step), head_range]
 
             for device in range(tp):
                 piece = mine_hbm if device == s else right_hbm[device - s - 1] if device > s else left_hbm[s - device - 1]
@@ -459,6 +456,15 @@
             @at((c > 0) & (t != s))
             def _(s=s, where=where):
                 pltpu.make_async_copy(full_hbm.at[s, c - 1], where, load_sem.at[s]).start()
+
+        @at(c == 0)
+        def _():
+            for n in range(1, last + 1):
+                tokens.hop(n)
+
+        for s in range(tp):
+            head_range = pl.ds(s * head_cols, head_cols)
+            tail_rows = cx.at[pl.ds(step, dec), head_range]
 
             @at(t == s)
             def _(s=s, tail_rows=tail_rows):
@@ -608,19 +614,21 @@
     )(ctx, dctx, mine, right, left, x, y, gain, w_full, w_gate_up, w_gate_up, w_down)[0]
 
 
-def decode_local(tokens, cache_lens, k_cache, v_cache, gain, w_qkv):
+def decode_project(tokens, cache_lens, gain, w_qkv):
     group_q = w_qkv.shape[2] - 2
-    head_dim = w_qkv.shape[3]
+    normed = rms_norm(tokens, gain)
+    projected = jnp.einsum('bd,dkjh->bkjh', normed, w_qkv, preferred_element_type=F32)
+    rotated = rope_rotate(projected[:, :, :group_q + 1], cache_lens)
+    local_qkv = jnp.concatenate([rotated, projected[:, :, group_q + 1:]], axis=2).astype(BF)[:, 0]
+    return local_qkv
+
+
+def decode_local(full_qkv, cache_lens, k_cache, v_cache):
+    group_q, head_dim = full_qkv.shape[2] - 2, full_qkv.shape[3]
     cache_local = k_cache.shape[1]
     cache_pos = lax.axis_index('tp') * cache_local + jnp.arange(cache_local)
     write_mask = (cache_pos[None, :] == cache_lens[:, None])[:, :, None, None]
     allowed = (cache_pos[None, :] <= cache_lens[:, None])[None, :, None, :]
-    normed = rms_norm(tokens, gain)
-    projected = jnp.einsum('bd,dkjh->bkjh', normed, w_qkv, preferred_element_type=F32)
-    rotated = rope_rotate(projected[:, :, :group_q + 1], cache_lens)
-    local_qkv = jnp.concatenate([rotated, projected[:, :, group_q + 1:]], axis=2).astype(BF)[:, 0]
-    tp = k_cache.shape[2]
-    full_qkv = lax.all_to_all(jnp.broadcast_to(local_qkv, (tp,) + local_qkv.shape), 'tp', 0, 0)
     key_now = jnp.where(write_mask, jnp.moveaxis(full_qkv[:, :, group_q], 0, 1)[:, None], k_cache)
     value_now = jnp.where(write_mask, jnp.moveaxis(full_qkv[:, :, group_q + 1], 0, 1)[:, None], v_cache)
     scores = jnp.einsum('kbgh,btkh->kbgt', full_qkv[:, :, :group_q], key_now, preferred_element_type=F32) * head_dim ** -0.5
@@ -633,9 +641,8 @@
     return jnp.concatenate([mixed, stats[:, :, None]], axis=2), key_now, value_now
 
 
-def decode_combine(mixed):
-    heads = mixed.shape[2] - 1
-    own = lax.all_to_all(mixed, 'tp', 0, 0)
+def decode_combine(own):
+    heads = own.shape[2] - 1
     top, total = own[:, :, heads, :heads], own[:, :, heads, heads:2 * heads]
     factor = jnp.exp(top - jnp.max(top, axis=0))
     return (jnp.sum(own[:, :, :heads] * factor[..., None], axis=0) / jnp.sum(total * factor, axis=0)[..., None]).astype(BF)
@@ -669,30 +676,36 @@
         cos, sin = jnp.concatenate([cos, cos], -1), jnp.concatenate([-sin, sin], -1)
 
         w_full = gather_w_out(w_out[0, 0].reshape(group_q * head, width), mesh).reshape(tp, group_q * head, width)
-        mixed, key_now, value_now = decode_local(y_tok, c_len, k_cache[0], v_cache[0], attn_gain[0], w_qkv[0])
+        local_qkv = decode_project(y_tok, c_len, attn_gain[0], w_qkv[0])
+        local_qkv, x = lax.optimization_barrier((local_qkv, x))
+        full_qkv = lax.all_to_all(jnp.broadcast_to(local_qkv, (tp,) + local_qkv.shape), 'tp', 0, 0)
 
         w_slots = jnp.transpose(w_qkv[0, :, 0], (1, 0, 2))
         qkv = project_qkv(x, attn_gain, cos, sin, w_slots)
+        qkv, full_qkv = lax.optimization_barrier((qkv, full_qkv))
         step, dec = seq_len // CHUNKS, y_tok.shape[0] // CHUNKS
         mine = attend(s_len, qkv, 0, step, step)
         moved = [pass_on(mine, mine, 1, tp)]
-        kv_pair = (qkv[group_q:] * keep_mask)[:, :, None]
-        kv_by_pos = lax.all_to_all(kv_pair, 'tp', 1, 2, tiled=True)
-        w_gate_up, moved[0] = lax.optimization_barrier((w_gate_up, moved[0]))
+        kv_pair = qkv[group_q:] * keep_mask
+        full_qkv, mine = lax.optimization_barrier((full_qkv, mine))
+        mixed, key_now, value_now = decode_local(full_qkv, c_len, k_cache[0], v_cache[0])
+        kv_near = lax.ppermute(kv_pair, 'side', send_pairs)
+        w_gate_up, moved[0], mixed = lax.optimization_barrier((w_gate_up, moved[0], mixed))
+        mixed = lax.all_to_all(mixed, 'tp', 0, 0)
         moved.append(pass_on(*moved[0], 2, tp))
         gate_up = jnp.transpose(w_gate_up[0], (1, 0, 2))
-        qkv, gate_up, moved[1], kv_by_pos, mixed = lax.optimization_barrier((qkv, gate_up, moved[1], kv_by_pos, mixed))
+        qkv, gate_up, moved[1], mixed, kv_near = lax.optimization_barrier((qkv, gate_up, moved[1], mixed, kv_near))
         dctx = decode_combine(mixed)
+        kv_recv = lax.all_to_all(kv_near[:, :, None], 'tp', 1, 2, tiled=True)
         moved.append(pass_on(*moved[1], 3, tp))
         ctx = attend(s_len, qkv, step, seq_len - step, seq_len - step)
-        ctx, moved[2] = lax.optimization_barrier((ctx, moved[2]))
+        ctx, moved[2], kv_recv = lax.optimization_barrier((ctx, moved[2], kv_recv))
 
         done = layer_sums(ctx, dctx.reshape(-1, ctx.shape[1]), mine, [r for r, _ in moved], [l for _, l in moved], x, y_tok, mlp_gain, w_full, gate_up, w_down[0])
         done = done.reshape(CHUNKS, step + dec, width)
         hidden = done[:, :step].reshape(seq_len, width)
         tokens = done[:, step:].reshape(CHUNKS * dec, width)
 
-        kv_recv = lax.ppermute(kv_by_pos, 'side', send_pairs)
         return (hidden[None], tokens, kv_recv[0][None, None], kv_recv[1][None, None], key_now[None], value_now[None])
 
     cache_spec = P(None, group_axes, 'tp', None, None)

time: 1030 us -> 1010 us (0.981)
  starting transfers between devices: 47.6 us -> 29.6 us
  Pallas kernels: 819 us -> 808 us
    ppermute x3, waiting for transfers between devices: 0.01 us -> 20.8 us  [pass_on(): lax.ppermute(right, 'tp', [(place, place + 1) for place in range(hop - 1,...]
    ppermute x3, waiting for transfers between devices: 22.6 us -> 2.17 us  [pass_on(): lax.ppermute(left, 'tp', [(place, place - 1) for place in range(tp - hop,...]
    all_to_all x3, starting transfers between devices: 34.2 us -> 18.4 us  [the longest x1 8.48 us: device_fn(): mixed = lax.all_to_all(mixed, 'tp', 0, 0)]
    pallas_call x1, Pallas kernels: 719 us -> 708 us  [layer_sums(): pl.pallas_call(functools.partial(layer_kernel, geo), grid=(CHUNKS, out_ti...]
    optimization_barrier x1 -> x3, local copies, waits for them, and re-layouts: 45.3 us -> 45.6 us  [the longest x1 45.3 us: device_fn(): lax.optimization_barrier((w_gate_up, moved[0], mixed))]
  transfers between devices with their start and end apart: 11 -> 11, of which waited for: 2 -> 3; matrix products, arithmetic and copies ran while one was open for 8% -> 8% of each run, Pallas kernels for 10% -> 10%
where the time goes in v6:
time: 1010 us
  Pallas kernels  808 us (80%)
  local copies, waits for them, and re-layouts  70.3 us (7%)
  waiting for transfers between devices  56.8 us (6%)
  starting transfers between devices  29.6 us (3%)
  other arithmetic  23.6 us (2%)
  between operations  15 us (1%)
    pallas_call x1, Pallas kernels, layer_sums(): pl.pallas_call(functools.partial(layer_kernel, geo), grid=(CHUNKS, out_ti...  708 us
    pallas_call x2, Pallas kernels, attend(): pl.pallas_call(functools.partial(flash_kernel, block_q, block_k, some, ba...  70.9 us
    optimization_barrier x1, local copies, waits for them, and re-layouts, device_fn(): lax.optimization_barrier((w_gate_up, moved[0], mixed))  45.3 us
    all_to_all x1, waiting for transfers between devices, device_fn(): mixed = lax.all_to_all(mixed, 'tp', 0, 0)  33.8 us
    pallas_call x1, Pallas kernels, project_qkv(): pl.pallas_call(qkv_kernel, grid=(rows // rows_block,), in_specs=[pl.Block...  28.8 us
    ppermute x3, waiting for transfers between devices, pass_on(): lax.ppermute(right, 'tp', [(place, place + 1) for place in range(hop - 1,...  20.8 us
  transfers between devices with their start and end apart: 11, of which 3 were waited for; matrix products, arithmetic and copies ran while one was open for 8% of the time, Pallas kernels for 10%

profile of v6, /device:TPU:0, one launch (start us, length us, event | category | flops | bytes accessed | tf_op | source)
XLA Modules:
  0.0 1009.8 jit_solution(5648984394907460529)
XLA Ops:
  7.2 0.0 all-gather.3.cloned.1.call-start
  7.3 2.2 constant_dynamic-slice_fusion
  9.4 0.0 all-gather.3.cloned.1.call-update
  9.6 0.2 fusion.17
  9.7 0.1 multiply_cosine_fusion.1
  9.9 4.9 fusion.12
  14.8 0.1 subtract_convert_fusion
  14.9 0.1 maximum_bitcast_fusion
  15.0 0.8 broadcast_in_dim.75
  15.8 6.4 all-to-all-start
  22.8 3.7 fusion.20
  26.6 1.9 pad_maximum_fusion
  28.5 28.8 %project_qkv.1.q_ref.k_ref.v_ref = bf16[9,2048,128]{2,1,0:T(8,128)(2,1)} custom-call(bf16[2048,3584]{1,0:T(8,128)(2,1)} %bitcast.78, bf16[1,3584]{1,0:T(2,128)(2,1)} %gain_ref.2, f32[2048,128]{1,0:T(8,128)} %get-tuple-element.69.cos_ref, f32[2048,128]{1,0:T(8,128)} %get-tuple-element.70.sin_ref, bf16[9,3584,128]{2,1,0:T(8,128)(2,1)} %bitcast.68), custom_call_target="tpu_custom_call" | custom-call | flops 16911433728 | bytes 27656192 | tf_op jit(solution)/shard_map/project_qkv/pallas_call | solution.py:59
  57.3 0.1 broadcast_compare_fusion.1
  57.3 11.0 %attend.2.mine_hbm = bf16[512,896]{1,0:T(8,128)(2,1)} custom-call(s32[1]{0:T(128)} %copy.101.slen_ref, bf16[9,2048,128]{2,1,0:T(8,128)(2,1)} %project_qkv.1.q_ref.k_ref.v_ref, bf16[9,2048,128]{2,1,0:T(8,128)(2,1)} %project_qkv.1.q_ref.k_ref.v_ref, bf16[9,2048,128]{2,1,0:T(8,128)(2,1)} %project_qkv.1.q_ref.k_ref.v_ref), custom_call_target="tpu_custom_call" | custom-call | flops 704643072 | bytes 2097152 | tf_op jit(solution)/shard_map/attend/pallas_call | solution.py:227
  68.4 5.0 collective-permute-start
  73.4 1.3 collective-permute-start.1
  74.7 0.2 copy.69
  74.9 2.6 slice_multiply_fusion
  77.5 5.7 bitcast_select_fusion
  83.2 1.3 fusion.32
  84.5 0.4 fusion.15
  84.9 0.7 fusion.2
  85.6 0.1 select_maximum_fusion
  85.7 0.9 pad_maximum_fusion.2
  86.6 20.8 %collective-permute-done.right_hbm_0_ = bf16[512,896]{1,0:T(8,128)(2,1)} collective-permute-done((bf16[512,896]{1,0:T(8,128)(2,1)}, bf16[512,896]{1,0:T(8,128)(2,1)}, u32[]{:S(2)}, u32[]{:S(2)}) %collective-permute-start) | collective-permute-done | bytes 917536 | tf_op jit(solution)/shard_map/ppermute | solution.py:652
  107.4 2.2 collective-permute-done.1.left_hbm_0_
  109.6 1.6 collective-permute-start.2
  111.2 1.3 collective-permute-start.3
  112.5 8.5 all-to-all-start.1
  120.9 7.3 broadcast_select_fusion
  128.2 45.3 %copy.98 = bf16[1,3584,2,4736]{3,1,2,0:T(8,128)(2,1)} copy(bf16[1,3584,2,4736]{3,2,1,0:T(2,128)(2,1)} %param.22) | data formatting | bytes 135790592 | tf_op jit(solution)/shard_map/optimization_barrier | solution.py:693
  173.6 33.8 %all-to-all-done.1 = f32[4,32,8,128]{3,2,1,0:T(8,128)S(1)} async-done(((f32[4,32,8,128]{3,2,1,0:T(8,128)}), f32[4,32,8,128]{3,2,1,0:T(8,128)S(1)}, u32[]{:S(2)}, u32[]{:S(2)}) %all-to-all-start.1) | async-done | bytes 524320 | tf_op jit(solution)/shard_map/all_to_all | solution.py:694
  207.4 0.1 copy.79
  207.5 0.2 slice.55
  207.7 3.6 copy.77
  211.3 3.5 all-to-all-start.2
  214.9 0.2 multiply_reduce_fusion
  215.1 0.1 divide_convert_fusion
  215.2 0.6 copy.100
  215.9 0.7 collective-permute-start.5
  216.6 1.3 collective-permute-start.6
  217.9 59.9 %attend.3.ctx_hbm = bf16[1536,896]{1,0:T(8,128)(2,1)} custom-call(s32[1]{0:T(128)} %copy.101.slen_ref, bf16[9,2048,128]{2,1,0:T(8,128)(2,1)} %project_qkv.1.q_ref.k_ref.v_ref, bf16[9,2048,128]{2,1,0:T(8,128)(2,1)} %project_qkv.1.q_ref.k_ref.v_ref, bf16[9,2048,128]{2,1,0:T(8,128)(2,1)} %project_qkv.1.q_ref.k_ref.v_ref), custom_call_target="tpu_custom_call" | custom-call | flops 10569646080 | bytes 6291456 | tf_op jit(solution)/shard_map/attend/pallas_call | solution.py:227
  277.8 0.8 copy.99
  278.6 1.5 slice_bitcast_fusion
  280.2 707.8 %layer_sums.1 = (bf16[2080,3584]{1,0:T(8,128)(2,1)}, bf16[4,3,512,896]{3,2,1,0:T(8,128)(2,1)}, bf16[4,32,896]{2,1,0:T(8,128)(2,1)}, bf16[2080,3584]{1,0:T(8,128)(2,1)}) custom-call(bf16[1536,896]{1,0:T(8,128)(2,1)} %attend.3.ctx_hbm, bf16[32,896]{1,0:T(8,128)(2,1)} %bitcast.75, bf16[512,896]{1,0:T(8,128)(2,1)} %attend.2.mine_hbm, ...), custom_call_target="tpu_custom_call" | custom-call | flops 265268756480 | bytes 510132224 | tf_op jit(solution)/shard_map/layer_sums/pallas_call | solution.py:574
  988.0 13.3 %slice.67 = bf16[4,512,3584]{2,1,0:T(8,128)(2,1)} slice(bf16[4,520,3584]{2,1,0:T(8,128)(2,1)} %bitcast.65), slice={[0:4], [0:512], [0:3584]} | slice | bytes 29360128 | tf_op jit(solution)/shard_map/slice | solution.py:706
  1001.3 1.6 slice_bitcast_fusion.2
  (35 shorter events, 0.2 us)
Async XLA Ops:
  7.2 2.3 copy-start.3
  7.2 2.3 copy-start.2
  7.2 2.4 copy-start.1
  7.2 273.0 %all-gather.3.cloned.1.call-start = ((), (), s32[]{:S(2)}) async-start(), calls=%async_computation.3 | async-start | bytes 26492928 | tf_op jit(solution)/shard_map/all_gather | solution.py:660
  15.8 41.6 %all-to-all-start = ((bf16[4,32,9,128]{3,1,2,0:T(8,128)(2,1)}), bf16[4,32,9,128]{3,1,2,0:T(8,128)(2,1)S(1)}, u32[]{:S(2)}, u32[]{:S(2)}) async-start(bf16[4,32,9,128]{3,1,2,0:T(8,128)(2,1)} %broadcast_in_dim.75), calls=%async_computation | async-start | bytes 589824 | tf_op jit(solution)/shard_map/all_to_all | solution.py:681
  68.4 9.1 copy-start
  68.4 39.0 %collective-permute-start = (bf16[512,896]{1,0:T(8,128)(2,1)}, bf16[512,896]{1,0:T(8,128)(2,1)}, u32[]{:S(2)}, u32[]{:S(2)}) collective-permute-start(bf16[512,896]{1,0:T(8,128)(2,1)} %attend.2.mine_hbm), channel_id=1, source_target_pairs={{0,4},{4,8},{8,12},{1,5},{5,9},{9,13},{2,6},{6,10},{10,14},{3,7},{... | collective-permute-start | bytes 2752520 | tf_op jit(solution)/shard_map/ppermute | solution.py:652
  73.4 36.2 %collective-permute-start.1 = (bf16[512,896]{1,0:T(8,128)(2,1)}, bf16[512,896]{1,0:T(8,128)(2,1)}, u32[]{:S(2)}, u32[]{:S(2)}) collective-permute-start(bf16[512,896]{1,0:T(8,128)(2,1)} %attend.2.mine_hbm), channel_id=1, source_target_pairs={{12,8},{8,4},{4,0},{13,9},{9,5},{5,1},{14,10},{10,6},{6,2},{15,11}... | collective-permute-start | bytes 2752520 | tf_op jit(solution)/shard_map/ppermute | solution.py:653
  77.5 96.1 %collective-permute-start.4 = (bf16[2,2048,128]{2,1,0:T(8,128)(2,1)}, bf16[2,2048,128]{2,1,0:T(8,128)(2,1)}, u32[]{:S(2)}, u32[]{:S(2)}) collective-permute-start(bf16[2,2048,128]{2,1,0:T(8,128)(2,1)} %slice_multiply_fusion), channel_id=1, source_target_pairs={{0,1},{1,2},{2,3},{3,0},{4,5},{5,6},{6,7},{7,4},{8,9},{9,10},{10,1... | collective-permute-start | bytes 3145736 | tf_op jit(solution)/shard_map/ppermute | solution.py:692
  109.6 97.9 %collective-permute-start.2 = (bf16[512,896]{1,0:T(8,128)(2,1)}, bf16[512,896]{1,0:T(8,128)(2,1)}, u32[]{:S(2)}, u32[]{:S(2)}) collective-permute-start(bf16[512,896]{1,0:T(8,128)(2,1)} %collective-permute-done.right_hbm_0_), channel_id=1, source_target_pairs={{4,8},{8,12},{5,9},{9,13},{6,10},{10,14},{7,11},{11,15},{20,24},{2... | collective-permute-start | bytes 2752520 | tf_op jit(solution)/shard_map/ppermute | solution.py:652
  111.2 96.2 %collective-permute-start.3 = (bf16[512,896]{1,0:T(8,128)(2,1)}, bf16[512,896]{1,0:T(8,128)(2,1)}, u32[]{:S(2)}, u32[]{:S(2)}) collective-permute-start(bf16[512,896]{1,0:T(8,128)(2,1)} %collective-permute-done.1.left_hbm_0_), channel_id=1, source_target_pairs={{8,4},{4,0},{9,5},{5,1},{10,6},{6,2},{11,7},{7,3},{24,20},{20,16},... | collective-permute-start | bytes 2752520 | tf_op jit(solution)/shard_map/ppermute | solution.py:653
  112.5 94.9 %all-to-all-start.1 = ((f32[4,32,8,128]{3,2,1,0:T(8,128)}), f32[4,32,8,128]{3,2,1,0:T(8,128)S(1)}, u32[]{:S(2)}, u32[]{:S(2)}) async-start(f32[4,32,8,128]{3,2,1,0:T(8,128)} %pad_maximum_fusion.2), calls=%async_computation.1 | async-start | bytes 1048576 | tf_op jit(solution)/shard_map/all_to_all | solution.py:694
  211.3 66.4 %all-to-all-start.2 = ((bf16[2,2048,1,128]{3,0,2,1:T(2,128)(2,1)}), bf16[2,2048,1,128]{3,0,2,1:T(2,128)(2,1)S(1)}, u32[]{:S(2)}, u32[]{:S(2)}) async-start(bf16[2,2048,1,128]{3,0,2,1:T(2,128)(2,1)} %copy.77), calls=%async_computation.2 | async-start | bytes 2097152 | tf_op jit(solution)/shard_map/all_to_all | solution.py:699
  215.9 62.7 %collective-permute-start.5 = (bf16[512,896]{1,0:T(8,128)(2,1)}, bf16[512,896]{1,0:T(8,128)(2,1)S(1)}, u32[]{:S(2)}, u32[]{:S(2)}) collective-permute-start(bf16[512,896]{1,0:T(8,128)(2,1)} %collective-permute-done.2.right_hbm_1_), channel_id=1, source_target_pairs={{8,12},{9,13},{10,14},{11,15},{24,28},{25,29},{26,30},{27,31}} | collective-permute-start | bytes 2752520 | tf_op jit(solution)/shard_map/ppermute | solution.py:652
  216.6 62.0 %collective-permute-start.6 = (bf16[512,896]{1,0:T(8,128)(2,1)}, bf16[512,896]{1,0:T(8,128)(2,1)S(1)}, u32[]{:S(2)}, u32[]{:S(2)}) collective-permute-start(bf16[512,896]{1,0:T(8,128)(2,1)} %collective-permute-done.3.left_hbm_1_), channel_id=1, source_target_pairs={{4,0},{5,1},{6,2},{7,3},{20,16},{21,17},{22,18},{23,19}} | collective-permute-start | bytes 2752520 | tf_op jit(solution)/shard_map/ppermute | solution.py:653
  278.6 1.6 copy-start.4
  278.6 1.6 copy-start.5
Sparse Core Ops, SparseCore 0:
  10.8 205.6 all-gather.2

commit v7 on v6

--- a/solution.py
+++ b/solution.py
@@ -53,7 +53,7 @@
             o_ref[s] = part.astype(BF)
 
 
-def project_qkv(x, gain, cos, sin, w, rows_block=256):
+def project_qkv(x, gain, cos, sin, w, rows_block=512):
     rows, width = x.shape
     slots, _, head = w.shape
     return pl.pallas_call(
@@ -690,15 +690,18 @@
         full_qkv, mine = lax.optimization_barrier((full_qkv, mine))
         mixed, key_now, value_now = decode_local(full_qkv, c_len, k_cache[0], v_cache[0])
         kv_near = lax.ppermute(kv_pair, 'side', send_pairs)
-        w_gate_up, moved[0], mixed = lax.optimization_barrier((w_gate_up, moved[0], mixed))
+        w_gate_up, moved[0], mixed, value_now = lax.optimization_barrier((w_gate_up, moved[0], mixed, value_now))
         mixed = lax.all_to_all(mixed, 'tp', 0, 0)
         moved.append(pass_on(*moved[0], 2, tp))
         gate_up = jnp.transpose(w_gate_up[0], (1, 0, 2))
-        qkv, gate_up, moved[1], mixed, kv_near = lax.optimization_barrier((qkv, gate_up, moved[1], mixed, kv_near))
+        qkv, gate_up = lax.optimization_barrier((qkv, gate_up))
+        rest = seq_len - step
+        ctx = attend(s_len, qkv, step, rest - step, rest)
+        ctx, moved[1], mixed, kv_near = lax.optimization_barrier((ctx, moved[1], mixed, kv_near))
         dctx = decode_combine(mixed)
         kv_recv = lax.all_to_all(kv_near[:, :, None], 'tp', 1, 2, tiled=True)
         moved.append(pass_on(*moved[1], 3, tp))
-        ctx = attend(s_len, qkv, step, seq_len - step, seq_len - step)
+        ctx = attend(s_len, qkv, rest, step, rest, ctx)
         ctx, moved[2], kv_recv = lax.optimization_barrier((ctx, moved[2], kv_recv))
 
         done = layer_sums(ctx, dctx.reshape(-1, ctx.shape[1]), mine, [r for r, _ in moved], [l for _, l in moved], x, y_tok, mlp_gain, w_full, gate_up, w_down[0])

time: 1010 us -> 985 us (0.975)
  waiting for transfers between devices: 56.8 us -> 30.1 us
    all_to_all x1, waiting for transfers between devices: 33.8 us -> 6.49 us  [device_fn(): mixed = lax.all_to_all(mixed, 'tp', 0, 0)]
    pallas_call x2 -> x3, Pallas kernels: 70.9 us -> 73 us  [attend(): pl.pallas_call(functools.partial(flash_kernel, block_q, block_k, some, ba...]
  transfers between devices with their start and end apart: 11 -> 11, of which waited for: 3 -> 4; matrix products, arithmetic and copies ran while one was open for 8% -> 8% of each run, Pallas kernels for 10% -> 10%
where the time goes in v7:
time: 985 us; the launch traced here: 984 us
  Pallas kernels  809 us (82%)
  local copies, waits for them, and re-layouts  71.3 us (7%)
  starting transfers between devices  30.3 us (3%)
  waiting for transfers between devices  30.1 us (3%)
  other arithmetic  20.9 us (2%)
  between operations  15 us (2%)
    pallas_call x1, Pallas kernels, layer_sums(): pl.pallas_call(functools.partial(layer_kernel, geo), grid=(CHUNKS, out_ti...  707 us
    pallas_call x3, Pallas kernels, attend(): pl.pallas_call(functools.partial(flash_kernel, block_q, block_k, some, ba...  73 us
    optimization_barrier x1, local copies, waits for them, and re-layouts, device_fn(): lax.optimization_barrier((w_gate_up, moved[0], mixed, value_now))  45.3 us
    pallas_call x1, Pallas kernels, project_qkv(): pl.pallas_call(qkv_kernel, grid=(rows // rows_block,), in_specs=[pl.Block...  28.8 us
    ppermute x3, waiting for transfers between devices, pass_on(): lax.ppermute(right, 'tp', [(place, place + 1) for place in range(hop - 1,...  20.8 us
  transfers between devices with their start and end apart: 11, of which 4 were waited for; matrix products, arithmetic and copies ran while one was open for 8% of the time, Pallas kernels for 10%

profile of v7, /device:TPU:0, one launch (start us, length us, event | category | flops | bytes accessed | tf_op | source)
XLA Modules:
  0.0 983.7 jit_solution(1223854937668391812)
XLA Ops:
  7.3 2.2 constant_dynamic-slice_fusion
  9.6 0.2 fusion.17
  9.7 0.1 multiply_cosine_fusion.1
  9.9 4.9 fusion.12
  14.8 0.1 subtract_convert_fusion
  14.9 0.1 maximum_bitcast_fusion
  15.0 0.8 broadcast_in_dim.75
  15.8 6.4 all-to-all-start
  22.8 3.7 fusion.20
  26.6 1.9 pad_maximum_fusion
  28.5 28.8 %project_qkv.1.q_ref.k_ref.v_ref = bf16[9,2048,128]{2,1,0:T(8,128)(2,1)} custom-call(bf16[2048,3584]{1,0:T(8,128)(2,1)} %bitcast.79, bf16[1,3584]{1,0:T(2,128)(2,1)} %gain_ref.2, f32[2048,128]{1,0:T(8,128)} %get-tuple-element.71.cos_ref, f32[2048,128]{1,0:T(8,128)} %get-tuple-element.72.sin_ref, bf16[9,3584,128]{2,1,0:T(8,128)(2,1)} %bitcast.70), custom_call_target="tpu_custom_call" | custom-call | flops 16911433728 | bytes 27656192 | tf_op jit(solution)/shard_map/project_qkv/pallas_call | solution.py:59
  57.3 0.1 broadcast_compare_fusion.1
  57.4 11.0 %attend.3.mine_hbm = bf16[512,896]{1,0:T(8,128)(2,1)} custom-call(s32[1]{0:T(128)} %copy.98.slen_ref, bf16[9,2048,128]{2,1,0:T(8,128)(2,1)} %project_qkv.1.q_ref.k_ref.v_ref, bf16[9,2048,128]{2,1,0:T(8,128)(2,1)} %project_qkv.1.q_ref.k_ref.v_ref, bf16[9,2048,128]{2,1,0:T(8,128)(2,1)} %project_qkv.1.q_ref.k_ref.v_ref), custom_call_target="tpu_custom_call" | custom-call | flops 704643072 | bytes 2097152 | tf_op jit(solution)/shard_map/attend/pallas_call | solution.py:227
  68.4 5.0 collective-permute-start
  73.4 1.3 collective-permute-start.1
  74.7 0.2 copy.66
  74.9 2.5 slice_multiply_fusion
  77.5 5.7 bitcast_select_fusion
  83.2 1.3 fusion.32
  84.5 0.4 fusion.15
  84.9 0.7 fusion.2
  85.6 0.1 select_maximum_fusion
  85.7 0.9 pad_maximum_fusion.2
  86.6 20.8 %collective-permute-done.right_hbm_0_ = bf16[512,896]{1,0:T(8,128)(2,1)} collective-permute-done((bf16[512,896]{1,0:T(8,128)(2,1)}, bf16[512,896]{1,0:T(8,128)(2,1)}, u32[]{:S(2)}, u32[]{:S(2)}) %collective-permute-start) | collective-permute-done | bytes 917536 | tf_op jit(solution)/shard_map/ppermute | solution.py:652
  107.4 2.2 collective-permute-done.1.left_hbm_0_
  109.5 1.6 collective-permute-start.2
  111.2 1.3 collective-permute-start.3
  112.4 8.5 all-to-all-start.1
  120.9 45.3 %copy.94 = bf16[1,3584,2,4736]{3,1,2,0:T(8,128)(2,1)} copy(bf16[1,3584,2,4736]{3,2,1,0:T(2,128)(2,1)} %param.22) | data formatting | bytes 135790592 | tf_op jit(solution)/shard_map/optimization_barrier | solution.py:693
  166.3 34.6 %attend.4.refs_0_ = bf16[1536,896]{1,0:T(8,128)(2,1)} custom-call(s32[1]{0:T(128)} %copy.98.slen_ref, bf16[9,2048,128]{2,1,0:T(8,128)(2,1)} %project_qkv.1.q_ref.k_ref.v_ref, bf16[9,2048,128]{2,1,0:T(8,128)(2,1)} %project_qkv.1.q_ref.k_ref.v_ref, bf16[9,2048,128]{2,1,0:T(8,128)(2,1)} %project_qkv.1.q_ref.k_ref.v_ref), custom_call_target="tpu_custom_call" | custom-call | flops 5637144576 | bytes 4194304 | tf_op jit(solution)/shard_map/attend/pallas_call | solution.py:227
  200.9 6.5 all-to-all-done.1
  207.4 3.6 copy.74
  211.0 4.3 all-to-all-start.2
  215.3 4.6 broadcast_select_fusion
  219.8 0.1 copy.76
  220.0 0.2 slice.55
  220.2 0.7 collective-permute-start.5
  220.9 1.3 collective-permute-start.6
  222.2 0.2 multiply_reduce_fusion
  222.4 0.1 divide_convert_fusion
  222.6 0.6 copy.96
  223.2 27.3 %attend.5.ctx_hbm = bf16[1536,896]{1,0:T(8,128)(2,1)} custom-call(s32[1]{0:T(128)} %copy.98.slen_ref, bf16[9,2048,128]{2,1,0:T(8,128)(2,1)} %project_qkv.1.q_ref.k_ref.v_ref, bf16[9,2048,128]{2,1,0:T(8,128)(2,1)} %project_qkv.1.q_ref.k_ref.v_ref, bf16[9,2048,128]{2,1,0:T(8,128)(2,1)} %project_qkv.1.q_ref.k_ref.v_ref, ...), custom_call_target="tpu_custom_call", output_to_operand_aliasing={{}: (4, {})} | custom-call | flops 4932501504 | bytes 2097152 | tf_op jit(solution)/shard_map/attend/pallas_call | solution.py:227
  250.5 2.0 copy.95
  252.6 0.6 collective-permute-done.6.left_hbm_2_
  253.2 1.3 slice_bitcast_fusion
  254.5 707.5 %layer_sums.1 = (bf16[2080,3584]{1,0:T(8,128)(2,1)}, bf16[4,3,512,896]{3,2,1,0:T(8,128)(2,1)}, bf16[4,32,896]{2,1,0:T(8,128)(2,1)}, bf16[2080,3584]{1,0:T(8,128)(2,1)}) custom-call(bf16[1536,896]{1,0:T(8,128)(2,1)} %attend.5.ctx_hbm, bf16[32,896]{1,0:T(8,128)(2,1)} %bitcast.76, bf16[512,896]{1,0:T(8,128)(2,1)} %attend.3.mine_hbm, ...), custom_call_target="tpu_custom_call" | custom-call | flops 265268756480 | bytes 510132224 | tf_op jit(solution)/shard_map/layer_sums/pallas_call | solution.py:574
  962.0 13.3 %slice.67 = bf16[4,512,3584]{2,1,0:T(8,128)(2,1)} slice(bf16[4,520,3584]{2,1,0:T(8,128)(2,1)} %bitcast.66), slice={[0:4], [0:512], [0:3584]} | slice | bytes 29360128 | tf_op jit(solution)/shard_map/slice | solution.py:709
  975.2 1.6 slice_bitcast_fusion.2
  (38 shorter events, 0.3 us)
Async XLA Ops:
  7.2 2.3 copy-start.4
  7.2 2.3 copy-start.3
  7.2 2.4 copy-start.2
  7.2 247.3 %all-gather.3.cloned.1.call-start = ((), (), s32[]{:S(2)}) async-start(), calls=%async_computation.3 | async-start | bytes 26492928 | tf_op jit(solution)/shard_map/all_gather | solution.py:660
  15.8 41.6 %all-to-all-start = ((bf16[4,32,9,128]{3,1,2,0:T(8,128)(2,1)}), bf16[4,32,9,128]{3,1,2,0:T(8,128)(2,1)S(1)}, u32[]{:S(2)}, u32[]{:S(2)}) async-start(bf16[4,32,9,128]{3,1,2,0:T(8,128)(2,1)} %broadcast_in_dim.75), calls=%async_computation | async-start | bytes 589824 | tf_op jit(solution)/shard_map/all_to_all | solution.py:681
  68.4 9.0 copy-start
  68.4 39.0 %collective-permute-start = (bf16[512,896]{1,0:T(8,128)(2,1)}, bf16[512,896]{1,0:T(8,128)(2,1)}, u32[]{:S(2)}, u32[]{:S(2)}) collective-permute-start(bf16[512,896]{1,0:T(8,128)(2,1)} %attend.3.mine_hbm), channel_id=1, source_target_pairs={{0,4},{4,8},{8,12},{1,5},{5,9},{9,13},{2,6},{6,10},{10,14},{3,7},{... | collective-permute-start | bytes 2752520 | tf_op jit(solution)/shard_map/ppermute | solution.py:652
  73.4 36.1 %collective-permute-start.1 = (bf16[512,896]{1,0:T(8,128)(2,1)}, bf16[512,896]{1,0:T(8,128)(2,1)}, u32[]{:S(2)}, u32[]{:S(2)}) collective-permute-start(bf16[512,896]{1,0:T(8,128)(2,1)} %attend.3.mine_hbm), channel_id=1, source_target_pairs={{12,8},{8,4},{4,0},{13,9},{9,5},{5,1},{14,10},{10,6},{6,2},{15,11}... | collective-permute-start | bytes 2752520 | tf_op jit(solution)/shard_map/ppermute | solution.py:653
  77.4 123.5 %collective-permute-start.4 = (bf16[2,2048,128]{2,1,0:T(8,128)(2,1)}, bf16[2,2048,128]{2,1,0:T(8,128)(2,1)}, u32[]{:S(2)}, u32[]{:S(2)}) collective-permute-start(bf16[2,2048,128]{2,1,0:T(8,128)(2,1)} %slice_multiply_fusion), channel_id=1, source_target_pairs={{0,1},{1,2},{2,3},{3,0},{4,5},{5,6},{6,7},{7,4},{8,9},{9,10},{10,1... | collective-permute-start | bytes 3145736 | tf_op jit(solution)/shard_map/ppermute | solution.py:692
  83.2 2.4 copy-start.1
  109.5 97.9 %collective-permute-start.2 = (bf16[512,896]{1,0:T(8,128)(2,1)}, bf16[512,896]{1,0:T(8,128)(2,1)}, u32[]{:S(2)}, u32[]{:S(2)}) collective-permute-start(bf16[512,896]{1,0:T(8,128)(2,1)} %collective-permute-done.right_hbm_0_), channel_id=1, source_target_pairs={{4,8},{8,12},{5,9},{9,13},{6,10},{10,14},{7,11},{11,15},{20,24},{2... | collective-permute-start | bytes 2752520 | tf_op jit(solution)/shard_map/ppermute | solution.py:652
  111.2 96.2 %collective-permute-start.3 = (bf16[512,896]{1,0:T(8,128)(2,1)}, bf16[512,896]{1,0:T(8,128)(2,1)}, u32[]{:S(2)}, u32[]{:S(2)}) collective-permute-start(bf16[512,896]{1,0:T(8,128)(2,1)} %collective-permute-done.1.left_hbm_0_), channel_id=1, source_target_pairs={{8,4},{4,0},{9,5},{5,1},{10,6},{6,2},{11,7},{7,3},{24,20},{20,16},... | collective-permute-start | bytes 2752520 | tf_op jit(solution)/shard_map/ppermute | solution.py:653
  112.4 95.0 %all-to-all-start.1 = ((f32[4,32,8,128]{3,2,1,0:T(8,128)}), f32[4,32,8,128]{3,2,1,0:T(8,128)S(1)}, u32[]{:S(2)}, u32[]{:S(2)}) async-start(f32[4,32,8,128]{3,2,1,0:T(8,128)} %pad_maximum_fusion.2), calls=%async_computation.1 | async-start | bytes 1048576 | tf_op jit(solution)/shard_map/all_to_all | solution.py:694
  211.0 39.5 %all-to-all-start.2 = ((bf16[2,2048,1,128]{3,0,2,1:T(2,128)(2,1)}), bf16[2,2048,1,128]{3,0,2,1:T(2,128)(2,1)}, u32[]{:S(2)}, u32[]{:S(2)}) async-start(bf16[2,2048,1,128]{3,0,2,1:T(2,128)(2,1)} %copy.74), calls=%async_computation.2 | async-start | bytes 2097152 | tf_op jit(solution)/shard_map/all_to_all | solution.py:702
  220.2 32.4 %collective-permute-start.5 = (bf16[512,896]{1,0:T(8,128)(2,1)}, bf16[512,896]{1,0:T(8,128)(2,1)S(1)}, u32[]{:S(2)}, u32[]{:S(2)}) collective-permute-start(bf16[512,896]{1,0:T(8,128)(2,1)} %collective-permute-done.2.right_hbm_1_), channel_id=1, source_target_pairs={{8,12},{9,13},{10,14},{11,15},{24,28},{25,29},{26,30},{27,31}} | collective-permute-start | bytes 2752520 | tf_op jit(solution)/shard_map/ppermute | solution.py:652
  220.9 32.3 %collective-permute-start.6 = (bf16[512,896]{1,0:T(8,128)(2,1)}, bf16[512,896]{1,0:T(8,128)(2,1)S(1)}, u32[]{:S(2)}, u32[]{:S(2)}) collective-permute-start(bf16[512,896]{1,0:T(8,128)(2,1)} %collective-permute-done.3.left_hbm_1_), channel_id=1, source_target_pairs={{4,0},{5,1},{6,2},{7,3},{20,16},{21,17},{22,18},{23,19}} | collective-permute-start | bytes 2752520 | tf_op jit(solution)/shard_map/ppermute | solution.py:653
  252.6 1.9 copy-start.5
  253.2 1.3 copy-start.6
Sparse Core Ops, SparseCore 0:
  10.8 205.5 all-gather.2

commit v8 on v6

--- a/solution.py
+++ b/solution.py
@@ -216,12 +216,12 @@
         o_ref[:, h * head:(h + 1) * head] = (acc_ref[here] / jnp.sum(l_ref[here], axis=-1, keepdims=True)).astype(BF)
 
 
-def attend(slen, qkv, first, count, total, into=None, block_q=256, block_k=512, some=32):
+def attend(slen, qkv, first, count, origin, total, into=None, block_q=256, block_k=512, some=32):
     slots, rows, head = qkv.shape
     heads = slots - 2
     tall = heads * block_q
     base = first // block_q
-    place = 0 if into is None else (total - count) // block_q
+    place = (first - origin) // block_q
     more = [] if into is None else [into]
     share = (first + count) ** 2 - first ** 2
     return pl.pallas_call(
@@ -684,21 +684,25 @@
         qkv = project_qkv(x, attn_gain, cos, sin, w_slots)
         qkv, full_qkv = lax.optimization_barrier((qkv, full_qkv))
         step, dec = seq_len // CHUNKS, y_tok.shape[0] // CHUNKS
-        mine = attend(s_len, qkv, 0, step, step)
+        mine = attend(s_len, qkv, 0, step, 0, step)
         moved = [pass_on(mine, mine, 1, tp)]
         kv_pair = qkv[group_q:] * keep_mask
         full_qkv, mine = lax.optimization_barrier((full_qkv, mine))
         mixed, key_now, value_now = decode_local(full_qkv, c_len, k_cache[0], v_cache[0])
         kv_near = lax.ppermute(kv_pair, 'side', send_pairs)
-        w_gate_up, moved[0], mixed = lax.optimization_barrier((w_gate_up, moved[0], mixed))
+        late = seq_len - step
+        ctx = attend(s_len, qkv, step, step, step, late)
+        w_gate_up, moved[0], mixed, value_now, ctx = lax.optimization_barrier((w_gate_up, moved[0], mixed, value_now, ctx))
         mixed = lax.all_to_all(mixed, 'tp', 0, 0)
         moved.append(pass_on(*moved[0], 2, tp))
         gate_up = jnp.transpose(w_gate_up[0], (1, 0, 2))
-        qkv, gate_up, moved[1], mixed, kv_near = lax.optimization_barrier((qkv, gate_up, moved[1], mixed, kv_near))
+        qkv, gate_up, ctx = lax.optimization_barrier((qkv, gate_up, ctx))
+        ctx = attend(s_len, qkv, late, step, step, late, ctx)
+        ctx, moved[1], mixed, kv_near = lax.optimization_barrier((ctx, moved[1], mixed, kv_near))
         dctx = decode_combine(mixed)
         kv_recv = lax.all_to_all(kv_near[:, :, None], 'tp', 1, 2, tiled=True)
         moved.append(pass_on(*moved[1], 3, tp))
-        ctx = attend(s_len, qkv, step, seq_len - step, seq_len - step)
+        ctx = attend(s_len, qkv, 2 * step, late - 2 * step, step, late, ctx)
         ctx, moved[2], kv_recv = lax.optimization_barrier((ctx, moved[2], kv_recv))
 
         done = layer_sums(ctx, dctx.reshape(-1, ctx.shape[1]), mine, [r for r, _ in moved], [l for _, l in moved], x, y_tok, mlp_gain, w_full, gate_up, w_down[0])

time: 1010 us -> 984 us (0.974)
  waiting for transfers between devices: 56.8 us -> 25.3 us
    all_to_all x1, waiting for transfers between devices: 33.8 us -> 13.9 us  [device_fn(): mixed = lax.all_to_all(mixed, 'tp', 0, 0)]
    ppermute x3, waiting for transfers between devices: 20.8 us -> 2.08 us  [pass_on(): lax.ppermute(right, 'tp', [(place, place + 1) for place in range(hop - 1,...]
    pallas_call x2 -> x4, Pallas kernels: 70.9 us -> 75.1 us  [attend(): pl.pallas_call(functools.partial(flash_kernel, block_q, block_k, some, ba...]
  transfers between devices with their start and end apart: 11 -> 11, of which waited for: 3 -> 4; matrix products, arithmetic and copies ran while one was open for 8% -> 9% of each run, Pallas kernels for 10% -> 11%
where the time goes in v8:
time: 984 us; the launch traced here: 983 us
  Pallas kernels  811 us (82%)
  local copies, waits for them, and re-layouts  71.2 us (7%)
  starting transfers between devices  30.3 us (3%)
  waiting for transfers between devices  25.3 us (3%)
  other arithmetic  22.1 us (2%)
  between operations  15 us (2%)
    pallas_call x1, Pallas kernels, layer_sums(): pl.pallas_call(functools.partial(layer_kernel, geo), grid=(CHUNKS, out_ti...  707 us
    pallas_call x4, Pallas kernels, attend(): pl.pallas_call(functools.partial(flash_kernel, block_q, block_k, some, ba...  75.1 us
    optimization_barrier x1, local copies, waits for them, and re-layouts, device_fn(): lax.optimization_barrier((w_gate_up, moved[0], mixed, value_now, ctx))  45.2 us
    pallas_call x1, Pallas kernels, project_qkv(): pl.pallas_call(qkv_kernel, grid=(rows // rows_block,), in_specs=[pl.Block...  28.8 us
  transfers between devices with their start and end apart: 11, of which 4 were waited for; matrix products, arithmetic and copies ran while one was open for 9% of the time, Pallas kernels for 11%

profile of v8, /device:TPU:0, one launch (start us, length us, event | category | flops | bytes accessed | tf_op | source)
XLA Modules:
  0.0 983.1 jit_solution(4315402610192024501)
XLA Ops:
  7.3 2.2 constant_dynamic-slice_fusion
  9.6 0.2 fusion.17
  9.7 0.1 multiply_cosine_fusion.1
  9.9 4.9 fusion.12
  14.8 0.1 subtract_convert_fusion
  14.9 0.1 maximum_bitcast_fusion
  15.0 0.8 broadcast_in_dim.75
  15.8 6.4 all-to-all-start
  22.8 3.7 fusion.20
  26.6 1.9 pad_maximum_fusion
  28.5 28.8 %project_qkv.1.q_ref.k_ref.v_ref = bf16[9,2048,128]{2,1,0:T(8,128)(2,1)} custom-call(bf16[2048,3584]{1,0:T(8,128)(2,1)} %bitcast.79, bf16[1,3584]{1,0:T(2,128)(2,1)} %gain_ref.2, f32[2048,128]{1,0:T(8,128)} %get-tuple-element.75.cos_ref, f32[2048,128]{1,0:T(8,128)} %get-tuple-element.76.sin_ref, bf16[9,3584,128]{2,1,0:T(8,128)(2,1)} %bitcast.70), custom_call_target="tpu_custom_call" | custom-call | flops 16911433728 | bytes 27656192 | tf_op jit(solution)/shard_map/project_qkv/pallas_call | solution.py:59
  57.4 11.0 %attend.4.mine_hbm = bf16[512,896]{1,0:T(8,128)(2,1)} custom-call(s32[1]{0:T(128)} %copy.100.slen_ref, bf16[9,2048,128]{2,1,0:T(8,128)(2,1)} %project_qkv.1.q_ref.k_ref.v_ref, bf16[9,2048,128]{2,1,0:T(8,128)(2,1)} %project_qkv.1.q_ref.k_ref.v_ref, bf16[9,2048,128]{2,1,0:T(8,128)(2,1)} %project_qkv.1.q_ref.k_ref.v_ref), custom_call_target="tpu_custom_call" | custom-call | flops 704643072 | bytes 2097152 | tf_op jit(solution)/shard_map/attend/pallas_call | solution.py:227
  68.4 5.0 collective-permute-start
  73.4 1.3 collective-permute-start.1
  74.7 0.2 copy.67
  74.9 2.5 slice_multiply_fusion
  77.4 6.9 bitcast_select_fusion
  84.4 1.3 fusion.32
  85.6 0.4 fusion.15
  86.0 15.9 %attend.5.refs_0_ = bf16[1536,896]{1,0:T(8,128)(2,1)} custom-call(s32[1]{0:T(128)} %copy.100.slen_ref, bf16[9,2048,128]{2,1,0:T(8,128)(2,1)} %project_qkv.1.q_ref.k_ref.v_ref, bf16[9,2048,128]{2,1,0:T(8,128)(2,1)} %project_qkv.1.q_ref.k_ref.v_ref, bf16[9,2048,128]{2,1,0:T(8,128)(2,1)} %project_qkv.1.q_ref.k_ref.v_ref), custom_call_target="tpu_custom_call" | custom-call | flops 2113929216 | bytes 2097152 | tf_op jit(solution)/shard_map/attend/pallas_call | solution.py:227
  102.0 2.3 fusion.2
  104.3 0.1 select_maximum_fusion
  104.4 0.9 pad_maximum_fusion.2
  105.3 2.1 collective-permute-done.right_hbm_0_
  107.4 2.2 collective-permute-done.1.left_hbm_0_
  109.5 1.6 collective-permute-start.2
  111.1 1.3 collective-permute-start.3
  112.4 8.5 all-to-all-start.1
  120.9 45.2 %copy.95 = bf16[1,3584,2,4736]{3,1,2,0:T(8,128)(2,1)} copy(bf16[1,3584,2,4736]{3,2,1,0:T(2,128)(2,1)} %param.22) | data formatting | bytes 135790592 | tf_op jit(solution)/shard_map/optimization_barrier | solution.py:695
  166.1 27.3 %attend.6.refs_0_ = bf16[1536,896]{1,0:T(8,128)(2,1)} custom-call(s32[1]{0:T(128)} %copy.100.slen_ref, bf16[9,2048,128]{2,1,0:T(8,128)(2,1)} %project_qkv.1.q_ref.k_ref.v_ref, bf16[9,2048,128]{2,1,0:T(8,128)(2,1)} %project_qkv.1.q_ref.k_ref.v_ref, bf16[9,2048,128]{2,1,0:T(8,128)(2,1)} %project_qkv.1.q_ref.k_ref.v_ref, ...), custom_call_target="tpu_custom_call", output_to_operand_aliasing={{}: (4, {})} | custom-call | flops 4932501504 | bytes 2097152 | tf_op jit(solution)/shard_map/attend/pallas_call | solution.py:227
  193.5 13.9 %all-to-all-done.1 = f32[4,32,8,128]{3,2,1,0:T(8,128)S(1)} async-done(((f32[4,32,8,128]{3,2,1,0:T(8,128)}), f32[4,32,8,128]{3,2,1,0:T(8,128)S(1)}, u32[]{:S(2)}, u32[]{:S(2)}) %all-to-all-start.1) | async-done | bytes 524320 | tf_op jit(solution)/shard_map/all_to_all | solution.py:696
  207.4 3.6 copy.75
  211.0 4.2 all-to-all-start.2
  215.3 4.6 broadcast_select_fusion
  219.8 0.1 copy.77
  219.9 0.2 slice.55
  220.1 0.7 collective-permute-start.5
  220.9 1.3 collective-permute-start.6
  222.2 0.2 multiply_reduce_fusion
  222.4 0.1 divide_convert_fusion
  222.5 0.6 copy.97
  223.2 20.8 %attend.7.ctx_hbm = bf16[1536,896]{1,0:T(8,128)(2,1)} custom-call(s32[1]{0:T(128)} %copy.100.slen_ref, bf16[9,2048,128]{2,1,0:T(8,128)(2,1)} %project_qkv.1.q_ref.k_ref.v_ref, bf16[9,2048,128]{2,1,0:T(8,128)(2,1)} %project_qkv.1.q_ref.k_ref.v_ref, bf16[9,2048,128]{2,1,0:T(8,128)(2,1)} %project_qkv.1.q_ref.k_ref.v_ref, ...), custom_call_target="tpu_custom_call", output_to_operand_aliasing={{}: (4, {})} | custom-call | flops 3523215360 | bytes 2097152 | tf_op jit(solution)/shard_map/attend/pallas_call | solution.py:227
  243.9 2.0 copy.96
  246.0 7.1 collective-permute-done.6.left_hbm_2_
  253.1 1.3 slice_bitcast_fusion
  254.5 706.9 %layer_sums.1 = (bf16[2080,3584]{1,0:T(8,128)(2,1)}, bf16[4,3,512,896]{3,2,1,0:T(8,128)(2,1)}, bf16[4,32,896]{2,1,0:T(8,128)(2,1)}, bf16[2080,3584]{1,0:T(8,128)(2,1)}) custom-call(bf16[1536,896]{1,0:T(8,128)(2,1)} %attend.7.ctx_hbm, bf16[32,896]{1,0:T(8,128)(2,1)} %bitcast.76, bf16[512,896]{1,0:T(8,128)(2,1)} %attend.4.mine_hbm, ...), custom_call_target="tpu_custom_call" | custom-call | flops 265268756480 | bytes 510132224 | tf_op jit(solution)/shard_map/layer_sums/pallas_call | solution.py:574
  961.4 13.3 %slice.67 = bf16[4,512,3584]{2,1,0:T(8,128)(2,1)} slice(bf16[4,520,3584]{2,1,0:T(8,128)(2,1)} %bitcast.66), slice={[0:4], [0:512], [0:3584]} | slice | bytes 29360128 | tf_op jit(solution)/shard_map/slice | solution.py:710
  974.6 1.6 slice_bitcast_fusion.2
  (37 shorter events, 0.4 us)
Async XLA Ops:
  7.2 2.3 copy-start.3
  7.2 2.3 copy-start.2
  7.2 2.4 copy-start.1
  7.2 247.3 %all-gather.3.cloned.1.call-start = ((), (), s32[]{:S(2)}) async-start(), calls=%async_computation.3 | async-start | bytes 26492928 | tf_op jit(solution)/shard_map/all_gather | solution.py:660
  15.8 41.6 %all-to-all-start = ((bf16[4,32,9,128]{3,1,2,0:T(8,128)(2,1)}), bf16[4,32,9,128]{3,1,2,0:T(8,128)(2,1)S(1)}, u32[]{:S(2)}, u32[]{:S(2)}) async-start(bf16[4,32,9,128]{3,1,2,0:T(8,128)(2,1)} %broadcast_in_dim.75), calls=%async_computation | async-start | bytes 589824 | tf_op jit(solution)/shard_map/all_to_all | solution.py:681
  68.4 9.0 copy-start
  68.4 39.0 %collective-permute-start = (bf16[512,896]{1,0:T(8,128)(2,1)}, bf16[512,896]{1,0:T(8,128)(2,1)}, u32[]{:S(2)}, u32[]{:S(2)}) collective-permute-start(bf16[512,896]{1,0:T(8,128)(2,1)} %attend.4.mine_hbm), channel_id=1, source_target_pairs={{0,4},{4,8},{8,12},{1,5},{5,9},{9,13},{2,6},{6,10},{10,14},{3,7},{... | collective-permute-start | bytes 2752520 | tf_op jit(solution)/shard_map/ppermute | solution.py:652
  73.4 36.1 %collective-permute-start.1 = (bf16[512,896]{1,0:T(8,128)(2,1)}, bf16[512,896]{1,0:T(8,128)(2,1)}, u32[]{:S(2)}, u32[]{:S(2)}) collective-permute-start(bf16[512,896]{1,0:T(8,128)(2,1)} %attend.4.mine_hbm), channel_id=1, source_target_pairs={{12,8},{8,4},{4,0},{13,9},{9,5},{5,1},{14,10},{10,6},{6,2},{15,11}... | collective-permute-start | bytes 2752520 | tf_op jit(solution)/shard_map/ppermute | solution.py:653
  77.4 116.1 %collective-permute-start.4 = (bf16[2,2048,128]{2,1,0:T(8,128)(2,1)}, bf16[2,2048,128]{2,1,0:T(8,128)(2,1)}, u32[]{:S(2)}, u32[]{:S(2)}) collective-permute-start(bf16[2,2048,128]{2,1,0:T(8,128)(2,1)} %slice_multiply_fusion), channel_id=1, source_target_pairs={{0,1},{1,2},{2,3},{3,0},{4,5},{5,6},{6,7},{7,4},{8,9},{9,10},{10,1... | collective-permute-start | bytes 3145736 | tf_op jit(solution)/shard_map/ppermute | solution.py:692
  109.5 97.9 %collective-permute-start.2 = (bf16[512,896]{1,0:T(8,128)(2,1)}, bf16[512,896]{1,0:T(8,128)(2,1)}, u32[]{:S(2)}, u32[]{:S(2)}) collective-permute-start(bf16[512,896]{1,0:T(8,128)(2,1)} %collective-permute-done.right_hbm_0_), channel_id=1, source_target_pairs={{4,8},{8,12},{5,9},{9,13},{6,10},{10,14},{7,11},{11,15},{20,24},{2... | collective-permute-start | bytes 2752520 | tf_op jit(solution)/shard_map/ppermute | solution.py:652
  111.1 96.2 %collective-permute-start.3 = (bf16[512,896]{1,0:T(8,128)(2,1)}, bf16[512,896]{1,0:T(8,128)(2,1)}, u32[]{:S(2)}, u32[]{:S(2)}) collective-permute-start(bf16[512,896]{1,0:T(8,128)(2,1)} %collective-permute-done.1.left_hbm_0_), channel_id=1, source_target_pairs={{8,4},{4,0},{9,5},{5,1},{10,6},{6,2},{11,7},{7,3},{24,20},{20,16},... | collective-permute-start | bytes 2752520 | tf_op jit(solution)/shard_map/ppermute | solution.py:653
  112.4 95.0 %all-to-all-start.1 = ((f32[4,32,8,128]{3,2,1,0:T(8,128)}), f32[4,32,8,128]{3,2,1,0:T(8,128)S(1)}, u32[]{:S(2)}, u32[]{:S(2)}) async-start(f32[4,32,8,128]{3,2,1,0:T(8,128)} %pad_maximum_fusion.2), calls=%async_computation.1 | async-start | bytes 1048576 | tf_op jit(solution)/shard_map/all_to_all | solution.py:696
  211.0 32.9 %all-to-all-start.2 = ((bf16[2,2048,1,128]{3,0,2,1:T(2,128)(2,1)}), bf16[2,2048,1,128]{3,0,2,1:T(2,128)(2,1)}, u32[]{:S(2)}, u32[]{:S(2)}) async-start(bf16[2,2048,1,128]{3,0,2,1:T(2,128)(2,1)} %copy.75), calls=%async_computation.2 | async-start | bytes 2097152 | tf_op jit(solution)/shard_map/all_to_all | solution.py:703
  220.1 25.8 %collective-permute-start.5 = (bf16[512,896]{1,0:T(8,128)(2,1)}, bf16[512,896]{1,0:T(8,128)(2,1)S(1)}, u32[]{:S(2)}, u32[]{:S(2)}) collective-permute-start(bf16[512,896]{1,0:T(8,128)(2,1)} %collective-permute-done.2.right_hbm_1_), channel_id=1, source_target_pairs={{8,12},{9,13},{10,14},{11,15},{24,28},{25,29},{26,30},{27,31}} | collective-permute-start | bytes 2752520 | tf_op jit(solution)/shard_map/ppermute | solution.py:652
  220.9 32.3 %collective-permute-start.6 = (bf16[512,896]{1,0:T(8,128)(2,1)}, bf16[512,896]{1,0:T(8,128)(2,1)S(1)}, u32[]{:S(2)}, u32[]{:S(2)}) collective-permute-start(bf16[512,896]{1,0:T(8,128)(2,1)} %collective-permute-done.3.left_hbm_1_), channel_id=1, source_target_pairs={{4,0},{5,1},{6,2},{7,3},{20,16},{21,17},{22,18},{23,19}} | collective-permute-start | bytes 2752520 | tf_op jit(solution)/shard_map/ppermute | solution.py:653
  246.0 8.5 copy-start.4
  253.1 1.3 copy-start.5
Sparse Core Ops, SparseCore 0:
  10.8 205.5 all-gather.2
